TPU v7x, 32 devices: a whole 2x2x4 slice. The times are simulated.
32 devices in a mesh: ty: 16 (over z, y, core), tx: 2 (over x).
Axes of the slice: x: 2, y: 2, z: 4, core: 2. Of those that a mesh axis runs over, the one named last changes fastest.
Arguments:
- ctrl: float32 [16, 2, 512, 640], P('ty', 'tx'), may hold values from -6 to 6
- interp_wt: float32 [16, 2, 4, 128, 384], P('ty', 'tx'), may hold values from -0.3125 to 0.3125
- interp_cols: int32 [16, 2, 4, 384], P('ty', 'tx'), may hold values from 0 to 1023
- conv_wt: float32 [16, 2, 4, 128, 512], P('ty', 'tx'), may hold values from -0.25 to 0.25
- conv_cols: int32 [16, 2, 4, 512], P('ty', 'tx'), may hold values from 0 to 1023
- halo_index: int32 [16, 2, 8, 64], P('ty', 'tx'), may hold values from 0 to 511
- valid: int32 [16, 2], P('ty', 'tx'), may hold values from 256 to 512
Outputs:
- localized: float32 [16, 2, 512, 640], P('ty', 'tx')
Inputs may be any that keep to these rules, and one draw needn't show every extreme that they name: `interp_cols`: indices into a tile's extended subgrid of 1024 rows; repeats are allowed. `conv_cols`: indices into a tile's extended subgrid; repeats are allowed. `halo_index`: owned row indices; repeats are allowed.
All inputs are finite; a program needn't handle non-finite values.
Results may differ from a plain program's by a relative error of at most 0.0001.
Values sent between devices are 32-bit elements; how exact they have to be, the bound alone decides.
No kernel may reach another device: no remote copies, remote signals or barrier semaphores. Data moves between devices by JAX's collectives and lax.ppermute only.
A program may use at most 64 MiB of HBM per device.

v0:
```python
import functools

import jax
import jax.numpy as jnp
from jax import lax
from jax.experimental import pallas as pl
from jax.experimental.pallas import tpu as pltpu
from jax.sharding import PartitionSpec as P


F32, BF16 = jnp.float32, jnp.bfloat16
VMEM = pl.BlockSpec(memory_space=pltpu.VMEM)
HBM = pl.BlockSpec(memory_space=pltpu.HBM)
SMEM = pl.BlockSpec(memory_space=pltpu.SMEM)
PARAMS = pltpu.CompilerParams(vmem_limit_bytes=40 * 1024 * 1024)
TILE = 256


def split(x):
    high = x.astype(BF16)
    return high, (x - high.astype(F32)).astype(BF16)


def mul(left, right):
    return jnp.dot(left, right, preferred_element_type=F32)


def mul_nt(left, right):
    return lax.dot_general(left, right, (((1,), (1,)), ((), ())), preferred_element_type=F32)


def one_hot_t(row, count):
    ids = lax.broadcasted_iota(jnp.int32, (count, row.shape[1]), 0)
    return jnp.where(ids == row, 1.0, 0.0).astype(BF16)


PLACES = ((None, -1), (None, 1), (0, -1), (0, 0), (0, 1), (1, -1), (1, 0), (1, 1))


def slot_groups(columns):
    groups = {}
    for place_id, (partner, step) in enumerate(PLACES):
        groups.setdefault((partner, step % columns), []).append(place_id)
    order = sorted(groups, key=lambda key: (key[1] == 0, {1: 0, 0: 1, None: 2}[key[0]]))
    return [tuple(groups[key]) for key in order]


def exchange(pieces, groups, sign):
    rows_n, cols_n = lax.axis_size("ty"), lax.axis_size("tx")
    arrived = []
    for piece, group in zip(pieces, groups):
        partner, step = PLACES[group[0]]
        pairs = []
        for i in range(rows_n):
            target = i if partner is None else ((i + partner) ^ 1) - partner
            if 0 <= target < rows_n:
                pairs += [(i * cols_n + j, target * cols_n + (j + sign * step) % cols_n) for j in range(cols_n)]
        if partner is None and step % cols_n == 0:
            arrived.append(piece)
        else:
            arrived.append(lax.ppermute(piece, ("ty", "tx"), pairs))
    return arrived


def relabelled(cols, odd, own, halo):
    above = jnp.where(odd, 5, 2)
    below = jnp.where(odd, -3, 0)
    moved = jnp.where(cols < own + 3 * halo, above, jnp.where(cols < own + 5 * halo, -3, below))
    return jnp.where(cols < own, cols, cols + moved * halo)


def place(refs, groups, halo):
    spots = {}
    for ref, group in zip(refs, groups):
        for k, slot in enumerate(group):
            spots[slot] = (ref, k * halo)
    return spots


def emit(block, start, own_ref, spots, own, halo):
    if start < own:
        own_ref[start : start + block.shape[0], :] = block
        return
    for at in range(0, block.shape[0], halo):
        ref, row = spots[(start - own + at) // halo]
        ref[row : row + halo, :] = block[at : at + halo]


def collect(spots, high_ref, low_ref, base, halo):
    for slot, (ref, row) in spots.items():
        high, low = split(ref[row : row + halo, :])
        at = base + slot * halo
        high_ref[at : at + halo, :] = high
        low_ref[at : at + halo, :] = low


def fetch(source, target, sems):
    copies = [pltpu.make_async_copy(source.at[0, 0, b], target.at[b], sems.at[b]) for b in range(target.shape[0])]
    for copy in copies:
        copy.start()
    return copies


def block_hot(cols_ref, b, count, order):
    return one_hot_t(relabelled(cols_ref[0, 0, b : b + 1, :], *order), count)


def build_t(wt_ref, copies, cols_ref, high_ref, low_ref, order):
    count = high_ref.shape[0]
    size = wt_ref.shape[1]
    for b in range(wt_ref.shape[0]):
        hot = block_hot(cols_ref, b, count, order)
        copies[b].wait()
        both = mul_nt(hot, jnp.concatenate(split(wt_ref[b]), axis=0))
        high, low = split(both[:, :size] + both[:, size:])
        high_ref[:, b * size : (b + 1) * size] = high
        low_ref[:, b * size : (b + 1) * size] = low


def build(wt_ref, cols_ref, high_ref, low_ref, order):
    count = high_ref.shape[1]
    size = wt_ref.shape[1]
    for b in range(wt_ref.shape[0]):
        both = mul_nt(jnp.concatenate(split(wt_ref[b]), axis=0), block_hot(cols_ref, b, count, order))
        high, low = split(both[:size] + both[size:])
        high_ref[b * size : (b + 1) * size, :] = high
        low_ref[b * size : (b + 1) * size, :] = low


def apply_t(high, low, mt_high, mt_low, own_ref, spots, own, halo):
    for start in range(0, mt_high.shape[0], TILE):
        rows = slice(start, start + TILE)
        block = mul(mt_high[rows, :], high) + mul(mt_high[rows, :], low) + mul(mt_low[rows, :], high)
        emit(block, start, own_ref, spots, own, halo)


def masked_apply(valid, field, mt_high, mt_low, own_out, pieces, groups, own, halo):
    ids = lax.broadcasted_iota(jnp.int32, field.shape, 0)
    high, low = split(jnp.where(ids < valid[0, 0], field, 0.0))
    apply_t(high, low, mt_high, mt_low, own_out, place(pieces, groups, halo), own, halo)


def first_kernel(valid, odd, ctrl, wt, cols, *refs, off, width, groups, own, halo):
    n = len(groups)
    (own_out, *pieces), (mt_high, mt_low, field, blocks, sem, sems) = refs[: n + 1], refs[n + 1 :]
    copies = fetch(wt, blocks, sems)
    copy = pltpu.make_async_copy(ctrl.at[0, 0, :, pl.ds(off, width)], field, sem)
    copy.start()
    build_t(blocks, copies, cols, mt_high, mt_low, (odd[0, 0] == 1, own, halo))
    copy.wait()
    masked_apply(valid, field[...], mt_high, mt_low, own_out, pieces, groups, own, halo)


def again_kernel(valid, ctrl, mt_high, mt_low, own_out, *refs, off, width, groups, own, halo):
    *pieces, field, sem = refs
    copy = pltpu.make_async_copy(ctrl.at[0, 0, :, pl.ds(off, width)], field, sem)
    copy.start()
    copy.wait()
    masked_apply(valid, field[...], mt_high, mt_low, own_out, pieces, groups, own, halo)


def build_kernel(odd, iwt, icols, cwt, ccols, halo_row, i_high, i_low, c_high, c_low, ct_high, ct_low, h_out, ht_out,
                 i_blocks, c_blocks, i_sems, c_sems, *, halo):
    own = ht_out.shape[0]
    order = (odd[0, 0] == 1, own, halo)
    c_copies = fetch(cwt, c_blocks, c_sems)
    i_copies = fetch(iwt, i_blocks, i_sems)
    ids = lax.broadcasted_iota(jnp.int32, (own, halo_row.shape[1]), 0)
    hot = jnp.where(ids == halo_row[...], 1.0, 0.0)
    ht_out[...] = hot.astype(BF16)
    h_out[...] = hot.T.astype(BF16)
    build_t(c_blocks, c_copies, ccols, ct_high, ct_low, order)
    build(c_blocks, ccols, c_high, c_low, order)
    for copy in i_copies:
        copy.wait()
    build(i_blocks, icols, i_high, i_low, order)


def owners(own_in, spots, ht, high_ref, low_ref, halo):
    collect(spots, high_ref, low_ref, 0, halo)
    return own_in[...] + mul(ht[...], high_ref[...]) + mul(ht[...], low_ref[...])


def second_kernel(own_in, *refs, groups, own, halo):
    n = len(groups)
    arrived, (ht, mt_high, mt_low, own_out), pieces, (s_high, s_low) = (
        refs[:n], refs[n : n + 4], refs[n + 4 : 2 * n + 4], refs[2 * n + 4 :])
    high, low = split(owners(own_in, place(arrived, groups, halo), ht, s_high, s_low, halo))
    apply_t(high, low, mt_high, mt_low, own_out, place(pieces, groups, halo), own, halo)


def send_rows(field, h, spots, own, halo):
    high, low = split(field)
    for start in range(0, h.shape[0], TILE):
        rows = slice(start, start + TILE)
        block = mul(h[rows, :], high) + mul(h[rows, :], low)
        emit(block, own + start, None, spots, own, halo)


def third_kernel(own_in, *refs, groups, own, halo):
    n = len(groups)
    arrived, (ht, h, own_out), pieces, (s_high, s_low) = (
        refs[:n], refs[n : n + 3], refs[n + 3 : 2 * n + 3], refs[2 * n + 3 :])
    total = owners(own_in, place(arrived, groups, halo), ht, s_high, s_low, halo)
    own_out[...] = total
    send_rows(total, h, place(pieces, groups, halo), own, halo)


def forward(own_in, arrived, groups, m_high, m_low, s_high, s_low, out, own, halo):
    high, low = split(own_in[...])
    s_high[0:own, :] = high
    s_low[0:own, :] = low
    collect(place(arrived, groups, halo), s_high, s_low, own, halo)
    for start in range(0, m_high.shape[0], TILE):
        rows = slice(start, start + TILE)
        out(rows, mul(m_high[rows, :], s_high[...]) + mul(m_high[rows, :], s_low[...])
            + mul(m_low[rows, :], s_high[...]))


def fourth_kernel(own_in, *refs, groups, own, halo):
    n = len(groups)
    arrived, (m_high, m_low, h, own_out), pieces, (s_high, s_low) = (
        refs[:n], refs[n : n + 4], refs[n + 4 : 2 * n + 4], refs[2 * n + 4 :])

    def store(rows, block):
        own_out[rows, :] = block

    forward(own_in, arrived, groups, m_high, m_low, s_high, s_low, store, own, halo)
    send_rows(own_out[...], h, place(pieces, groups, halo), own, halo)


def last_kernel(valid, own_in, *refs, groups, own, halo, off, width, chained):
    n = len(groups)
    arrived, (m_high, m_low, *rest) = refs[:n], refs[n:]
    out, s_high, s_low, result, sems = rest[1:] if chained else rest
    copies = []

    def store(rows, block):
        ids = lax.broadcasted_iota(jnp.int32, block.shape, 0) + rows.start
        result[rows, :] = jnp.where(ids < valid[0, 0], block, 0.0)
        copy = pltpu.make_async_copy(
            result.at[rows, :], out.at[0, 0, rows, pl.ds(off, width)], sems.at[rows.start // TILE])
        copy.start()
        copies.append(copy)

    forward(own_in, arrived, groups, m_high, m_low, s_high, s_low, store, own, halo)
    for copy in copies:
        copy.wait()


def body(ctrl, interp_wt, interp_cols, conv_wt, conv_cols, halo_index, valid):
    halo = halo_index.shape[3]
    grid_rows, width_all = ctrl.shape[2:]
    blocks, block_rows = conv_wt.shape[2:4]
    own = blocks * block_rows
    slots = 8 * halo
    ext = own + slots
    odd = lax.axis_index("ty") % 2
    index = halo_index[0, 0]
    up, down = index[0:3], index[5:8]
    halo_row = jnp.concatenate(
        [index[3:5], jnp.where(odd == 1, up, down), jnp.where(odd == 1, down, up)]).reshape(1, -1)
    odd = odd.astype(jnp.int32).reshape(1, 1)
    groups = slot_groups(lax.axis_size("tx"))
    known = dict(groups=groups, own=own, halo=halo)

    def shape(rows, cols, kind=F32):
        return jax.ShapeDtypeStruct((rows, cols), kind)

    def call(kernel, outs, args, specs, scratch=(), aliases=None, out_spec=VMEM, **more):
        return pl.pallas_call(
            functools.partial(kernel, **more),
            out_shape=outs,
            in_specs=list(specs) + [VMEM] * (len(args) - len(specs)),
            out_specs=jax.tree.map(lambda _: out_spec, outs),
            scratch_shapes=list(scratch),
            input_output_aliases=aliases or {},
            compiler_params=PARAMS,
            cost_estimate=pl.CostEstimate(flops=1 << 30, transcendentals=0, bytes_accessed=4 << 20),
        )(*args)

    lanes = 128
    second = (width_all // (2 * lanes)) * lanes
    chunks = [(0, width_all - second), (width_all - second, second)] if second else [(0, width_all)]
    dma = pltpu.SemaphoreType.DMA

    def leaving(width):
        return [shape(own, width)] + [shape(len(group) * halo, width) for group in groups]

    def weight_scratch(weights):
        return pltpu.VMEM(weights.shape[2:], F32), dma((weights.shape[2],))

    i_blocks, i_sems = weight_scratch(interp_wt)
    c_blocks, c_sems = weight_scratch(conv_wt)
    state = []
    for number, (off, width) in enumerate(chunks):
        more = dict(off=off, width=width, **known)
        field = pltpu.VMEM((grid_rows, width), F32)
        if number == 0:
            *got, it_high, it_low = call(
                first_kernel, leaving(width) + [shape(ext, grid_rows, BF16)] * 2,
                (valid, odd, ctrl, interp_wt, interp_cols), [SMEM, SMEM, HBM, HBM],
                [field, i_blocks, dma(()), i_sems], **more)
        else:
            got = call(again_kernel, leaving(width), (valid, ctrl, it_high, it_low), [SMEM, HBM],
                       [field, dma(())], **more)
        state.append(got)
    operators = [shape(grid_rows, ext, BF16)] * 2 + [shape(own, ext, BF16)] * 2 + [shape(ext, own, BF16)] * 2
    i_high, i_low, c_high, c_low, ct_high, ct_low, h, ht = call(
        build_kernel, operators + [shape(slots, own, BF16), shape(own, slots, BF16)],
        (odd, interp_wt, interp_cols, conv_wt, conv_cols, halo_row), [SMEM, HBM, VMEM, HBM],
        [i_blocks, c_blocks, i_sems, c_sems], halo=halo)

    def scratch(rows, width):
        return [pltpu.VMEM((rows, width), BF16)] * 2

    def arrive(number, sign):
        mine, *out = state[number]
        return mine, *exchange(out, groups, sign)

    def advance(sign, kernel, operands, rows):
        for number, (_, width) in enumerate(chunks):
            state[number] = call(kernel, leaving(width),
                                 (*arrive(number, sign), *operands), (), scratch(rows, width), **known)

    advance(-1, second_kernel, (ht, ct_high, ct_low), slots)
    advance(-1, third_kernel, (ht, h), slots)
    advance(1, fourth_kernel, (c_high, c_low, h), ext)
    result = None
    for number, (off, width) in enumerate(chunks):
        args = (valid, *arrive(number, 1), i_high, i_low)
        specs = [SMEM] + [VMEM] * (len(args) - 1)
        if number:
            args, specs = (*args, result), specs + [HBM]
        result = call(last_kernel, jax.ShapeDtypeStruct(ctrl.shape, F32), args, specs,
                      scratch(ext, width) + [pltpu.VMEM((grid_rows, width), F32), dma((grid_rows // TILE,))],
                      {len(args) - 1: 0} if number else None, HBM,
                      off=off, width=width, chained=number > 0, **known)
    return result


def solution(mesh):
    placed = (
        P("ty", "tx", None, None),
        P("ty", "tx", None, None, None),
        P("ty", "tx", None, None),
        P("ty", "tx", None, None, None),
        P("ty", "tx", None, None),
        P("ty", "tx", None, None),
        P("ty", "tx"),
    )

    return jax.shard_map(body, mesh=mesh, in_specs=placed, out_specs=P("ty", "tx", None, None), check_vma=False)
```

profile of v0, /device:TPU:1, one launch (start us, length us, event | category | flops | bytes accessed | tf_op | source)
XLA Modules:
  0.0 123.5 jit_solution(5888499143968550112)
XLA Ops:
  0.7 1.3 %copy-done = f32[1,1,512,640]{3,2,1,0:T(8,128)S(1)} copy-done((f32[1,1,512,640]{3,2,1,0:T(8,128)S(1)}, f32[1,1,512,640]{3,2,1,0:T(8,128)}, u32[]{:S(2)}) %copy-start) | copy-done | bytes 1310744
  2.0 1.1 copy-done.3
  3.1 0.7 copy-done.6
  3.8 7.3 %shard_map.73 = (f32[512,384]{1,0:T(8,128)S(1)}, f32[128,384]{1,0:T(8,128)S(1)}, f32[128,384]{1,0:T(8,128)S(1)}, f32[128,384]{1,0:T(8,128)S(1)}, f32[64,384]{1,0...) custom-call(s32[1,1]{1,0:T(1,128)S(6)} %copy.10.valid, ...), custom_call_target="tpu_custom_call" | custom-call | flops 1073741824 | bytes 4194304 | tf_op jit(solution)/shard_map/pallas_call | solution.py:271
  11.1 1.0 copy-done.8
  12.1 1.0 copy-done.10
  13.1 4.5 %collective-permute-start.23 = (f32[64,384]{1,0:T(8,128)}, f32[64,384]{1,0:T(8,128)S(1)}, u32[]{:S(2)}, u32[]{:S(2)}) collective-permute-start(f32[64,384]{1,0:T(8,128)} %get-tuple-element.101), channel_id=1, source_target_pairs={{2,4},{3,5},{4,2},{5,3},{6,8},{7,9},{8,6},{9,7},{10,12},{11,13},{1... | collective-permute-start | bytes 294920 | tf_op jit(solution)/shard_map/ppermute | solution.py:61
  17.6 0.1 collective-permute-start.24
  17.7 4.4 %collective-permute-start.20 = (f32[128,384]{1,0:T(8,128)S(1)}, f32[128,384]{1,0:T(8,128)S(1)}, u32[]{:S(2)}, u32[]{:S(2)}) collective-permute-start(f32[128,384]{1,0:T(8,128)S(1)} %get-tuple-element.98), channel_id=1, source_target_pairs={{2,5},{3,4},{4,3},{5,2},{6,9},{7,8},{8,7},{9,6},{10,13},{11,12},{1... | collective-permute-start | bytes 589832 | tf_op jit(solution)/shard_map/ppermute | solution.py:61
  22.2 0.1 collective-permute-start.21
  22.3 0.3 collective-permute-start.22
  22.6 0.1 reshape.14.halo_row
  22.7 1.2 copy-done.9
  23.9 1.2 copy-done.11
  25.1 1.1 shard_map.74
  26.2 4.8 %collective-permute-start = (f32[128,256]{1,0:T(8,128)S(1)}, f32[128,256]{1,0:T(8,128)S(1)}, u32[]{:S(2)}, u32[]{:S(2)}) collective-permute-start(f32[128,256]{1,0:T(8,128)S(1)} %get-tuple-element.66), channel_id=1, source_target_pairs={{2,5},{3,4},{4,3},{5,2},{6,9},{7,8},{8,7},{9,6},{10,13},{11,12},{1... | collective-permute-start | bytes 393224 | tf_op jit(solution)/shard_map/ppermute | solution.py:61
  31.1 7.8 %shard_map.75 = (bf16[512,1024]{1,0:T(8,128)(2,1)S(1)}, bf16[512,1024]{1,0:T(8,128)(2,1)S(1)}, bf16[512,1024]{1,0:T(8,128)(2,1)S(1)}, bf16[512,1024]{1,0:T(8,128...) custom-call(s32[1,1]{1,0:T(1,128)} %bitcast.odd, ...), custom_call_target="tpu_custom_call" | custom-call | flops 1073741824 | bytes 4194304 | tf_op jit(solution)/shard_map/pallas_call | solution.py:271
  38.9 2.1 %collective-permute-start.3 = (f32[64,256]{1,0:T(8,128)S(1)}, f32[64,256]{1,0:T(8,128)S(1)}, u32[]{:S(2)}, u32[]{:S(2)}) collective-permute-start(f32[64,256]{1,0:T(8,128)S(1)} %get-tuple-element.69), channel_id=1, source_target_pairs={{2,4},{3,5},{4,2},{5,3},{6,8},{7,9},{8,6},{9,7},{10,12},{11,13},{1... | collective-permute-start | bytes 196616 | tf_op jit(solution)/shard_map/ppermute | solution.py:61
  41.0 0.1 collective-permute-start.4
  41.1 1.6 %collective-permute-start.1 = (f32[128,256]{1,0:T(8,128)S(1)}, f32[128,256]{1,0:T(8,128)S(1)}, u32[]{:S(2)}, u32[]{:S(2)}) collective-permute-start(f32[128,256]{1,0:T(8,128)S(1)} %get-tuple-element.67), channel_id=1, source_target_pairs={{0,3},{1,2},{2,1},{3,0},{4,7},{5,6},{6,5},{7,4},{8,11},{9,10},{10,... | collective-permute-start | bytes 393224 | tf_op jit(solution)/shard_map/ppermute | solution.py:61
  42.7 0.3 collective-permute-start.2
  43.0 2.5 %shard_map.79 = (f32[512,384]{1,0:T(8,128)S(1)}, f32[128,384]{1,0:T(8,128)S(1)}, f32[128,384]{1,0:T(8,128)S(1)}, f32[128,384]{1,0:T(8,128)S(1)}, f32[64,384]{1,0:T(8,128)S(1)}, /*index=5*/f32[64,384]{1,0:T(8,128)S(1)}) custom-call(f32[512,384]{1,0:T(8,128)S(1)} %get-tuple-element.97.own_in, f32[128,384]{1,0:T(8,128)S(1)} %collective-permute-done.20.refs_0_, ...), custom_call_target="tpu_custom_call" | custom-call | flops 1073741824 | bytes 4194304 | tf_op jit(solution)/shard_map/pallas_call | solution.py:271
  45.4 4.8 %collective-permute-start.25 = (f32[128,384]{1,0:T(8,128)S(1)}, f32[128,384]{1,0:T(8,128)S(1)}, u32[]{:S(2)}, u32[]{:S(2)}) collective-permute-start(f32[128,384]{1,0:T(8,128)S(1)} %get-tuple-element.104), channel_id=1, source_target_pairs={{2,5},{3,4},{4,3},{5,2},{6,9},{7,8},{8,7},{9,6},{10,13},{11,12},{1... | collective-permute-start | bytes 589832 | tf_op jit(solution)/shard_map/ppermute | solution.py:61
  50.3 0.1 collective-permute-start.26
  50.4 0.5 collective-permute-start.27
  50.8 5.6 %collective-permute-start.28 = (f32[64,384]{1,0:T(8,128)S(1)}, f32[64,384]{1,0:T(8,128)S(1)}, u32[]{:S(2)}, u32[]{:S(2)}) collective-permute-start(f32[64,384]{1,0:T(8,128)S(1)} %get-tuple-element.107), channel_id=1, source_target_pairs={{2,4},{3,5},{4,2},{5,3},{6,8},{7,9},{8,6},{9,7},{10,12},{11,13},{1... | collective-permute-start | bytes 294920 | tf_op jit(solution)/shard_map/ppermute | solution.py:61
  56.4 0.1 collective-permute-start.29
  56.5 1.8 %shard_map.76 = (f32[512,256]{1,0:T(8,128)S(1)}, f32[128,256]{1,0:T(8,128)S(1)}, f32[128,256]{1,0:T(8,128)S(1)}, f32[128,256]{1,0:T(8,128)S(1)}, f32[64,256]{1,0:T(8,128)S(1)}, /*index=5*/f32[64,256]{1,0:T(8,128)S(1)}) custom-call(f32[512,256]{1,0:T(8,128)S(1)} %get-tuple-element.65.own_in, f32[128,256]{1,0:T(8,128)S(1)} %collective-permute-done.refs_0_, ...), custom_call_target="tpu_custom_call" | custom-call | flops 1073741824 | bytes 4194304 | tf_op jit(solution)/shard_map/pallas_call | solution.py:271
  58.4 0.6 collective-permute-done.28.refs_3_
  59.0 4.4 %collective-permute-start.5 = (f32[128,256]{1,0:T(8,128)S(1)}, f32[128,256]{1,0:T(8,128)S(1)}, u32[]{:S(2)}, u32[]{:S(2)}) collective-permute-start(f32[128,256]{1,0:T(8,128)S(1)} %get-tuple-element.75), channel_id=1, source_target_pairs={{2,5},{3,4},{4,3},{5,2},{6,9},{7,8},{8,7},{9,6},{10,13},{11,12},{1... | collective-permute-start | bytes 393224 | tf_op jit(solution)/shard_map/ppermute | solution.py:61
  63.4 1.9 %collective-permute-start.8 = (f32[64,256]{1,0:T(8,128)S(1)}, f32[64,256]{1,0:T(8,128)S(1)}, u32[]{:S(2)}, u32[]{:S(2)}) collective-permute-start(f32[64,256]{1,0:T(8,128)S(1)} %get-tuple-element.78), channel_id=1, source_target_pairs={{2,4},{3,5},{4,2},{5,3},{6,8},{7,9},{8,6},{9,7},{10,12},{11,13},{1... | collective-permute-start | bytes 196616 | tf_op jit(solution)/shard_map/ppermute | solution.py:61
  65.4 0.1 collective-permute-start.9
  65.5 1.3 %collective-permute-start.6 = (f32[128,256]{1,0:T(8,128)S(1)}, f32[128,256]{1,0:T(8,128)S(1)}, u32[]{:S(2)}, u32[]{:S(2)}) collective-permute-start(f32[128,256]{1,0:T(8,128)S(1)} %get-tuple-element.76), channel_id=1, source_target_pairs={{0,3},{1,2},{2,1},{3,0},{4,7},{5,6},{6,5},{7,4},{8,11},{9,10},{10,... | collective-permute-start | bytes 393224 | tf_op jit(solution)/shard_map/ppermute | solution.py:61
  66.8 0.5 collective-permute-start.7
  67.3 1.4 %shard_map.80 = (f32[512,384]{1,0:T(8,128)S(1)}, f32[128,384]{1,0:T(8,128)S(1)}, f32[128,384]{1,0:T(8,128)S(1)}, f32[128,384]{1,0:T(8,128)S(1)}, f32[64,384]{1,0:T(8,128)S(1)}, /*index=5*/f32[64,384]{1,0:T(8,128)S(1)}) custom-call(f32[512,384]{1,0:T(8,128)S(1)} %get-tuple-element.103.own_in, f32[128,384]{1,0:T(8,128)S(1)} %collective-permute-done.25.refs_0_, ...), custom_call_target="tpu_custom_call" | custom-call | flops 1073741824 | bytes 4194304 | tf_op jit(solution)/shard_map/pallas_call | solution.py:271
  68.7 0.6 collective-permute-done.8.refs_3_
  69.3 4.0 %collective-permute-start.30 = (f32[128,384]{1,0:T(8,128)S(1)}, f32[128,384]{1,0:T(8,128)S(1)}, u32[]{:S(2)}, u32[]{:S(2)}) collective-permute-start(f32[128,384]{1,0:T(8,128)S(1)} %get-tuple-element.110), channel_id=1, source_target_pairs={{2,5},{3,4},{4,3},{5,2},{6,9},{7,8},{8,7},{9,6},{10,13},{11,12},{1... | collective-permute-start | bytes 589832 | tf_op jit(solution)/shard_map/ppermute | solution.py:61
  73.3 0.1 collective-permute-start.31
  73.4 0.6 collective-permute-start.32
  74.0 4.7 %collective-permute-start.33 = (f32[64,384]{1,0:T(8,128)S(1)}, f32[64,384]{1,0:T(8,128)S(1)}, u32[]{:S(2)}, u32[]{:S(2)}) collective-permute-start(f32[64,384]{1,0:T(8,128)S(1)} %get-tuple-element.113), channel_id=1, source_target_pairs={{2,4},{3,5},{4,2},{5,3},{6,8},{7,9},{8,6},{9,7},{10,12},{11,13},{1... | collective-permute-start | bytes 294920 | tf_op jit(solution)/shard_map/ppermute | solution.py:61
  78.8 0.1 collective-permute-start.34
  78.8 1.3 %shard_map.77 = (f32[512,256]{1,0:T(8,128)S(1)}, f32[128,256]{1,0:T(8,128)S(1)}, f32[128,256]{1,0:T(8,128)S(1)}, f32[128,256]{1,0:T(8,128)S(1)}, f32[64,256]{1,0:T(8,128)S(1)}, /*index=5*/f32[64,256]{1,0:T(8,128)S(1)}) custom-call(f32[512,256]{1,0:T(8,128)S(1)} %get-tuple-element.74.own_in, f32[128,256]{1,0:T(8,128)S(1)} %collective-permute-done.5.refs_0_, ...), custom_call_target="tpu_custom_call" | custom-call | flops 1073741824 | bytes 4194304 | tf_op jit(solution)/shard_map/pallas_call | solution.py:271
  80.1 1.2 collective-permute-done.33.refs_3_
  81.3 4.4 %collective-permute-start.13 = (f32[64,256]{1,0:T(8,128)S(1)}, f32[64,256]{1,0:T(8,128)S(1)}, u32[]{:S(2)}, u32[]{:S(2)}) collective-permute-start(f32[64,256]{1,0:T(8,128)S(1)} %get-tuple-element.85), channel_id=1, source_target_pairs={{2,4},{3,5},{4,2},{5,3},{6,8},{7,9},{8,6},{9,7},{10,12},{11,13},{1... | collective-permute-start | bytes 196616 | tf_op jit(solution)/shard_map/ppermute | solution.py:61
  85.7 0.1 collective-permute-start.14
  85.8 4.1 %collective-permute-start.10 = (f32[128,256]{1,0:T(8,128)S(1)}, f32[128,256]{1,0:T(8,128)S(1)}, u32[]{:S(2)}, u32[]{:S(2)}) collective-permute-start(f32[128,256]{1,0:T(8,128)S(1)} %get-tuple-element.82), channel_id=1, source_target_pairs={{2,5},{3,4},{4,3},{5,2},{6,9},{7,8},{8,7},{9,6},{10,13},{11,12},{1... | collective-permute-start | bytes 393224 | tf_op jit(solution)/shard_map/ppermute | solution.py:61
  90.0 0.1 collective-permute-start.11
  90.0 0.9 collective-permute-start.12
  90.9 2.5 %shard_map.81 = (f32[512,384]{1,0:T(8,128)S(1)}, f32[128,384]{1,0:T(8,128)S(1)}, f32[128,384]{1,0:T(8,128)S(1)}, f32[128,384]{1,0:T(8,128)S(1)}, f32[64,384]{1,0:T(8,128)S(1)}, /*index=5*/f32[64,384]{1,0:T(8,128)S(1)}) custom-call(f32[512,384]{1,0:T(8,128)S(1)} %get-tuple-element.109.own_in, f32[128,384]{1,0:T(8,128)S(1)} %collective-permute-done.30.refs_0_, ...), custom_call_target="tpu_custom_call" | custom-call | flops 1073741824 | bytes 4194304 | tf_op jit(solution)/shard_map/pallas_call | solution.py:271
  93.4 4.6 %collective-permute-start.35 = (f32[128,384]{1,0:T(8,128)S(1)}, f32[128,384]{1,0:T(8,128)S(1)}, u32[]{:S(2)}, u32[]{:S(2)}) collective-permute-start(f32[128,384]{1,0:T(8,128)S(1)} %get-tuple-element.116), channel_id=1, source_target_pairs={{2,5},{3,4},{4,3},{5,2},{6,9},{7,8},{8,7},{9,6},{10,13},{11,12},{1... | collective-permute-start | bytes 589832 | tf_op jit(solution)/shard_map/ppermute | solution.py:61
  98.0 0.1 collective-permute-start.36
  98.1 1.0 collective-permute-start.37
  99.1 3.9 %collective-permute-start.38 = (f32[64,384]{1,0:T(8,128)S(1)}, f32[64,384]{1,0:T(8,128)S(1)}, u32[]{:S(2)}, u32[]{:S(2)}) collective-permute-start(f32[64,384]{1,0:T(8,128)S(1)} %get-tuple-element.119), channel_id=1, source_target_pairs={{2,4},{3,5},{4,2},{5,3},{6,8},{7,9},{8,6},{9,7},{10,12},{11,13},{1... | collective-permute-start | bytes 294920 | tf_op jit(solution)/shard_map/ppermute | solution.py:61
  103.1 0.1 collective-permute-start.39
  103.2 1.4 %shard_map.78 = (f32[512,256]{1,0:T(8,128)S(1)}, f32[128,256]{1,0:T(8,128)S(1)}, f32[128,256]{1,0:T(8,128)S(1)}, f32[128,256]{1,0:T(8,128)S(1)}, f32[64,256]{1,0:T(8,128)S(1)}, /*index=5*/f32[64,256]{1,0:T(8,128)S(1)}) custom-call(f32[512,256]{1,0:T(8,128)S(1)} %get-tuple-element.81.own_in, f32[128,256]{1,0:T(8,128)S(1)} %collective-permute-done.10.refs_0_, ...), custom_call_target="tpu_custom_call" | custom-call | flops 1073741824 | bytes 4194304 | tf_op jit(solution)/shard_map/pallas_call | solution.py:271
  104.6 2.2 %collective-permute-done.38.refs_3_ = f32[64,384]{1,0:T(8,128)S(1)} collective-permute-done((f32[64,384]{1,0:T(8,128)S(1)}, f32[64,384]{1,0:T(8,128)S(1)}, u32[]{:S(2)}, u32[]{:S(2)}) %collective-permute-start.38) | collective-permute-done | bytes 98336 | tf_op jit(solution)/shard_map/ppermute | solution.py:61
  106.8 4.7 %collective-permute-start.15 = (f32[128,256]{1,0:T(8,128)S(1)}, f32[128,256]{1,0:T(8,128)S(1)}, u32[]{:S(2)}, u32[]{:S(2)}) collective-permute-start(f32[128,256]{1,0:T(8,128)S(1)} %get-tuple-element.90), channel_id=1, source_target_pairs={{2,5},{3,4},{4,3},{5,2},{6,9},{7,8},{8,7},{9,6},{10,13},{11,12},{1... | collective-permute-start | bytes 393224 | tf_op jit(solution)/shard_map/ppermute | solution.py:61
  111.5 0.1 collective-permute-start.16
  111.6 0.9 collective-permute-start.17
  112.5 3.9 %collective-permute-start.18 = (f32[64,256]{1,0:T(8,128)S(1)}, f32[64,256]{1,0:T(8,128)S(1)}, u32[]{:S(2)}, u32[]{:S(2)}) collective-permute-start(f32[64,256]{1,0:T(8,128)S(1)} %get-tuple-element.93), channel_id=1, source_target_pairs={{2,4},{3,5},{4,2},{5,3},{6,8},{7,9},{8,6},{9,7},{10,12},{11,13},{1... | collective-permute-start | bytes 196616 | tf_op jit(solution)/shard_map/ppermute | solution.py:61
  116.4 0.1 collective-permute-start.19
  116.5 2.7 %shard_map.82.refs_7_ = f32[1,1,512,640]{3,2,1,0:T(8,128)} custom-call(s32[1,1]{1,0:T(1,128)S(6)} %copy.10.valid, f32[512,384]{1,0:T(8,128)S(1)} %get-tuple-element.115.own_in, f32[128,384]{1,0:T(8,128)S(1)} %collective-permute-done.35.refs_0_, f32[128,384]{1,0:T(8,128)S(1)} %collective-permute-done.36.refs_1_, ...), custom_call_target="tpu_custom_call" | custom-call | flops 1073741824 | bytes 4194304 | tf_op jit(solution)/shard_map/pallas_call | solution.py:271
  119.2 2.3 %collective-permute-done.17.refs_2_ = f32[128,256]{1,0:T(8,128)S(1)} collective-permute-done((f32[128,256]{1,0:T(8,128)S(1)}, f32[128,256]{1,0:T(8,128)S(1)}, u32[]{:S(2)}, u32[]{:S(2)}) %collective-permute-start.17) | collective-permute-done | bytes 131104 | tf_op jit(solution)/shard_map/ppermute | solution.py:61
  121.5 1.8 %shard_map.83 = f32[1,1,512,640]{3,2,1,0:T(8,128)} custom-call(s32[1,1]{1,0:T(1,128)S(6)} %copy.10.valid, f32[512,256]{1,0:T(8,128)S(1)} %get-tuple-element.89.own_in, f32[128,256]{1,0:T(8,128)S(1)} %collective-permute-done.15.refs_0_, f32[128,256]{1,0:T(8,128)S(1)} %collective-permute-done.16.refs_1_, ...), custom_call_target="tpu_custom_call", output_to_operand_aliasing={{}: (9, {})} | custom-call | flops 1073741824 | bytes 4194304 | tf_op jit(solution)/shard_map/pallas_call | solution.py:271
  (57 shorter events, 0.1 us)
Async XLA Ops:
  0.7 1.3 %copy-start = (f32[1,1,512,640]{3,2,1,0:T(8,128)S(1)}, f32[1,1,512,640]{3,2,1,0:T(8,128)}, u32[]{:S(2)}) copy-start(f32[1,1,512,640]{3,2,1,0:T(8,128)} %ctrl.3) | copy-start | bytes 3932164
  2.0 1.1 copy-start.3
  3.1 0.7 copy-start.6
  3.8 18.8 %copy-start.12 = (s32[1,1,8,64]{3,2,1,0:T(8,128)S(1)}, s32[1,1,8,64]{3,2,1,0:T(8,128)}, u32[]{:S(2)}) copy-start(s32[1,1,8,64]{3,2,1,0:T(8,128)} %param.12) | copy-start | bytes 6148
  3.8 18.9 %copy-start.1 = (f32[1,1,512,640]{3,2,1,0:T(8,128)S(1)}, f32[1,1,512,640]{3,2,1,0:T(8,128)}, u32[]{:S(2)}) copy-start(f32[1,1,512,640]{3,2,1,0:T(8,128)} %ctrl.3) | copy-start | bytes 3932164
  11.1 1.0 copy-start.8
  12.1 1.0 copy-start.10
  13.1 13.1 %collective-permute-start.23 = (f32[64,384]{1,0:T(8,128)}, f32[64,384]{1,0:T(8,128)S(1)}, u32[]{:S(2)}, u32[]{:S(2)}) collective-permute-start(f32[64,384]{1,0:T(8,128)} %get-tuple-element.101), channel_id=1, source_target_pairs={{2,4},{3,5},{4,2},{5,3},{6,8},{7,9},{8,6},{9,7},{10,12},{11,13},{1... | collective-permute-start | bytes 294920 | tf_op jit(solution)/shard_map/ppermute | solution.py:61
  17.6 21.2 %collective-permute-start.24 = (f32[64,384]{1,0:T(8,128)}, f32[64,384]{1,0:T(8,128)S(1)}, u32[]{:S(2)}, u32[]{:S(2)}) collective-permute-start(f32[64,384]{1,0:T(8,128)} %get-tuple-element.102), channel_id=1, source_target_pairs={{0,2},{1,3},{2,0},{3,1},{4,6},{5,7},{6,4},{7,5},{8,10},{9,11},{10,... | collective-permute-start | bytes 294920 | tf_op jit(solution)/shard_map/ppermute | solution.py:61
  17.7 23.3 %collective-permute-start.20 = (f32[128,384]{1,0:T(8,128)S(1)}, f32[128,384]{1,0:T(8,128)S(1)}, u32[]{:S(2)}, u32[]{:S(2)}) collective-permute-start(f32[128,384]{1,0:T(8,128)S(1)} %get-tuple-element.98), channel_id=1, source_target_pairs={{2,5},{3,4},{4,3},{5,2},{6,9},{7,8},{8,7},{9,6},{10,13},{11,12},{1... | collective-permute-start | bytes 589832 | tf_op jit(solution)/shard_map/ppermute | solution.py:61
  22.2 18.9 %collective-permute-start.21 = (f32[128,384]{1,0:T(8,128)S(1)}, f32[128,384]{1,0:T(8,128)S(1)}, u32[]{:S(2)}, u32[]{:S(2)}) collective-permute-start(f32[128,384]{1,0:T(8,128)S(1)} %get-tuple-element.99), channel_id=1, source_target_pairs={{0,3},{1,2},{2,1},{3,0},{4,7},{5,6},{6,5},{7,4},{8,11},{9,10},{10,... | collective-permute-start | bytes 589832 | tf_op jit(solution)/shard_map/ppermute | solution.py:61
  22.3 20.4 %collective-permute-start.22 = (f32[128,384]{1,0:T(8,128)S(1)}, f32[128,384]{1,0:T(8,128)S(1)}, u32[]{:S(2)}, u32[]{:S(2)}) collective-permute-start(f32[128,384]{1,0:T(8,128)S(1)} %get-tuple-element.100), channel_id=1, source_target_pairs={{0,1},{1,0},{2,3},{3,2},{4,5},{5,4},{6,7},{7,6},{8,9},{9,8},{10,11... | collective-permute-start | bytes 589832 | tf_op jit(solution)/shard_map/ppermute | solution.py:61
  22.7 1.2 copy-start.9
  23.9 1.2 copy-start.11
  25.1 5.9 %copy-start.2 = (f32[1,1,4,128,512]{4,3,2,1,0:T(8,128)S(1)}, f32[1,1,4,128,512]{4,3,2,1,0:T(8,128)}, u32[]{:S(2)}) copy-start(f32[1,1,4,128,512]{4,3,2,1,0:T(8,128)} %cwt.1) | copy-start | bytes 3145732
  25.1 5.9 %copy-start.4 = (f32[1,1,4,128,384]{4,3,2,1,0:T(8,128)S(1)}, f32[1,1,4,128,384]{4,3,2,1,0:T(8,128)}, u32[]{:S(2)}) copy-start(f32[1,1,4,128,384]{4,3,2,1,0:T(8,128)} %iwt.1) | copy-start | bytes 2359300
  25.1 5.9 %copy-start.5 = (s32[1,1,4,512]{3,2,1,0:T(4,128)S(1)}, s32[1,1,4,512]{3,2,1,0:T(4,128)}, u32[]{:S(2)}) copy-start(s32[1,1,4,512]{3,2,1,0:T(4,128)} %ccols.1) | copy-start | bytes 24580
  25.1 6.0 %copy-start.7 = (s32[1,1,4,384]{3,2,1,0:T(4,128)S(1)}, s32[1,1,4,384]{3,2,1,0:T(4,128)}, u32[]{:S(2)}) copy-start(s32[1,1,4,384]{3,2,1,0:T(4,128)} %icols.1) | copy-start | bytes 18436
  26.2 24.1 %collective-permute-start = (f32[128,256]{1,0:T(8,128)S(1)}, f32[128,256]{1,0:T(8,128)S(1)}, u32[]{:S(2)}, u32[]{:S(2)}) collective-permute-start(f32[128,256]{1,0:T(8,128)S(1)} %get-tuple-element.66), channel_id=1, source_target_pairs={{2,5},{3,4},{4,3},{5,2},{6,9},{7,8},{8,7},{9,6},{10,13},{11,12},{1... | collective-permute-start | bytes 393224 | tf_op jit(solution)/shard_map/ppermute | solution.py:61
  38.9 6.6 %collective-permute-start.3 = (f32[64,256]{1,0:T(8,128)S(1)}, f32[64,256]{1,0:T(8,128)S(1)}, u32[]{:S(2)}, u32[]{:S(2)}) collective-permute-start(f32[64,256]{1,0:T(8,128)S(1)} %get-tuple-element.69), channel_id=1, source_target_pairs={{2,4},{3,5},{4,2},{5,3},{6,8},{7,9},{8,6},{9,7},{10,12},{11,13},{1... | collective-permute-start | bytes 196616 | tf_op jit(solution)/shard_map/ppermute | solution.py:61
  41.0 9.3 %collective-permute-start.4 = (f32[64,256]{1,0:T(8,128)S(1)}, f32[64,256]{1,0:T(8,128)S(1)}, u32[]{:S(2)}, u32[]{:S(2)}) collective-permute-start(f32[64,256]{1,0:T(8,128)S(1)} %get-tuple-element.70), channel_id=1, source_target_pairs={{0,2},{1,3},{2,0},{3,1},{4,6},{5,7},{6,4},{7,5},{8,10},{9,11},{10,... | collective-permute-start | bytes 196616 | tf_op jit(solution)/shard_map/ppermute | solution.py:61
  41.1 9.7 %collective-permute-start.1 = (f32[128,256]{1,0:T(8,128)S(1)}, f32[128,256]{1,0:T(8,128)S(1)}, u32[]{:S(2)}, u32[]{:S(2)}) collective-permute-start(f32[128,256]{1,0:T(8,128)S(1)} %get-tuple-element.67), channel_id=1, source_target_pairs={{0,3},{1,2},{2,1},{3,0},{4,7},{5,6},{6,5},{7,4},{8,11},{9,10},{10,... | collective-permute-start | bytes 393224 | tf_op jit(solution)/shard_map/ppermute | solution.py:61
  42.7 13.8 %collective-permute-start.2 = (f32[128,256]{1,0:T(8,128)S(1)}, f32[128,256]{1,0:T(8,128)S(1)}, u32[]{:S(2)}, u32[]{:S(2)}) collective-permute-start(f32[128,256]{1,0:T(8,128)S(1)} %get-tuple-element.68), channel_id=1, source_target_pairs={{0,1},{1,0},{2,3},{3,2},{4,5},{5,4},{6,7},{7,6},{8,9},{9,8},{10,11... | collective-permute-start | bytes 393224 | tf_op jit(solution)/shard_map/ppermute | solution.py:61
  45.4 19.9 %collective-permute-start.25 = (f32[128,384]{1,0:T(8,128)S(1)}, f32[128,384]{1,0:T(8,128)S(1)}, u32[]{:S(2)}, u32[]{:S(2)}) collective-permute-start(f32[128,384]{1,0:T(8,128)S(1)} %get-tuple-element.104), channel_id=1, source_target_pairs={{2,5},{3,4},{4,3},{5,2},{6,9},{7,8},{8,7},{9,6},{10,13},{11,12},{1... | collective-permute-start | bytes 589832 | tf_op jit(solution)/shard_map/ppermute | solution.py:61
  50.3 15.2 %collective-permute-start.26 = (f32[128,384]{1,0:T(8,128)S(1)}, f32[128,384]{1,0:T(8,128)S(1)}, u32[]{:S(2)}, u32[]{:S(2)}) collective-permute-start(f32[128,384]{1,0:T(8,128)S(1)} %get-tuple-element.105), channel_id=1, source_target_pairs={{0,3},{1,2},{2,1},{3,0},{4,7},{5,6},{6,5},{7,4},{8,11},{9,10},{10,... | collective-permute-start | bytes 589832 | tf_op jit(solution)/shard_map/ppermute | solution.py:61
  50.4 16.4 %collective-permute-start.27 = (f32[128,384]{1,0:T(8,128)S(1)}, f32[128,384]{1,0:T(8,128)S(1)}, u32[]{:S(2)}, u32[]{:S(2)}) collective-permute-start(f32[128,384]{1,0:T(8,128)S(1)} %get-tuple-element.106), channel_id=1, source_target_pairs={{0,1},{1,0},{2,3},{3,2},{4,5},{5,4},{6,7},{7,6},{8,9},{9,8},{10,11... | collective-permute-start | bytes 589832 | tf_op jit(solution)/shard_map/ppermute | solution.py:61
  50.8 8.2 %collective-permute-start.28 = (f32[64,384]{1,0:T(8,128)S(1)}, f32[64,384]{1,0:T(8,128)S(1)}, u32[]{:S(2)}, u32[]{:S(2)}) collective-permute-start(f32[64,384]{1,0:T(8,128)S(1)} %get-tuple-element.107), channel_id=1, source_target_pairs={{2,4},{3,5},{4,2},{5,3},{6,8},{7,9},{8,6},{9,7},{10,12},{11,13},{1... | collective-permute-start | bytes 294920 | tf_op jit(solution)/shard_map/ppermute | solution.py:61
  56.4 7.0 %collective-permute-start.29 = (f32[64,384]{1,0:T(8,128)S(1)}, f32[64,384]{1,0:T(8,128)S(1)}, u32[]{:S(2)}, u32[]{:S(2)}) collective-permute-start(f32[64,384]{1,0:T(8,128)S(1)} %get-tuple-element.108), channel_id=1, source_target_pairs={{0,2},{1,3},{2,0},{3,1},{4,6},{5,7},{6,4},{7,5},{8,10},{9,11},{10,... | collective-permute-start | bytes 294920 | tf_op jit(solution)/shard_map/ppermute | solution.py:61
  59.0 14.4 %collective-permute-start.5 = (f32[128,256]{1,0:T(8,128)S(1)}, f32[128,256]{1,0:T(8,128)S(1)}, u32[]{:S(2)}, u32[]{:S(2)}) collective-permute-start(f32[128,256]{1,0:T(8,128)S(1)} %get-tuple-element.75), channel_id=1, source_target_pairs={{2,5},{3,4},{4,3},{5,2},{6,9},{7,8},{8,7},{9,6},{10,13},{11,12},{1... | collective-permute-start | bytes 393224 | tf_op jit(solution)/shard_map/ppermute | solution.py:61
  63.4 5.9 %collective-permute-start.8 = (f32[64,256]{1,0:T(8,128)S(1)}, f32[64,256]{1,0:T(8,128)S(1)}, u32[]{:S(2)}, u32[]{:S(2)}) collective-permute-start(f32[64,256]{1,0:T(8,128)S(1)} %get-tuple-element.78), channel_id=1, source_target_pairs={{2,4},{3,5},{4,2},{5,3},{6,8},{7,9},{8,6},{9,7},{10,12},{11,13},{1... | collective-permute-start | bytes 196616 | tf_op jit(solution)/shard_map/ppermute | solution.py:61
  65.4 7.9 %collective-permute-start.9 = (f32[64,256]{1,0:T(8,128)S(1)}, f32[64,256]{1,0:T(8,128)S(1)}, u32[]{:S(2)}, u32[]{:S(2)}) collective-permute-start(f32[64,256]{1,0:T(8,128)S(1)} %get-tuple-element.79), channel_id=1, source_target_pairs={{0,2},{1,3},{2,0},{3,1},{4,6},{5,7},{6,4},{7,5},{8,10},{9,11},{10,... | collective-permute-start | bytes 196616 | tf_op jit(solution)/shard_map/ppermute | solution.py:61
  65.5 8.6 %collective-permute-start.6 = (f32[128,256]{1,0:T(8,128)S(1)}, f32[128,256]{1,0:T(8,128)S(1)}, u32[]{:S(2)}, u32[]{:S(2)}) collective-permute-start(f32[128,256]{1,0:T(8,128)S(1)} %get-tuple-element.76), channel_id=1, source_target_pairs={{0,3},{1,2},{2,1},{3,0},{4,7},{5,6},{6,5},{7,4},{8,11},{9,10},{10,... | collective-permute-start | bytes 393224 | tf_op jit(solution)/shard_map/ppermute | solution.py:61
  66.8 12.0 %collective-permute-start.7 = (f32[128,256]{1,0:T(8,128)S(1)}, f32[128,256]{1,0:T(8,128)S(1)}, u32[]{:S(2)}, u32[]{:S(2)}) collective-permute-start(f32[128,256]{1,0:T(8,128)S(1)} %get-tuple-element.77), channel_id=1, source_target_pairs={{0,1},{1,0},{2,3},{3,2},{4,5},{5,4},{6,7},{7,6},{8,9},{9,8},{10,11... | collective-permute-start | bytes 393224 | tf_op jit(solution)/shard_map/ppermute | solution.py:61
  69.3 16.5 %collective-permute-start.30 = (f32[128,384]{1,0:T(8,128)S(1)}, f32[128,384]{1,0:T(8,128)S(1)}, u32[]{:S(2)}, u32[]{:S(2)}) collective-permute-start(f32[128,384]{1,0:T(8,128)S(1)} %get-tuple-element.110), channel_id=1, source_target_pairs={{2,5},{3,4},{4,3},{5,2},{6,9},{7,8},{8,7},{9,6},{10,13},{11,12},{1... | collective-permute-start | bytes 589832 | tf_op jit(solution)/shard_map/ppermute | solution.py:61
  73.3 16.6 %collective-permute-start.31 = (f32[128,384]{1,0:T(8,128)S(1)}, f32[128,384]{1,0:T(8,128)S(1)}, u32[]{:S(2)}, u32[]{:S(2)}) collective-permute-start(f32[128,384]{1,0:T(8,128)S(1)} %get-tuple-element.111), channel_id=1, source_target_pairs={{0,3},{1,2},{2,1},{3,0},{4,7},{5,6},{6,5},{7,4},{8,11},{9,10},{10,... | collective-permute-start | bytes 589832 | tf_op jit(solution)/shard_map/ppermute | solution.py:61
  73.4 16.6 %collective-permute-start.32 = (f32[128,384]{1,0:T(8,128)S(1)}, f32[128,384]{1,0:T(8,128)S(1)}, u32[]{:S(2)}, u32[]{:S(2)}) collective-permute-start(f32[128,384]{1,0:T(8,128)S(1)} %get-tuple-element.112), channel_id=1, source_target_pairs={{0,1},{1,0},{2,3},{3,2},{4,5},{5,4},{6,7},{7,6},{8,9},{9,8},{10,11... | collective-permute-start | bytes 589832 | tf_op jit(solution)/shard_map/ppermute | solution.py:61
  74.0 7.3 %collective-permute-start.33 = (f32[64,384]{1,0:T(8,128)S(1)}, f32[64,384]{1,0:T(8,128)S(1)}, u32[]{:S(2)}, u32[]{:S(2)}) collective-permute-start(f32[64,384]{1,0:T(8,128)S(1)} %get-tuple-element.113), channel_id=1, source_target_pairs={{2,4},{3,5},{4,2},{5,3},{6,8},{7,9},{8,6},{9,7},{10,12},{11,13},{1... | collective-permute-start | bytes 294920 | tf_op jit(solution)/shard_map/ppermute | solution.py:61
  78.8 7.0 %collective-permute-start.34 = (f32[64,384]{1,0:T(8,128)S(1)}, f32[64,384]{1,0:T(8,128)S(1)}, u32[]{:S(2)}, u32[]{:S(2)}) collective-permute-start(f32[64,384]{1,0:T(8,128)S(1)} %get-tuple-element.114), channel_id=1, source_target_pairs={{0,2},{1,3},{2,0},{3,1},{4,6},{5,7},{6,4},{7,5},{8,10},{9,11},{10,... | collective-permute-start | bytes 294920 | tf_op jit(solution)/shard_map/ppermute | solution.py:61
  81.3 12.1 %collective-permute-start.13 = (f32[64,256]{1,0:T(8,128)S(1)}, f32[64,256]{1,0:T(8,128)S(1)}, u32[]{:S(2)}, u32[]{:S(2)}) collective-permute-start(f32[64,256]{1,0:T(8,128)S(1)} %get-tuple-element.85), channel_id=1, source_target_pairs={{2,4},{3,5},{4,2},{5,3},{6,8},{7,9},{8,6},{9,7},{10,12},{11,13},{1... | collective-permute-start | bytes 196616 | tf_op jit(solution)/shard_map/ppermute | solution.py:61
  85.7 12.3 %collective-permute-start.14 = (f32[64,256]{1,0:T(8,128)S(1)}, f32[64,256]{1,0:T(8,128)S(1)}, u32[]{:S(2)}, u32[]{:S(2)}) collective-permute-start(f32[64,256]{1,0:T(8,128)S(1)} %get-tuple-element.86), channel_id=1, source_target_pairs={{0,2},{1,3},{2,0},{3,1},{4,6},{5,7},{6,4},{7,5},{8,10},{9,11},{10,... | collective-permute-start | bytes 196616 | tf_op jit(solution)/shard_map/ppermute | solution.py:61
  85.8 12.3 %collective-permute-start.10 = (f32[128,256]{1,0:T(8,128)S(1)}, f32[128,256]{1,0:T(8,128)S(1)}, u32[]{:S(2)}, u32[]{:S(2)}) collective-permute-start(f32[128,256]{1,0:T(8,128)S(1)} %get-tuple-element.82), channel_id=1, source_target_pairs={{2,5},{3,4},{4,3},{5,2},{6,9},{7,8},{8,7},{9,6},{10,13},{11,12},{1... | collective-permute-start | bytes 393224 | tf_op jit(solution)/shard_map/ppermute | solution.py:61
  90.0 9.2 %collective-permute-start.11 = (f32[128,256]{1,0:T(8,128)S(1)}, f32[128,256]{1,0:T(8,128)S(1)}, u32[]{:S(2)}, u32[]{:S(2)}) collective-permute-start(f32[128,256]{1,0:T(8,128)S(1)} %get-tuple-element.83), channel_id=1, source_target_pairs={{0,3},{1,2},{2,1},{3,0},{4,7},{5,6},{6,5},{7,4},{8,11},{9,10},{10,... | collective-permute-start | bytes 393224 | tf_op jit(solution)/shard_map/ppermute | solution.py:61
  90.0 13.0 %collective-permute-start.12 = (f32[128,256]{1,0:T(8,128)S(1)}, f32[128,256]{1,0:T(8,128)S(1)}, u32[]{:S(2)}, u32[]{:S(2)}) collective-permute-start(f32[128,256]{1,0:T(8,128)S(1)} %get-tuple-element.84), channel_id=1, source_target_pairs={{0,1},{1,0},{2,3},{3,2},{4,5},{5,4},{6,7},{7,6},{8,9},{9,8},{10,11... | collective-permute-start | bytes 393224 | tf_op jit(solution)/shard_map/ppermute | solution.py:61
  93.4 18.2 %collective-permute-start.35 = (f32[128,384]{1,0:T(8,128)S(1)}, f32[128,384]{1,0:T(8,128)S(1)}, u32[]{:S(2)}, u32[]{:S(2)}) collective-permute-start(f32[128,384]{1,0:T(8,128)S(1)} %get-tuple-element.116), channel_id=1, source_target_pairs={{2,5},{3,4},{4,3},{5,2},{6,9},{7,8},{8,7},{9,6},{10,13},{11,12},{1... | collective-permute-start | bytes 589832 | tf_op jit(solution)/shard_map/ppermute | solution.py:61
  98.0 14.5 %collective-permute-start.36 = (f32[128,384]{1,0:T(8,128)S(1)}, f32[128,384]{1,0:T(8,128)S(1)}, u32[]{:S(2)}, u32[]{:S(2)}) collective-permute-start(f32[128,384]{1,0:T(8,128)S(1)} %get-tuple-element.117), channel_id=1, source_target_pairs={{0,3},{1,2},{2,1},{3,0},{4,7},{5,6},{6,5},{7,4},{8,11},{9,10},{10,... | collective-permute-start | bytes 589832 | tf_op jit(solution)/shard_map/ppermute | solution.py:61
  98.1 18.3 %collective-permute-start.37 = (f32[128,384]{1,0:T(8,128)S(1)}, f32[128,384]{1,0:T(8,128)S(1)}, u32[]{:S(2)}, u32[]{:S(2)}) collective-permute-start(f32[128,384]{1,0:T(8,128)S(1)} %get-tuple-element.118), channel_id=1, source_target_pairs={{0,1},{1,0},{2,3},{3,2},{4,5},{5,4},{6,7},{7,6},{8,9},{9,8},{10,11... | collective-permute-start | bytes 589832 | tf_op jit(solution)/shard_map/ppermute | solution.py:61
  99.1 7.6 %collective-permute-start.38 = (f32[64,384]{1,0:T(8,128)S(1)}, f32[64,384]{1,0:T(8,128)S(1)}, u32[]{:S(2)}, u32[]{:S(2)}) collective-permute-start(f32[64,384]{1,0:T(8,128)S(1)} %get-tuple-element.119), channel_id=1, source_target_pairs={{2,4},{3,5},{4,2},{5,3},{6,8},{7,9},{8,6},{9,7},{10,12},{11,13},{1... | collective-permute-start | bytes 294920 | tf_op jit(solution)/shard_map/ppermute | solution.py:61
  103.1 8.4 %collective-permute-start.39 = (f32[64,384]{1,0:T(8,128)S(1)}, f32[64,384]{1,0:T(8,128)S(1)}, u32[]{:S(2)}, u32[]{:S(2)}) collective-permute-start(f32[64,384]{1,0:T(8,128)S(1)} %get-tuple-element.120), channel_id=1, source_target_pairs={{0,2},{1,3},{2,0},{3,1},{4,6},{5,7},{6,4},{7,5},{8,10},{9,11},{10,... | collective-permute-start | bytes 294920 | tf_op jit(solution)/shard_map/ppermute | solution.py:61
  106.8 12.4 %collective-permute-start.15 = (f32[128,256]{1,0:T(8,128)S(1)}, f32[128,256]{1,0:T(8,128)S(1)}, u32[]{:S(2)}, u32[]{:S(2)}) collective-permute-start(f32[128,256]{1,0:T(8,128)S(1)} %get-tuple-element.90), channel_id=1, source_target_pairs={{2,5},{3,4},{4,3},{5,2},{6,9},{7,8},{8,7},{9,6},{10,13},{11,12},{1... | collective-permute-start | bytes 393224 | tf_op jit(solution)/shard_map/ppermute | solution.py:61
  111.5 7.7 %collective-permute-start.16 = (f32[128,256]{1,0:T(8,128)S(1)}, f32[128,256]{1,0:T(8,128)S(1)}, u32[]{:S(2)}, u32[]{:S(2)}) collective-permute-start(f32[128,256]{1,0:T(8,128)S(1)} %get-tuple-element.91), channel_id=1, source_target_pairs={{0,3},{1,2},{2,1},{3,0},{4,7},{5,6},{6,5},{7,4},{8,11},{9,10},{10,... | collective-permute-start | bytes 393224 | tf_op jit(solution)/shard_map/ppermute | solution.py:61
  111.6 9.9 %collective-permute-start.17 = (f32[128,256]{1,0:T(8,128)S(1)}, f32[128,256]{1,0:T(8,128)S(1)}, u32[]{:S(2)}, u32[]{:S(2)}) collective-permute-start(f32[128,256]{1,0:T(8,128)S(1)} %get-tuple-element.92), channel_id=1, source_target_pairs={{0,1},{1,0},{2,3},{3,2},{4,5},{5,4},{6,7},{7,6},{8,9},{9,8},{10,11... | collective-permute-start | bytes 393224 | tf_op jit(solution)/shard_map/ppermute | solution.py:61
  112.5 6.6 %collective-permute-start.18 = (f32[64,256]{1,0:T(8,128)S(1)}, f32[64,256]{1,0:T(8,128)S(1)}, u32[]{:S(2)}, u32[]{:S(2)}) collective-permute-start(f32[64,256]{1,0:T(8,128)S(1)} %get-tuple-element.93), channel_id=1, source_target_pairs={{2,4},{3,5},{4,2},{5,3},{6,8},{7,9},{8,6},{9,7},{10,12},{11,13},{1... | collective-permute-start | bytes 196616 | tf_op jit(solution)/shard_map/ppermute | solution.py:61
  116.4 2.8 %collective-permute-start.19 = (f32[64,256]{1,0:T(8,128)S(1)}, f32[64,256]{1,0:T(8,128)S(1)}, u32[]{:S(2)}, u32[]{:S(2)}) collective-permute-start(f32[64,256]{1,0:T(8,128)S(1)} %get-tuple-element.94), channel_id=1, source_target_pairs={{0,2},{1,3},{2,0},{3,1},{4,6},{5,7},{6,4},{7,5},{8,10},{9,11},{10,... | collective-permute-start | bytes 196616 | tf_op jit(solution)/shard_map/ppermute | solution.py:61
where the time goes:
time: 124 us
  starting transfers between devices  75.8 us (61%)
  Pallas kernels  31.5 us (25%)
  local copies, waits for them, and re-layouts  7.69 us (6%)
  waiting for transfers between devices  7.08 us (6%)
  between operations  1.46 us (1%)
    ppermute x40, starting transfers between devices, exchange(): arrived.append(lax.ppermute(piece, ('ty', 'tx'), pairs))  75.8 us
    pallas_call x11, Pallas kernels, call(): pl.pallas_call(functools.partial(kernel, **more), out_shape=outs, in_spec...  31.5 us
    unnamed x26, local copies, waits for them, and re-layouts  7.61 us
    ppermute x40, waiting for transfers between devices, exchange(): arrived.append(lax.ppermute(piece, ('ty', 'tx'), pairs))  7.08 us
  transfers between devices with their start and end apart: 40, of which 5 were waited for; matrix products, arithmetic and copies ran while one was open for 0% of the time, Pallas kernels for 18%

commit v1 on v0

--- a/solution.py
+++ b/solution.py
@@ -12,7 +12,7 @@
 VMEM = pl.BlockSpec(memory_space=pltpu.VMEM)
 HBM = pl.BlockSpec(memory_space=pltpu.HBM)
 SMEM = pl.BlockSpec(memory_space=pltpu.SMEM)
-PARAMS = pltpu.CompilerParams(vmem_limit_bytes=40 * 1024 * 1024)
+PARAMS = pltpu.CompilerParams(vmem_limit_bytes=24 * 1024 * 1024)
 TILE = 256
 
 
@@ -94,34 +94,24 @@
         low_ref[at : at + halo, :] = low
 
 
-def fetch(source, target, sems):
-    copies = [pltpu.make_async_copy(source.at[0, 0, b], target.at[b], sems.at[b]) for b in range(target.shape[0])]
-    for copy in copies:
-        copy.start()
-    return copies
-
-
-def block_hot(cols_ref, b, count, order):
-    return one_hot_t(relabelled(cols_ref[0, 0, b : b + 1, :], *order), count)
-
-
-def build_t(wt_ref, copies, cols_ref, high_ref, low_ref, order):
-    count = high_ref.shape[0]
-    size = wt_ref.shape[1]
-    for b in range(wt_ref.shape[0]):
-        hot = block_hot(cols_ref, b, count, order)
-        copies[b].wait()
-        both = mul_nt(hot, jnp.concatenate(split(wt_ref[b]), axis=0))
+def hot_blocks(cols, count, order):
+    cols = relabelled(cols, *order)
+    return [one_hot_t(cols[b : b + 1, :], count) for b in range(cols.shape[0])]
+
+
+def build_t(wt_ref, hots, high_ref, low_ref):
+    size = wt_ref.shape[-2]
+    for b, hot in enumerate(hots):
+        both = mul_nt(hot, jnp.concatenate(split(wt_ref[0, 0, b]), axis=0))
         high, low = split(both[:, :size] + both[:, size:])
         high_ref[:, b * size : (b + 1) * size] = high
         low_ref[:, b * size : (b + 1) * size] = low
 
 
-def build(wt_ref, cols_ref, high_ref, low_ref, order):
-    count = high_ref.shape[1]
-    size = wt_ref.shape[1]
-    for b in range(wt_ref.shape[0]):
-        both = mul_nt(jnp.concatenate(split(wt_ref[b]), axis=0), block_hot(cols_ref, b, count, order))
+def build(wt_ref, hots, high_ref, low_ref):
+    size = wt_ref.shape[-2]
+    for b, hot in enumerate(hots):
+        both = mul_nt(jnp.concatenate(split(wt_ref[0, 0, b]), axis=0), hot)
         high, low = split(both[:size] + both[size:])
         high_ref[b * size : (b + 1) * size, :] = high
         low_ref[b * size : (b + 1) * size, :] = low
@@ -142,12 +132,19 @@
 
 def first_kernel(valid, odd, ctrl, wt, cols, *refs, off, width, groups, own, halo):
     n = len(groups)
-    (own_out, *pieces), (mt_high, mt_low, field, blocks, sem, sems) = refs[: n + 1], refs[n + 1 :]
-    copies = fetch(wt, blocks, sems)
-    copy = pltpu.make_async_copy(ctrl.at[0, 0, :, pl.ds(off, width)], field, sem)
-    copy.start()
-    build_t(blocks, copies, cols, mt_high, mt_low, (odd[0, 0] == 1, own, halo))
-    copy.wait()
+    (own_out, *pieces), (mt_high, mt_low, field, blocks, cols_in, sems) = refs[: n + 1], refs[n + 1 :]
+    copies = [
+        pltpu.make_async_copy(cols, cols_in, sems.at[0]),
+        pltpu.make_async_copy(wt, blocks, sems.at[1]),
+        pltpu.make_async_copy(ctrl.at[0, 0, :, pl.ds(off, width)], field, sems.at[2]),
+    ]
+    for copy in copies:
+        copy.start()
+    copies[0].wait()
+    hots = hot_blocks(cols_in[0, 0], mt_high.shape[0], (odd[0, 0] == 1, own, halo))
+    copies[1].wait()
+    build_t(blocks, hots, mt_high, mt_low)
+    copies[2].wait()
     masked_apply(valid, field[...], mt_high, mt_low, own_out, pieces, groups, own, halo)
 
 
@@ -159,21 +156,19 @@
     masked_apply(valid, field[...], mt_high, mt_low, own_out, pieces, groups, own, halo)
 
 
-def build_kernel(odd, iwt, icols, cwt, ccols, halo_row, i_high, i_low, c_high, c_low, ct_high, ct_low, h_out, ht_out,
-                 i_blocks, c_blocks, i_sems, c_sems, *, halo):
+def early_kernel(odd, wt, cols, halo_row, ct_high, ct_low, ht_out, *, halo):
     own = ht_out.shape[0]
-    order = (odd[0, 0] == 1, own, halo)
-    c_copies = fetch(cwt, c_blocks, c_sems)
-    i_copies = fetch(iwt, i_blocks, i_sems)
-    ids = lax.broadcasted_iota(jnp.int32, (own, halo_row.shape[1]), 0)
-    hot = jnp.where(ids == halo_row[...], 1.0, 0.0)
-    ht_out[...] = hot.astype(BF16)
-    h_out[...] = hot.T.astype(BF16)
-    build_t(c_blocks, c_copies, ccols, ct_high, ct_low, order)
-    build(c_blocks, ccols, c_high, c_low, order)
-    for copy in i_copies:
-        copy.wait()
-    build(i_blocks, icols, i_high, i_low, order)
+    ht_out[...] = one_hot_t(halo_row[...], own)
+    build_t(wt, hot_blocks(cols[0, 0], ct_high.shape[0], (odd[0, 0] == 1, own, halo)), ct_high, ct_low)
+
+
+def conv_kernel(odd, wt, cols, ht, c_high, c_low, h_out, *, halo):
+    h_out[...] = ht[...].astype(F32).T.astype(BF16)
+    build(wt, hot_blocks(cols[0, 0], c_high.shape[1], (odd[0, 0] == 1, ht.shape[0], halo)), c_high, c_low)
+
+
+def interp_kernel(odd, wt, cols, high, low, *, own, halo):
+    build(wt, hot_blocks(cols[0, 0], high.shape[1], (odd[0, 0] == 1, own, halo)), high, low)
 
 
 def owners(own_in, spots, ht, high_ref, low_ref, halo):
@@ -255,6 +250,8 @@
     own = blocks * block_rows
     slots = 8 * halo
     ext = own + slots
+    far_ctrl, far_wt, far_cols = (
+        pltpu.with_memory_space_constraint(array, pltpu.HBM) for array in (ctrl, interp_wt, interp_cols))
     odd = lax.axis_index("ty") % 2
     index = halo_index[0, 0]
     up, down = index[0:3], index[5:8]
@@ -287,11 +284,6 @@
     def leaving(width):
         return [shape(own, width)] + [shape(len(group) * halo, width) for group in groups]
 
-    def weight_scratch(weights):
-        return pltpu.VMEM(weights.shape[2:], F32), dma((weights.shape[2],))
-
-    i_blocks, i_sems = weight_scratch(interp_wt)
-    c_blocks, c_sems = weight_scratch(conv_wt)
     state = []
     for number, (off, width) in enumerate(chunks):
         more = dict(off=off, width=width, **known)
@@ -299,17 +291,21 @@
         if number == 0:
             *got, it_high, it_low = call(
                 first_kernel, leaving(width) + [shape(ext, grid_rows, BF16)] * 2,
-                (valid, odd, ctrl, interp_wt, interp_cols), [SMEM, SMEM, HBM, HBM],
-                [field, i_blocks, dma(()), i_sems], **more)
+                (valid, odd, far_ctrl, far_wt, far_cols), [SMEM, SMEM, HBM, HBM, HBM],
+                [field, pltpu.VMEM(interp_wt.shape, F32), pltpu.VMEM(interp_cols.shape, jnp.int32), dma((3,))], **more)
         else:
-            got = call(again_kernel, leaving(width), (valid, ctrl, it_high, it_low), [SMEM, HBM],
+            got = call(again_kernel, leaving(width), (valid, far_ctrl, it_high, it_low), [SMEM, HBM],
                        [field, dma(())], **more)
         state.append(got)
-    operators = [shape(grid_rows, ext, BF16)] * 2 + [shape(own, ext, BF16)] * 2 + [shape(ext, own, BF16)] * 2
-    i_high, i_low, c_high, c_low, ct_high, ct_low, h, ht = call(
-        build_kernel, operators + [shape(slots, own, BF16), shape(own, slots, BF16)],
-        (odd, interp_wt, interp_cols, conv_wt, conv_cols, halo_row), [SMEM, HBM, VMEM, HBM],
-        [i_blocks, c_blocks, i_sems, c_sems], halo=halo)
+    ct_high, ct_low, ht = call(
+        early_kernel, [shape(ext, own, BF16)] * 2 + [shape(own, slots, BF16)],
+        (odd, conv_wt, conv_cols, halo_row), [SMEM], halo=halo)
+    c_high, c_low, h = call(
+        conv_kernel, [shape(own, ext, BF16)] * 2 + [shape(slots, own, BF16)],
+        (odd, conv_wt, conv_cols, ht), [SMEM], halo=halo)
+    i_high, i_low = call(
+        interp_kernel, [shape(grid_rows, ext, BF16)] * 2, (odd, interp_wt, interp_cols), [SMEM],
+        own=own, halo=halo)
 
     def scratch(rows, width):
         return [pltpu.VMEM((rows, width), BF16)] * 2

time: 124 us -> 113 us (0.911)
  the two profiles are of different devices: /device:TPU:1 before, /device:TPU:0 now
where the time goes in v1:
time: 113 us
  starting transfers between devices  81.5 us (72%)
  Pallas kernels  26.5 us (23%)
  local copies, waits for them, and re-layouts  2.29 us (2%)
  between operations  1.3 us (1%)
    ppermute x40, starting transfers between devices, exchange(): arrived.append(lax.ppermute(piece, ('ty', 'tx'), pairs))  81.5 us
    pallas_call x13, Pallas kernels, call(): pl.pallas_call(functools.partial(kernel, **more), out_shape=outs, in_spec...  26.5 us
  transfers between devices with their start and end apart: 40, of which 1 were waited for; matrix products, arithmetic and copies ran while one was open for 0% of the time, Pallas kernels for 18%

profile of v1, /device:TPU:0, one launch (start us, length us, event | category | flops | bytes accessed | tf_op | source)
XLA Modules:
  0.0 112.6 jit_solution(10558626127681015545)
XLA Ops:
  0.7 4.7 %shard_map.73 = (f32[512,384]{1,0:T(8,128)S(1)}, f32[128,384]{1,0:T(8,128)S(1)}, f32[128,384]{1,0:T(8,128)S(1)}, f32[128,384]{1,0:T(8,128)S(1)}, f32[64,384]{1,0...) custom-call(s32[1,1]{1,0:T(1,128)S(6)} %copy.10.valid, ...), custom_call_target="tpu_custom_call" | custom-call | flops 1073741824 | bytes 4194304 | tf_op jit(solution)/shard_map/pallas_call | solution.py:268
  5.4 0.0 copy-start.4
  5.4 1.0 copy-done.4
  6.4 0.7 collective-permute-start.20
  7.0 5.5 %collective-permute-start.21 = (f32[128,384]{1,0:T(8,128)S(1)}, f32[128,384]{1,0:T(8,128)S(1)}, u32[]{:S(2)}, u32[]{:S(2)}) collective-permute-start(f32[128,384]{1,0:T(8,128)S(1)} %get-tuple-element.99), channel_id=1, source_target_pairs={{0,3},{1,2},{2,1},{3,0},{4,7},{5,6},{6,5},{7,4},{8,11},{9,10},{10,... | collective-permute-start | bytes 589832 | tf_op jit(solution)/shard_map/ppermute | solution.py:61
  12.5 1.5 %collective-permute-start.22 = (f32[128,384]{1,0:T(8,128)S(1)}, f32[128,384]{1,0:T(8,128)S(1)}, u32[]{:S(2)}, u32[]{:S(2)}) collective-permute-start(f32[128,384]{1,0:T(8,128)S(1)} %get-tuple-element.100), channel_id=1, source_target_pairs={{0,1},{1,0},{2,3},{3,2},{4,5},{5,4},{6,7},{7,6},{8,9},{9,8},{10,11... | collective-permute-start | bytes 589832 | tf_op jit(solution)/shard_map/ppermute | solution.py:61
  14.0 0.7 collective-permute-start.23
  14.7 2.9 %collective-permute-start.24 = (f32[64,384]{1,0:T(8,128)S(1)}, f32[64,384]{1,0:T(8,128)S(1)}, u32[]{:S(2)}, u32[]{:S(2)}) collective-permute-start(f32[64,384]{1,0:T(8,128)S(1)} %get-tuple-element.102), channel_id=1, source_target_pairs={{0,2},{1,3},{2,0},{3,1},{4,6},{5,7},{6,4},{7,5},{8,10},{9,11},{10,... | collective-permute-start | bytes 294920 | tf_op jit(solution)/shard_map/ppermute | solution.py:61
  17.7 0.1 reshape.14.halo_row
  17.7 1.2 %copy-done.5 = bf16[1024,512]{1,0:T(8,128)(2,1)S(1)} copy-done((bf16[1024,512]{1,0:T(8,128)(2,1)S(1)}, bf16[1024,512]{1,0:T(8,128)(2,1)}, u32[]{:S(2)}) %copy-start.5) | copy-done | bytes 1048600
  19.0 2.2 %shard_map.74 = (f32[512,256]{1,0:T(8,128)S(1)}, f32[128,256]{1,0:T(8,128)S(1)}, f32[128,256]{1,0:T(8,128)S(1)}, f32[128,256]{1,0:T(8,128)S(1)}, f32[64,256]{1,0:T(8,128)S(1)}, /*index=5*/f32[64,256]{1,0:T(8,128)S(1)}) custom-call(s32[1,1]{1,0:T(1,128)S(6)} %copy.10.valid, f32[1,1,512,640]{3,2,1,0:T(8,128)} %ctrl.3, ...), custom_call_target="tpu_custom_call" | custom-call | flops 1073741824 | bytes 4194304 | tf_op jit(solution)/shard_map/pallas_call | solution.py:268
  21.1 0.0 collective-permute-done.23.refs_3_
  21.1 0.7 collective-permute-start
  21.8 4.0 %collective-permute-start.1 = (f32[128,256]{1,0:T(8,128)S(1)}, f32[128,256]{1,0:T(8,128)S(1)}, u32[]{:S(2)}, u32[]{:S(2)}) collective-permute-start(f32[128,256]{1,0:T(8,128)S(1)} %get-tuple-element.67), channel_id=1, source_target_pairs={{0,3},{1,2},{2,1},{3,0},{4,7},{5,6},{6,5},{7,4},{8,11},{9,10},{10,... | collective-permute-start | bytes 393224 | tf_op jit(solution)/shard_map/ppermute | solution.py:61
  25.8 0.9 collective-permute-start.2
  26.8 1.5 %shard_map.75 = (bf16[1024,512]{1,0:T(8,128)(2,1)S(1)}, bf16[1024,512]{1,0:T(8,128)(2,1)S(1)}, bf16[512,512]{1,0:T(8,128)(2,1)S(1)}) custom-call(s32[1,1]{1,0:T(1,128)} %bitcast.odd, f32[1,1,4,128,512]{4,3,2,1,0:T(8,128)S(1)} %copy-done, s32[1,1,4,512]{3,2,1,0:T(4,128)S(1)} %copy-done.2, s32[1,512]{1,0:T(1,128)S(1)} %reshape.14.halo_row), custom_call_target="tpu_custom_call" | custom-call | flops 1073741824 | bytes 4194304 | tf_op jit(solution)/shard_map/pallas_call | solution.py:268
  28.2 0.0 collective-permute-done.21.refs_1_
  28.3 0.7 collective-permute-start.3
  28.9 0.0 collective-permute-done.22.refs_2_
  28.9 2.6 %collective-permute-start.4 = (f32[64,256]{1,0:T(8,128)S(1)}, f32[64,256]{1,0:T(8,128)S(1)}, u32[]{:S(2)}, u32[]{:S(2)}) collective-permute-start(f32[64,256]{1,0:T(8,128)S(1)} %get-tuple-element.70), channel_id=1, source_target_pairs={{0,2},{1,3},{2,0},{3,1},{4,6},{5,7},{6,4},{7,5},{8,10},{9,11},{10,... | collective-permute-start | bytes 196616 | tf_op jit(solution)/shard_map/ppermute | solution.py:61
  31.5 2.5 %shard_map.81 = (f32[512,384]{1,0:T(8,128)S(1)}, f32[128,384]{1,0:T(8,128)S(1)}, f32[128,384]{1,0:T(8,128)S(1)}, f32[128,384]{1,0:T(8,128)S(1)}, f32[64,384]{1,0:T(8,128)S(1)}, /*index=5*/f32[64,384]{1,0:T(8,128)S(1)}) custom-call(f32[512,384]{1,0:T(8,128)S(1)} %get-tuple-element.97.own_in, f32[128,384]{1,0:T(8,128)S(1)} %collective-permute-done.20.refs_0_, ...), custom_call_target="tpu_custom_call" | custom-call | flops 1073741824 | bytes 4194304 | tf_op jit(solution)/shard_map/pallas_call | solution.py:268
  34.0 0.7 collective-permute-start.25
  34.7 4.4 %collective-permute-start.26 = (f32[128,384]{1,0:T(8,128)S(1)}, f32[128,384]{1,0:T(8,128)S(1)}, u32[]{:S(2)}, u32[]{:S(2)}) collective-permute-start(f32[128,384]{1,0:T(8,128)S(1)} %get-tuple-element.105), channel_id=1, source_target_pairs={{0,3},{1,2},{2,1},{3,0},{4,7},{5,6},{6,5},{7,4},{8,11},{9,10},{10,... | collective-permute-start | bytes 589832 | tf_op jit(solution)/shard_map/ppermute | solution.py:61
  39.1 1.3 %collective-permute-start.27 = (f32[128,384]{1,0:T(8,128)S(1)}, f32[128,384]{1,0:T(8,128)S(1)}, u32[]{:S(2)}, u32[]{:S(2)}) collective-permute-start(f32[128,384]{1,0:T(8,128)S(1)} %get-tuple-element.106), channel_id=1, source_target_pairs={{0,1},{1,0},{2,3},{3,2},{4,5},{5,4},{6,7},{7,6},{8,9},{9,8},{10,11... | collective-permute-start | bytes 589832 | tf_op jit(solution)/shard_map/ppermute | solution.py:61
  40.3 0.7 collective-permute-start.28
  41.0 1.8 %shard_map.76 = (f32[512,256]{1,0:T(8,128)S(1)}, f32[128,256]{1,0:T(8,128)S(1)}, f32[128,256]{1,0:T(8,128)S(1)}, f32[128,256]{1,0:T(8,128)S(1)}, f32[64,256]{1,0:T(8,128)S(1)}, /*index=5*/f32[64,256]{1,0:T(8,128)S(1)}) custom-call(f32[512,256]{1,0:T(8,128)S(1)} %get-tuple-element.65.own_in, f32[128,256]{1,0:T(8,128)S(1)} %collective-permute-done.refs_0_, ...), custom_call_target="tpu_custom_call" | custom-call | flops 1073741824 | bytes 4194304 | tf_op jit(solution)/shard_map/pallas_call | solution.py:268
  42.9 0.8 collective-permute-start.5
  43.7 4.7 %collective-permute-start.29 = (f32[64,384]{1,0:T(8,128)S(1)}, f32[64,384]{1,0:T(8,128)S(1)}, u32[]{:S(2)}, u32[]{:S(2)}) collective-permute-start(f32[64,384]{1,0:T(8,128)S(1)} %get-tuple-element.108), channel_id=1, source_target_pairs={{0,2},{1,3},{2,0},{3,1},{4,6},{5,7},{6,4},{7,5},{8,10},{9,11},{10,... | collective-permute-start | bytes 294920 | tf_op jit(solution)/shard_map/ppermute | solution.py:61
  48.5 1.5 %shard_map.77 = (bf16[512,1024]{1,0:T(8,128)(2,1)S(1)}, bf16[512,1024]{1,0:T(8,128)(2,1)S(1)}, bf16[512,512]{1,0:T(8,128)(2,1)S(1)}) custom-call(s32[1,1]{1,0:T(1,128)} %bitcast.odd, f32[1,1,4,128,512]{4,3,2,1,0:T(8,128)S(1)} %copy-done, s32[1,1,4,512]{3,2,1,0:T(4,128)S(1)} %copy-done.2, bf16[512,512]{1,0:T(8,128)(2,1)S(1)} %get-tuple-element.71.refs_5_.ht), custom_call_target="tpu_custom_call" | custom-call | flops 1073741824 | bytes 4194304 | tf_op jit(solution)/shard_map/pallas_call | solution.py:268
  49.9 0.0 collective-permute-done.29.refs_4_
  50.0 0.8 collective-permute-start.6
  50.7 0.9 collective-permute-start.7
  51.7 0.7 collective-permute-start.8
  52.3 0.0 collective-permute-done.27.refs_2_
  52.3 3.5 %collective-permute-start.9 = (f32[64,256]{1,0:T(8,128)S(1)}, f32[64,256]{1,0:T(8,128)S(1)}, u32[]{:S(2)}, u32[]{:S(2)}) collective-permute-start(f32[64,256]{1,0:T(8,128)S(1)} %get-tuple-element.79), channel_id=1, source_target_pairs={{0,2},{1,3},{2,0},{3,1},{4,6},{5,7},{6,4},{7,5},{8,10},{9,11},{10,... | collective-permute-start | bytes 196616 | tf_op jit(solution)/shard_map/ppermute | solution.py:61
  55.9 1.4 %shard_map.82 = (f32[512,384]{1,0:T(8,128)S(1)}, f32[128,384]{1,0:T(8,128)S(1)}, f32[128,384]{1,0:T(8,128)S(1)}, f32[128,384]{1,0:T(8,128)S(1)}, f32[64,384]{1,0:T(8,128)S(1)}, /*index=5*/f32[64,384]{1,0:T(8,128)S(1)}) custom-call(f32[512,384]{1,0:T(8,128)S(1)} %get-tuple-element.103.own_in, f32[128,384]{1,0:T(8,128)S(1)} %collective-permute-done.25.refs_0_, ...), custom_call_target="tpu_custom_call" | custom-call | flops 1073741824 | bytes 4194304 | tf_op jit(solution)/shard_map/pallas_call | solution.py:268
  57.3 0.0 collective-permute-done.8.refs_3_
  57.3 0.7 collective-permute-start.30
  58.0 4.5 %collective-permute-start.31 = (f32[128,384]{1,0:T(8,128)S(1)}, f32[128,384]{1,0:T(8,128)S(1)}, u32[]{:S(2)}, u32[]{:S(2)}) collective-permute-start(f32[128,384]{1,0:T(8,128)S(1)} %get-tuple-element.111), channel_id=1, source_target_pairs={{0,3},{1,2},{2,1},{3,0},{4,7},{5,6},{6,5},{7,4},{8,11},{9,10},{10,... | collective-permute-start | bytes 589832 | tf_op jit(solution)/shard_map/ppermute | solution.py:61
  62.5 2.1 %collective-permute-start.32 = (f32[128,384]{1,0:T(8,128)S(1)}, f32[128,384]{1,0:T(8,128)S(1)}, u32[]{:S(2)}, u32[]{:S(2)}) collective-permute-start(f32[128,384]{1,0:T(8,128)S(1)} %get-tuple-element.112), channel_id=1, source_target_pairs={{0,1},{1,0},{2,3},{3,2},{4,5},{5,4},{6,7},{7,6},{8,9},{9,8},{10,11... | collective-permute-start | bytes 589832 | tf_op jit(solution)/shard_map/ppermute | solution.py:61
  64.6 0.7 collective-permute-start.33
  65.3 3.5 %collective-permute-start.34 = (f32[64,384]{1,0:T(8,128)S(1)}, f32[64,384]{1,0:T(8,128)S(1)}, u32[]{:S(2)}, u32[]{:S(2)}) collective-permute-start(f32[64,384]{1,0:T(8,128)S(1)} %get-tuple-element.114), channel_id=1, source_target_pairs={{0,2},{1,3},{2,0},{3,1},{4,6},{5,7},{6,4},{7,5},{8,10},{9,11},{10,... | collective-permute-start | bytes 294920 | tf_op jit(solution)/shard_map/ppermute | solution.py:61
  68.8 1.3 %shard_map.78 = (f32[512,256]{1,0:T(8,128)S(1)}, f32[128,256]{1,0:T(8,128)S(1)}, f32[128,256]{1,0:T(8,128)S(1)}, f32[128,256]{1,0:T(8,128)S(1)}, f32[64,256]{1,0:T(8,128)S(1)}, /*index=5*/f32[64,256]{1,0:T(8,128)S(1)}) custom-call(f32[512,256]{1,0:T(8,128)S(1)} %get-tuple-element.74.own_in, f32[128,256]{1,0:T(8,128)S(1)} %collective-permute-done.5.refs_0_, ...), custom_call_target="tpu_custom_call" | custom-call | flops 1073741824 | bytes 4194304 | tf_op jit(solution)/shard_map/pallas_call | solution.py:268
  70.1 0.7 collective-permute-start.10
  70.8 6.1 %collective-permute-start.11 = (f32[128,256]{1,0:T(8,128)S(1)}, f32[128,256]{1,0:T(8,128)S(1)}, u32[]{:S(2)}, u32[]{:S(2)}) collective-permute-start(f32[128,256]{1,0:T(8,128)S(1)} %get-tuple-element.83), channel_id=1, source_target_pairs={{0,3},{1,2},{2,1},{3,0},{4,7},{5,6},{6,5},{7,4},{8,11},{9,10},{10,... | collective-permute-start | bytes 393224 | tf_op jit(solution)/shard_map/ppermute | solution.py:61
  76.9 1.2 %collective-permute-start.12 = (f32[128,256]{1,0:T(8,128)S(1)}, f32[128,256]{1,0:T(8,128)S(1)}, u32[]{:S(2)}, u32[]{:S(2)}) collective-permute-start(f32[128,256]{1,0:T(8,128)S(1)} %get-tuple-element.84), channel_id=1, source_target_pairs={{0,1},{1,0},{2,3},{3,2},{4,5},{5,4},{6,7},{7,6},{8,9},{9,8},{10,11... | collective-permute-start | bytes 393224 | tf_op jit(solution)/shard_map/ppermute | solution.py:61
  78.1 0.7 collective-permute-start.13
  78.8 2.5 %shard_map.83 = (f32[512,384]{1,0:T(8,128)S(1)}, f32[128,384]{1,0:T(8,128)S(1)}, f32[128,384]{1,0:T(8,128)S(1)}, f32[128,384]{1,0:T(8,128)S(1)}, f32[64,384]{1,0:T(8,128)S(1)}, /*index=5*/f32[64,384]{1,0:T(8,128)S(1)}) custom-call(f32[512,384]{1,0:T(8,128)S(1)} %get-tuple-element.109.own_in, f32[128,384]{1,0:T(8,128)S(1)} %collective-permute-done.30.refs_0_, ...), custom_call_target="tpu_custom_call" | custom-call | flops 1073741824 | bytes 4194304 | tf_op jit(solution)/shard_map/pallas_call | solution.py:268
  81.3 0.7 collective-permute-start.35
  81.9 3.9 %collective-permute-start.14 = (f32[64,256]{1,0:T(8,128)S(1)}, f32[64,256]{1,0:T(8,128)S(1)}, u32[]{:S(2)}, u32[]{:S(2)}) collective-permute-start(f32[64,256]{1,0:T(8,128)S(1)} %get-tuple-element.86), channel_id=1, source_target_pairs={{0,2},{1,3},{2,0},{3,1},{4,6},{5,7},{6,4},{7,5},{8,10},{9,11},{10,... | collective-permute-start | bytes 196616 | tf_op jit(solution)/shard_map/ppermute | solution.py:61
  85.9 0.9 collective-permute-done.14.refs_4_
  86.8 0.8 collective-permute-start.36
  87.6 1.2 %collective-permute-start.37 = (f32[128,384]{1,0:T(8,128)S(1)}, f32[128,384]{1,0:T(8,128)S(1)}, u32[]{:S(2)}, u32[]{:S(2)}) collective-permute-start(f32[128,384]{1,0:T(8,128)S(1)} %get-tuple-element.118), channel_id=1, source_target_pairs={{0,1},{1,0},{2,3},{3,2},{4,5},{5,4},{6,7},{7,6},{8,9},{9,8},{10,11... | collective-permute-start | bytes 589832 | tf_op jit(solution)/shard_map/ppermute | solution.py:61
  88.8 0.7 collective-permute-start.38
  89.4 3.3 %collective-permute-start.39 = (f32[64,384]{1,0:T(8,128)S(1)}, f32[64,384]{1,0:T(8,128)S(1)}, u32[]{:S(2)}, u32[]{:S(2)}) collective-permute-start(f32[64,384]{1,0:T(8,128)S(1)} %get-tuple-element.120), channel_id=1, source_target_pairs={{0,2},{1,3},{2,0},{3,1},{4,6},{5,7},{6,4},{7,5},{8,10},{9,11},{10,... | collective-permute-start | bytes 294920 | tf_op jit(solution)/shard_map/ppermute | solution.py:61
  92.7 1.4 %shard_map.79 = (f32[512,256]{1,0:T(8,128)S(1)}, f32[128,256]{1,0:T(8,128)S(1)}, f32[128,256]{1,0:T(8,128)S(1)}, f32[128,256]{1,0:T(8,128)S(1)}, f32[64,256]{1,0:T(8,128)S(1)}, /*index=5*/f32[64,256]{1,0:T(8,128)S(1)}) custom-call(f32[512,256]{1,0:T(8,128)S(1)} %get-tuple-element.81.own_in, f32[128,256]{1,0:T(8,128)S(1)} %collective-permute-done.10.refs_0_, ...), custom_call_target="tpu_custom_call" | custom-call | flops 1073741824 | bytes 4194304 | tf_op jit(solution)/shard_map/pallas_call | solution.py:268
  94.1 0.7 collective-permute-start.15
  94.8 5.2 %collective-permute-start.16 = (f32[128,256]{1,0:T(8,128)S(1)}, f32[128,256]{1,0:T(8,128)S(1)}, u32[]{:S(2)}, u32[]{:S(2)}) collective-permute-start(f32[128,256]{1,0:T(8,128)S(1)} %get-tuple-element.91), channel_id=1, source_target_pairs={{0,3},{1,2},{2,1},{3,0},{4,7},{5,6},{6,5},{7,4},{8,11},{9,10},{10,... | collective-permute-start | bytes 393224 | tf_op jit(solution)/shard_map/ppermute | solution.py:61
  100.0 1.0 collective-permute-start.17
  101.0 1.4 %shard_map.80 = (bf16[512,1024]{1,0:T(8,128)(2,1)S(1)}, bf16[512,1024]{1,0:T(8,128)(2,1)S(1)}) custom-call(s32[1,1]{1,0:T(1,128)} %bitcast.odd, f32[1,1,4,128,384]{4,3,2,1,0:T(8,128)S(1)} %copy-done.1, s32[1,1,4,384]{3,2,1,0:T(4,128)S(1)} %copy-done.3), custom_call_target="tpu_custom_call" | custom-call | flops 1073741824 | bytes 4194304 | tf_op jit(solution)/shard_map/pallas_call | solution.py:268
  102.4 0.7 collective-permute-start.18
  103.1 4.8 %collective-permute-start.19 = (f32[64,256]{1,0:T(8,128)S(1)}, f32[64,256]{1,0:T(8,128)S(1)}, u32[]{:S(2)}, u32[]{:S(2)}) collective-permute-start(f32[64,256]{1,0:T(8,128)S(1)} %get-tuple-element.94), channel_id=1, source_target_pairs={{0,2},{1,3},{2,0},{3,1},{4,6},{5,7},{6,4},{7,5},{8,10},{9,11},{10,... | collective-permute-start | bytes 196616 | tf_op jit(solution)/shard_map/ppermute | solution.py:61
  107.9 2.7 %shard_map.84.refs_7_ = f32[1,1,512,640]{3,2,1,0:T(8,128)} custom-call(s32[1,1]{1,0:T(1,128)S(6)} %copy.10.valid, f32[512,384]{1,0:T(8,128)S(1)} %get-tuple-element.115.own_in, f32[128,384]{1,0:T(8,128)S(1)} %collective-permute-done.35.refs_0_, f32[128,384]{1,0:T(8,128)S(1)} %collective-permute-done.36.refs_1_, ...), custom_call_target="tpu_custom_call" | custom-call | flops 1073741824 | bytes 4194304 | tf_op jit(solution)/shard_map/pallas_call | solution.py:268
  110.6 1.8 %shard_map.85 = f32[1,1,512,640]{3,2,1,0:T(8,128)} custom-call(s32[1,1]{1,0:T(1,128)S(6)} %copy.10.valid, f32[512,256]{1,0:T(8,128)S(1)} %get-tuple-element.89.own_in, f32[128,256]{1,0:T(8,128)S(1)} %collective-permute-done.15.refs_0_, f32[128,256]{1,0:T(8,128)S(1)} %collective-permute-done.16.refs_1_, ...), custom_call_target="tpu_custom_call", output_to_operand_aliasing={{}: (9, {})} | custom-call | flops 1073741824 | bytes 4194304 | tf_op jit(solution)/shard_map/pallas_call | solution.py:268
  (47 shorter events, 0.1 us)
Async XLA Ops:
  0.7 17.0 %copy-start.6 = (s32[1,1,8,64]{3,2,1,0:T(8,128)S(1)}, s32[1,1,8,64]{3,2,1,0:T(8,128)}, u32[]{:S(2)}) copy-start(s32[1,1,8,64]{3,2,1,0:T(8,128)} %param.12) | copy-start | bytes 6148
  5.4 1.0 copy-start.4
  6.4 19.5 %collective-permute-start.20 = (f32[128,384]{1,0:T(8,128)S(1)}, f32[128,384]{1,0:T(8,128)S(1)}, u32[]{:S(2)}, u32[]{:S(2)}) collective-permute-start(f32[128,384]{1,0:T(8,128)S(1)} %get-tuple-element.98), channel_id=1, source_target_pairs={{2,5},{3,4},{4,3},{5,2},{6,9},{7,8},{8,7},{9,6},{10,13},{11,12},{1... | collective-permute-start | bytes 589832 | tf_op jit(solution)/shard_map/ppermute | solution.py:61
  7.0 21.2 %collective-permute-start.21 = (f32[128,384]{1,0:T(8,128)S(1)}, f32[128,384]{1,0:T(8,128)S(1)}, u32[]{:S(2)}, u32[]{:S(2)}) collective-permute-start(f32[128,384]{1,0:T(8,128)S(1)} %get-tuple-element.99), channel_id=1, source_target_pairs={{0,3},{1,2},{2,1},{3,0},{4,7},{5,6},{6,5},{7,4},{8,11},{9,10},{10,... | collective-permute-start | bytes 589832 | tf_op jit(solution)/shard_map/ppermute | solution.py:61
  12.5 16.4 %collective-permute-start.22 = (f32[128,384]{1,0:T(8,128)S(1)}, f32[128,384]{1,0:T(8,128)S(1)}, u32[]{:S(2)}, u32[]{:S(2)}) collective-permute-start(f32[128,384]{1,0:T(8,128)S(1)} %get-tuple-element.100), channel_id=1, source_target_pairs={{0,1},{1,0},{2,3},{3,2},{4,5},{5,4},{6,7},{7,6},{8,9},{9,8},{10,11... | collective-permute-start | bytes 589832 | tf_op jit(solution)/shard_map/ppermute | solution.py:61
  14.0 7.1 %collective-permute-start.23 = (f32[64,384]{1,0:T(8,128)S(1)}, f32[64,384]{1,0:T(8,128)S(1)}, u32[]{:S(2)}, u32[]{:S(2)}) collective-permute-start(f32[64,384]{1,0:T(8,128)S(1)} %get-tuple-element.101), channel_id=1, source_target_pairs={{2,4},{3,5},{4,2},{5,3},{6,8},{7,9},{8,6},{9,7},{10,12},{11,13},{1... | collective-permute-start | bytes 294920 | tf_op jit(solution)/shard_map/ppermute | solution.py:61
  14.7 7.1 %collective-permute-start.24 = (f32[64,384]{1,0:T(8,128)S(1)}, f32[64,384]{1,0:T(8,128)S(1)}, u32[]{:S(2)}, u32[]{:S(2)}) collective-permute-start(f32[64,384]{1,0:T(8,128)S(1)} %get-tuple-element.102), channel_id=1, source_target_pairs={{0,2},{1,3},{2,0},{3,1},{4,6},{5,7},{6,4},{7,5},{8,10},{9,11},{10,... | collective-permute-start | bytes 294920 | tf_op jit(solution)/shard_map/ppermute | solution.py:61
  17.7 1.2 %copy-start.5 = (bf16[1024,512]{1,0:T(8,128)(2,1)S(1)}, bf16[1024,512]{1,0:T(8,128)(2,1)}, u32[]{:S(2)}) copy-start(bf16[1024,512]{1,0:T(8,128)(2,1)} %copy-done.4) | copy-start | bytes 3145732
  19.0 7.8 %copy-start = (f32[1,1,4,128,512]{4,3,2,1,0:T(8,128)S(1)}, f32[1,1,4,128,512]{4,3,2,1,0:T(8,128)}, u32[]{:S(2)}) copy-start(f32[1,1,4,128,512]{4,3,2,1,0:T(8,128)} %wt.6) | copy-start | bytes 3145732
  19.0 7.8 %copy-start.2 = (s32[1,1,4,512]{3,2,1,0:T(4,128)S(1)}, s32[1,1,4,512]{3,2,1,0:T(4,128)}, u32[]{:S(2)}) copy-start(s32[1,1,4,512]{3,2,1,0:T(4,128)} %cols.6) | copy-start | bytes 24580
  21.1 17.9 %collective-permute-start = (f32[128,256]{1,0:T(8,128)S(1)}, f32[128,256]{1,0:T(8,128)S(1)}, u32[]{:S(2)}, u32[]{:S(2)}) collective-permute-start(f32[128,256]{1,0:T(8,128)S(1)} %get-tuple-element.66), channel_id=1, source_target_pairs={{2,5},{3,4},{4,3},{5,2},{6,9},{7,8},{8,7},{9,6},{10,13},{11,12},{1... | collective-permute-start | bytes 393224 | tf_op jit(solution)/shard_map/ppermute | solution.py:61
  21.8 18.5 %collective-permute-start.1 = (f32[128,256]{1,0:T(8,128)S(1)}, f32[128,256]{1,0:T(8,128)S(1)}, u32[]{:S(2)}, u32[]{:S(2)}) collective-permute-start(f32[128,256]{1,0:T(8,128)S(1)} %get-tuple-element.67), channel_id=1, source_target_pairs={{0,3},{1,2},{2,1},{3,0},{4,7},{5,6},{6,5},{7,4},{8,11},{9,10},{10,... | collective-permute-start | bytes 393224 | tf_op jit(solution)/shard_map/ppermute | solution.py:61
  25.8 15.2 %collective-permute-start.2 = (f32[128,256]{1,0:T(8,128)S(1)}, f32[128,256]{1,0:T(8,128)S(1)}, u32[]{:S(2)}, u32[]{:S(2)}) collective-permute-start(f32[128,256]{1,0:T(8,128)S(1)} %get-tuple-element.68), channel_id=1, source_target_pairs={{0,1},{1,0},{2,3},{3,2},{4,5},{5,4},{6,7},{7,6},{8,9},{9,8},{10,11... | collective-permute-start | bytes 393224 | tf_op jit(solution)/shard_map/ppermute | solution.py:61
  28.3 5.7 %collective-permute-start.3 = (f32[64,256]{1,0:T(8,128)S(1)}, f32[64,256]{1,0:T(8,128)S(1)}, u32[]{:S(2)}, u32[]{:S(2)}) collective-permute-start(f32[64,256]{1,0:T(8,128)S(1)} %get-tuple-element.69), channel_id=1, source_target_pairs={{2,4},{3,5},{4,2},{5,3},{6,8},{7,9},{8,6},{9,7},{10,12},{11,13},{1... | collective-permute-start | bytes 196616 | tf_op jit(solution)/shard_map/ppermute | solution.py:61
  28.9 5.7 %collective-permute-start.4 = (f32[64,256]{1,0:T(8,128)S(1)}, f32[64,256]{1,0:T(8,128)S(1)}, u32[]{:S(2)}, u32[]{:S(2)}) collective-permute-start(f32[64,256]{1,0:T(8,128)S(1)} %get-tuple-element.70), channel_id=1, source_target_pairs={{0,2},{1,3},{2,0},{3,1},{4,6},{5,7},{6,4},{7,5},{8,10},{9,11},{10,... | collective-permute-start | bytes 196616 | tf_op jit(solution)/shard_map/ppermute | solution.py:61
  34.0 16.7 %collective-permute-start.25 = (f32[128,384]{1,0:T(8,128)S(1)}, f32[128,384]{1,0:T(8,128)S(1)}, u32[]{:S(2)}, u32[]{:S(2)}) collective-permute-start(f32[128,384]{1,0:T(8,128)S(1)} %get-tuple-element.104), channel_id=1, source_target_pairs={{2,5},{3,4},{4,3},{5,2},{6,9},{7,8},{8,7},{9,6},{10,13},{11,12},{1... | collective-permute-start | bytes 589832 | tf_op jit(solution)/shard_map/ppermute | solution.py:61
  34.7 17.0 %collective-permute-start.26 = (f32[128,384]{1,0:T(8,128)S(1)}, f32[128,384]{1,0:T(8,128)S(1)}, u32[]{:S(2)}, u32[]{:S(2)}) collective-permute-start(f32[128,384]{1,0:T(8,128)S(1)} %get-tuple-element.105), channel_id=1, source_target_pairs={{0,3},{1,2},{2,1},{3,0},{4,7},{5,6},{6,5},{7,4},{8,11},{9,10},{10,... | collective-permute-start | bytes 589832 | tf_op jit(solution)/shard_map/ppermute | solution.py:61
  39.1 13.3 %collective-permute-start.27 = (f32[128,384]{1,0:T(8,128)S(1)}, f32[128,384]{1,0:T(8,128)S(1)}, u32[]{:S(2)}, u32[]{:S(2)}) collective-permute-start(f32[128,384]{1,0:T(8,128)S(1)} %get-tuple-element.106), channel_id=1, source_target_pairs={{0,1},{1,0},{2,3},{3,2},{4,5},{5,4},{6,7},{7,6},{8,9},{9,8},{10,11... | collective-permute-start | bytes 589832 | tf_op jit(solution)/shard_map/ppermute | solution.py:61
  40.3 3.4 %collective-permute-start.28 = (f32[64,384]{1,0:T(8,128)S(1)}, f32[64,384]{1,0:T(8,128)S(1)}, u32[]{:S(2)}, u32[]{:S(2)}) collective-permute-start(f32[64,384]{1,0:T(8,128)S(1)} %get-tuple-element.107), channel_id=1, source_target_pairs={{2,4},{3,5},{4,2},{5,3},{6,8},{7,9},{8,6},{9,7},{10,12},{11,13},{1... | collective-permute-start | bytes 294920 | tf_op jit(solution)/shard_map/ppermute | solution.py:61
  42.9 19.7 %collective-permute-start.5 = (f32[128,256]{1,0:T(8,128)S(1)}, f32[128,256]{1,0:T(8,128)S(1)}, u32[]{:S(2)}, u32[]{:S(2)}) collective-permute-start(f32[128,256]{1,0:T(8,128)S(1)} %get-tuple-element.75), channel_id=1, source_target_pairs={{2,5},{3,4},{4,3},{5,2},{6,9},{7,8},{8,7},{9,6},{10,13},{11,12},{1... | collective-permute-start | bytes 393224 | tf_op jit(solution)/shard_map/ppermute | solution.py:61
  43.7 6.2 %collective-permute-start.29 = (f32[64,384]{1,0:T(8,128)S(1)}, f32[64,384]{1,0:T(8,128)S(1)}, u32[]{:S(2)}, u32[]{:S(2)}) collective-permute-start(f32[64,384]{1,0:T(8,128)S(1)} %get-tuple-element.108), channel_id=1, source_target_pairs={{0,2},{1,3},{2,0},{3,1},{4,6},{5,7},{6,4},{7,5},{8,10},{9,11},{10,... | collective-permute-start | bytes 294920 | tf_op jit(solution)/shard_map/ppermute | solution.py:61
  50.0 14.7 %collective-permute-start.6 = (f32[128,256]{1,0:T(8,128)S(1)}, f32[128,256]{1,0:T(8,128)S(1)}, u32[]{:S(2)}, u32[]{:S(2)}) collective-permute-start(f32[128,256]{1,0:T(8,128)S(1)} %get-tuple-element.76), channel_id=1, source_target_pairs={{0,3},{1,2},{2,1},{3,0},{4,7},{5,6},{6,5},{7,4},{8,11},{9,10},{10,... | collective-permute-start | bytes 393224 | tf_op jit(solution)/shard_map/ppermute | solution.py:61
  50.7 14.6 %collective-permute-start.7 = (f32[128,256]{1,0:T(8,128)S(1)}, f32[128,256]{1,0:T(8,128)S(1)}, u32[]{:S(2)}, u32[]{:S(2)}) collective-permute-start(f32[128,256]{1,0:T(8,128)S(1)} %get-tuple-element.77), channel_id=1, source_target_pairs={{0,1},{1,0},{2,3},{3,2},{4,5},{5,4},{6,7},{7,6},{8,9},{9,8},{10,11... | collective-permute-start | bytes 393224 | tf_op jit(solution)/shard_map/ppermute | solution.py:61
  51.7 5.6 %collective-permute-start.8 = (f32[64,256]{1,0:T(8,128)S(1)}, f32[64,256]{1,0:T(8,128)S(1)}, u32[]{:S(2)}, u32[]{:S(2)}) collective-permute-start(f32[64,256]{1,0:T(8,128)S(1)} %get-tuple-element.78), channel_id=1, source_target_pairs={{2,4},{3,5},{4,2},{5,3},{6,8},{7,9},{8,6},{9,7},{10,12},{11,13},{1... | collective-permute-start | bytes 196616 | tf_op jit(solution)/shard_map/ppermute | solution.py:61
  52.3 5.6 %collective-permute-start.9 = (f32[64,256]{1,0:T(8,128)S(1)}, f32[64,256]{1,0:T(8,128)S(1)}, u32[]{:S(2)}, u32[]{:S(2)}) collective-permute-start(f32[64,256]{1,0:T(8,128)S(1)} %get-tuple-element.79), channel_id=1, source_target_pairs={{0,2},{1,3},{2,0},{3,1},{4,6},{5,7},{6,4},{7,5},{8,10},{9,11},{10,... | collective-permute-start | bytes 196616 | tf_op jit(solution)/shard_map/ppermute | solution.py:61
  57.3 19.6 %collective-permute-start.30 = (f32[128,384]{1,0:T(8,128)S(1)}, f32[128,384]{1,0:T(8,128)S(1)}, u32[]{:S(2)}, u32[]{:S(2)}) collective-permute-start(f32[128,384]{1,0:T(8,128)S(1)} %get-tuple-element.110), channel_id=1, source_target_pairs={{2,5},{3,4},{4,3},{5,2},{6,9},{7,8},{8,7},{9,6},{10,13},{11,12},{1... | collective-permute-start | bytes 589832 | tf_op jit(solution)/shard_map/ppermute | solution.py:61
  58.0 20.1 %collective-permute-start.31 = (f32[128,384]{1,0:T(8,128)S(1)}, f32[128,384]{1,0:T(8,128)S(1)}, u32[]{:S(2)}, u32[]{:S(2)}) collective-permute-start(f32[128,384]{1,0:T(8,128)S(1)} %get-tuple-element.111), channel_id=1, source_target_pairs={{0,3},{1,2},{2,1},{3,0},{4,7},{5,6},{6,5},{7,4},{8,11},{9,10},{10,... | collective-permute-start | bytes 589832 | tf_op jit(solution)/shard_map/ppermute | solution.py:61
  62.5 16.2 %collective-permute-start.32 = (f32[128,384]{1,0:T(8,128)S(1)}, f32[128,384]{1,0:T(8,128)S(1)}, u32[]{:S(2)}, u32[]{:S(2)}) collective-permute-start(f32[128,384]{1,0:T(8,128)S(1)} %get-tuple-element.112), channel_id=1, source_target_pairs={{0,1},{1,0},{2,3},{3,2},{4,5},{5,4},{6,7},{7,6},{8,9},{9,8},{10,11... | collective-permute-start | bytes 589832 | tf_op jit(solution)/shard_map/ppermute | solution.py:61
  64.6 5.5 %collective-permute-start.33 = (f32[64,384]{1,0:T(8,128)S(1)}, f32[64,384]{1,0:T(8,128)S(1)}, u32[]{:S(2)}, u32[]{:S(2)}) collective-permute-start(f32[64,384]{1,0:T(8,128)S(1)} %get-tuple-element.113), channel_id=1, source_target_pairs={{2,4},{3,5},{4,2},{5,3},{6,8},{7,9},{8,6},{9,7},{10,12},{11,13},{1... | collective-permute-start | bytes 294920 | tf_op jit(solution)/shard_map/ppermute | solution.py:61
  65.3 5.5 %collective-permute-start.34 = (f32[64,384]{1,0:T(8,128)S(1)}, f32[64,384]{1,0:T(8,128)S(1)}, u32[]{:S(2)}, u32[]{:S(2)}) collective-permute-start(f32[64,384]{1,0:T(8,128)S(1)} %get-tuple-element.114), channel_id=1, source_target_pairs={{0,2},{1,3},{2,0},{3,1},{4,6},{5,7},{6,4},{7,5},{8,10},{9,11},{10,... | collective-permute-start | bytes 294920 | tf_op jit(solution)/shard_map/ppermute | solution.py:61
  70.1 17.4 %collective-permute-start.10 = (f32[128,256]{1,0:T(8,128)S(1)}, f32[128,256]{1,0:T(8,128)S(1)}, u32[]{:S(2)}, u32[]{:S(2)}) collective-permute-start(f32[128,256]{1,0:T(8,128)S(1)} %get-tuple-element.82), channel_id=1, source_target_pairs={{2,5},{3,4},{4,3},{5,2},{6,9},{7,8},{8,7},{9,6},{10,13},{11,12},{1... | collective-permute-start | bytes 393224 | tf_op jit(solution)/shard_map/ppermute | solution.py:61
  70.8 17.9 %collective-permute-start.11 = (f32[128,256]{1,0:T(8,128)S(1)}, f32[128,256]{1,0:T(8,128)S(1)}, u32[]{:S(2)}, u32[]{:S(2)}) collective-permute-start(f32[128,256]{1,0:T(8,128)S(1)} %get-tuple-element.83), channel_id=1, source_target_pairs={{0,3},{1,2},{2,1},{3,0},{4,7},{5,6},{6,5},{7,4},{8,11},{9,10},{10,... | collective-permute-start | bytes 393224 | tf_op jit(solution)/shard_map/ppermute | solution.py:61
  76.9 12.5 %collective-permute-start.12 = (f32[128,256]{1,0:T(8,128)S(1)}, f32[128,256]{1,0:T(8,128)S(1)}, u32[]{:S(2)}, u32[]{:S(2)}) collective-permute-start(f32[128,256]{1,0:T(8,128)S(1)} %get-tuple-element.84), channel_id=1, source_target_pairs={{0,1},{1,0},{2,3},{3,2},{4,5},{5,4},{6,7},{7,6},{8,9},{9,8},{10,11... | collective-permute-start | bytes 393224 | tf_op jit(solution)/shard_map/ppermute | solution.py:61
  78.1 3.8 %collective-permute-start.13 = (f32[64,256]{1,0:T(8,128)S(1)}, f32[64,256]{1,0:T(8,128)S(1)}, u32[]{:S(2)}, u32[]{:S(2)}) collective-permute-start(f32[64,256]{1,0:T(8,128)S(1)} %get-tuple-element.85), channel_id=1, source_target_pairs={{2,4},{3,5},{4,2},{5,3},{6,8},{7,9},{8,6},{9,7},{10,12},{11,13},{1... | collective-permute-start | bytes 196616 | tf_op jit(solution)/shard_map/ppermute | solution.py:61
  81.3 18.7 %collective-permute-start.35 = (f32[128,384]{1,0:T(8,128)S(1)}, f32[128,384]{1,0:T(8,128)S(1)}, u32[]{:S(2)}, u32[]{:S(2)}) collective-permute-start(f32[128,384]{1,0:T(8,128)S(1)} %get-tuple-element.116), channel_id=1, source_target_pairs={{2,5},{3,4},{4,3},{5,2},{6,9},{7,8},{8,7},{9,6},{10,13},{11,12},{1... | collective-permute-start | bytes 589832 | tf_op jit(solution)/shard_map/ppermute | solution.py:61
  81.9 4.8 %collective-permute-start.14 = (f32[64,256]{1,0:T(8,128)S(1)}, f32[64,256]{1,0:T(8,128)S(1)}, u32[]{:S(2)}, u32[]{:S(2)}) collective-permute-start(f32[64,256]{1,0:T(8,128)S(1)} %get-tuple-element.86), channel_id=1, source_target_pairs={{0,2},{1,3},{2,0},{3,1},{4,6},{5,7},{6,4},{7,5},{8,10},{9,11},{10,... | collective-permute-start | bytes 196616 | tf_op jit(solution)/shard_map/ppermute | solution.py:61
  86.8 15.6 %collective-permute-start.36 = (f32[128,384]{1,0:T(8,128)S(1)}, f32[128,384]{1,0:T(8,128)S(1)}, u32[]{:S(2)}, u32[]{:S(2)}) collective-permute-start(f32[128,384]{1,0:T(8,128)S(1)} %get-tuple-element.117), channel_id=1, source_target_pairs={{0,3},{1,2},{2,1},{3,0},{4,7},{5,6},{6,5},{7,4},{8,11},{9,10},{10,... | collective-permute-start | bytes 589832 | tf_op jit(solution)/shard_map/ppermute | solution.py:61
  87.6 15.5 %collective-permute-start.37 = (f32[128,384]{1,0:T(8,128)S(1)}, f32[128,384]{1,0:T(8,128)S(1)}, u32[]{:S(2)}, u32[]{:S(2)}) collective-permute-start(f32[128,384]{1,0:T(8,128)S(1)} %get-tuple-element.118), channel_id=1, source_target_pairs={{0,1},{1,0},{2,3},{3,2},{4,5},{5,4},{6,7},{7,6},{8,9},{9,8},{10,11... | collective-permute-start | bytes 589832 | tf_op jit(solution)/shard_map/ppermute | solution.py:61
  88.8 5.3 %collective-permute-start.38 = (f32[64,384]{1,0:T(8,128)S(1)}, f32[64,384]{1,0:T(8,128)S(1)}, u32[]{:S(2)}, u32[]{:S(2)}) collective-permute-start(f32[64,384]{1,0:T(8,128)S(1)} %get-tuple-element.119), channel_id=1, source_target_pairs={{2,4},{3,5},{4,2},{5,3},{6,8},{7,9},{8,6},{9,7},{10,12},{11,13},{1... | collective-permute-start | bytes 294920 | tf_op jit(solution)/shard_map/ppermute | solution.py:61
  89.4 5.3 %collective-permute-start.39 = (f32[64,384]{1,0:T(8,128)S(1)}, f32[64,384]{1,0:T(8,128)S(1)}, u32[]{:S(2)}, u32[]{:S(2)}) collective-permute-start(f32[64,384]{1,0:T(8,128)S(1)} %get-tuple-element.120), channel_id=1, source_target_pairs={{0,2},{1,3},{2,0},{3,1},{4,6},{5,7},{6,4},{7,5},{8,10},{9,11},{10,... | collective-permute-start | bytes 294920 | tf_op jit(solution)/shard_map/ppermute | solution.py:61
  92.7 8.3 %copy-start.1 = (f32[1,1,4,128,384]{4,3,2,1,0:T(8,128)S(1)}, f32[1,1,4,128,384]{4,3,2,1,0:T(8,128)}, u32[]{:S(2)}) copy-start(f32[1,1,4,128,384]{4,3,2,1,0:T(8,128)} %wt.7) | copy-start | bytes 2359300
  92.7 8.3 %copy-start.3 = (s32[1,1,4,384]{3,2,1,0:T(4,128)S(1)}, s32[1,1,4,384]{3,2,1,0:T(4,128)}, u32[]{:S(2)}) copy-start(s32[1,1,4,384]{3,2,1,0:T(4,128)} %cols.7) | copy-start | bytes 18436
  94.1 16.5 %collective-permute-start.15 = (f32[128,256]{1,0:T(8,128)S(1)}, f32[128,256]{1,0:T(8,128)S(1)}, u32[]{:S(2)}, u32[]{:S(2)}) collective-permute-start(f32[128,256]{1,0:T(8,128)S(1)} %get-tuple-element.90), channel_id=1, source_target_pairs={{2,5},{3,4},{4,3},{5,2},{6,9},{7,8},{8,7},{9,6},{10,13},{11,12},{1... | collective-permute-start | bytes 393224 | tf_op jit(solution)/shard_map/ppermute | solution.py:61
  94.8 15.8 %collective-permute-start.16 = (f32[128,256]{1,0:T(8,128)S(1)}, f32[128,256]{1,0:T(8,128)S(1)}, u32[]{:S(2)}, u32[]{:S(2)}) collective-permute-start(f32[128,256]{1,0:T(8,128)S(1)} %get-tuple-element.91), channel_id=1, source_target_pairs={{0,3},{1,2},{2,1},{3,0},{4,7},{5,6},{6,5},{7,4},{8,11},{9,10},{10,... | collective-permute-start | bytes 393224 | tf_op jit(solution)/shard_map/ppermute | solution.py:61
  100.0 10.7 %collective-permute-start.17 = (f32[128,256]{1,0:T(8,128)S(1)}, f32[128,256]{1,0:T(8,128)S(1)}, u32[]{:S(2)}, u32[]{:S(2)}) collective-permute-start(f32[128,256]{1,0:T(8,128)S(1)} %get-tuple-element.92), channel_id=1, source_target_pairs={{0,1},{1,0},{2,3},{3,2},{4,5},{5,4},{6,7},{7,6},{8,9},{9,8},{10,11... | collective-permute-start | bytes 393224 | tf_op jit(solution)/shard_map/ppermute | solution.py:61
  102.4 8.2 %collective-permute-start.18 = (f32[64,256]{1,0:T(8,128)S(1)}, f32[64,256]{1,0:T(8,128)S(1)}, u32[]{:S(2)}, u32[]{:S(2)}) collective-permute-start(f32[64,256]{1,0:T(8,128)S(1)} %get-tuple-element.93), channel_id=1, source_target_pairs={{2,4},{3,5},{4,2},{5,3},{6,8},{7,9},{8,6},{9,7},{10,12},{11,13},{1... | collective-permute-start | bytes 196616 | tf_op jit(solution)/shard_map/ppermute | solution.py:61
  103.1 7.5 %collective-permute-start.19 = (f32[64,256]{1,0:T(8,128)S(1)}, f32[64,256]{1,0:T(8,128)S(1)}, u32[]{:S(2)}, u32[]{:S(2)}) collective-permute-start(f32[64,256]{1,0:T(8,128)S(1)} %get-tuple-element.94), channel_id=1, source_target_pairs={{0,2},{1,3},{2,0},{3,1},{4,6},{5,7},{6,4},{7,5},{8,10},{9,11},{10,... | collective-permute-start | bytes 196616 | tf_op jit(solution)/shard_map/ppermute | solution.py:61

commit v2 on v1

--- a/solution.py
+++ b/solution.py
@@ -29,20 +29,24 @@
     return lax.dot_general(left, right, (((1,), (1,)), ((), ())), preferred_element_type=F32)
 
 
-def one_hot_t(row, count):
-    ids = lax.broadcasted_iota(jnp.int32, (count, row.shape[1]), 0)
+def one_hot_t(row, count, low=0, high=0, gap=0):
+    ids = lax.broadcasted_iota(jnp.int32, (count, row.shape[1]), 0) + low
+    if gap:
+        ids = jnp.where(ids < high, ids, ids + gap)
     return jnp.where(ids == row, 1.0, 0.0).astype(BF16)
 
 
-PLACES = ((None, -1), (None, 1), (0, -1), (0, 0), (0, 1), (1, -1), (1, 0), (1, 1))
+PLACES = ((None, -1), (None, 1), (0, -1), (0, 1), (1, -1), (1, 1), (0, 0), (1, 0))
+CROSSING = 6
+FACING = {0: (3, 4, 0, 2, 5, 7, 1, 6), 1: (3, 4, 5, 7, 0, 2, 6, 1)}
+TAKEN = {0: FACING[1], 1: FACING[0]}
 
 
 def slot_groups(columns):
     groups = {}
     for place_id, (partner, step) in enumerate(PLACES):
-        groups.setdefault((partner, step % columns), []).append(place_id)
-    order = sorted(groups, key=lambda key: (key[1] == 0, {1: 0, 0: 1, None: 2}[key[0]]))
-    return [tuple(groups[key]) for key in order]
+        groups.setdefault((place_id < CROSSING, partner, step % columns), []).append(place_id)
+    return [tuple(group) for group in groups.values()]
 
 
 def exchange(pieces, groups, sign):
@@ -63,10 +67,11 @@
 
 
 def relabelled(cols, odd, own, halo):
-    above = jnp.where(odd, 5, 2)
-    below = jnp.where(odd, -3, 0)
-    moved = jnp.where(cols < own + 3 * halo, above, jnp.where(cols < own + 5 * halo, -3, below))
-    return jnp.where(cols < own, cols, cols + moved * halo)
+    moved = jnp.zeros_like(cols)
+    for slot in reversed(range(8)):
+        shift = [(FACING[parity].index(slot) - slot) * halo for parity in (0, 1)]
+        moved = jnp.where(cols < own + (slot + 1) * halo, jnp.where(odd, shift[1], shift[0]), moved)
+    return jnp.where(cols < own, cols, cols + moved)
 
 
 def place(refs, groups, halo):
@@ -94,9 +99,9 @@
         low_ref[at : at + halo, :] = low
 
 
-def hot_blocks(cols, count, order):
+def hot_blocks(cols, count, order, **rows):
     cols = relabelled(cols, *order)
-    return [one_hot_t(cols[b : b + 1, :], count) for b in range(cols.shape[0])]
+    return [one_hot_t(cols[b : b + 1, :], count, **rows) for b in range(cols.shape[0])]
 
 
 def build_t(wt_ref, hots, high_ref, low_ref):
@@ -117,49 +122,52 @@
         low_ref[b * size : (b + 1) * size, :] = low
 
 
-def apply_t(high, low, mt_high, mt_low, own_ref, spots, own, halo):
-    for start in range(0, mt_high.shape[0], TILE):
-        rows = slice(start, start + TILE)
+def apply_t(high, low, mt_high, mt_low, own_ref, spots, own, halo, base=0, first=0, last=None):
+    last = mt_high.shape[0] if last is None else last
+    for start in range(first, last, TILE):
+        rows = slice(start, min(start + TILE, last))
         block = mul(mt_high[rows, :], high) + mul(mt_high[rows, :], low) + mul(mt_low[rows, :], high)
-        emit(block, start, own_ref, spots, own, halo)
-
-
-def masked_apply(valid, field, mt_high, mt_low, own_out, pieces, groups, own, halo):
-    ids = lax.broadcasted_iota(jnp.int32, field.shape, 0)
-    high, low = split(jnp.where(ids < valid[0, 0], field, 0.0))
-    apply_t(high, low, mt_high, mt_low, own_out, place(pieces, groups, halo), own, halo)
-
-
-def first_kernel(valid, odd, ctrl, wt, cols, *refs, off, width, groups, own, halo):
-    n = len(groups)
-    (own_out, *pieces), (mt_high, mt_low, field, blocks, cols_in, sems) = refs[: n + 1], refs[n + 1 :]
+        emit(block, start - first + base, own_ref, spots, own, halo)
+
+
+def first_kernel(valid, odd, ctrl, wt, cols, *refs, chunks, groups, own, halo, crossing):
+    n = len(groups)
+    each = n if crossing else n + 1
+    outs, (mt_high, mt_low, field, blocks, cols_in, sems) = refs[: each * len(chunks)], refs[each * len(chunks) :]
     copies = [
         pltpu.make_async_copy(cols, cols_in, sems.at[0]),
         pltpu.make_async_copy(wt, blocks, sems.at[1]),
-        pltpu.make_async_copy(ctrl.at[0, 0, :, pl.ds(off, width)], field, sems.at[2]),
+        pltpu.make_async_copy(ctrl, field, sems.at[2]),
     ]
     for copy in copies:
         copy.start()
     copies[0].wait()
-    hots = hot_blocks(cols_in[0, 0], mt_high.shape[0], (odd[0, 0] == 1, own, halo))
+    side = CROSSING * halo
+    rows = dict(low=own) if crossing else dict(high=own, gap=side)
+    hots = hot_blocks(cols_in[0, 0], mt_high.shape[0], (odd[0, 0] == 1, own, halo), **rows)
     copies[1].wait()
     build_t(blocks, hots, mt_high, mt_low)
     copies[2].wait()
-    masked_apply(valid, field[...], mt_high, mt_low, own_out, pieces, groups, own, halo)
-
-
-def again_kernel(valid, ctrl, mt_high, mt_low, own_out, *refs, off, width, groups, own, halo):
-    *pieces, field, sem = refs
-    copy = pltpu.make_async_copy(ctrl.at[0, 0, :, pl.ds(off, width)], field, sem)
-    copy.start()
-    copy.wait()
-    masked_apply(valid, field[...], mt_high, mt_low, own_out, pieces, groups, own, halo)
-
-
-def early_kernel(odd, wt, cols, halo_row, ct_high, ct_low, ht_out, *, halo):
+    for number, (off, width) in enumerate(chunks):
+        mine = outs[number * each : (number + 1) * each]
+        part = field[0, 0, :, off : off + width]
+        ids = lax.broadcasted_iota(jnp.int32, part.shape, 0)
+        high, low = split(jnp.where(ids < valid[0, 0], part, 0.0))
+        if crossing:
+            apply_t(high, low, mt_high, mt_low, None, place(mine, groups, halo), own, halo, base=own)
+        else:
+            spots = place(mine[1:], groups, halo)
+            apply_t(high, low, mt_high, mt_low, mine[0], spots, own, halo, last=own)
+            apply_t(high, low, mt_high, mt_low, mine[0], spots, own, halo, base=own + side, first=own)
+
+
+def early_kernel(odd, wt, cols, index, ct_high, ct_low, ht_out, *, halo):
     own = ht_out.shape[0]
-    ht_out[...] = one_hot_t(halo_row[...], own)
-    build_t(wt, hot_blocks(cols[0, 0], ct_high.shape[0], (odd[0, 0] == 1, own, halo)), ct_high, ct_low)
+    turned = odd[0, 0] == 1
+    for at, (even_slot, odd_slot) in enumerate(zip(TAKEN[0], TAKEN[1])):
+        row = jnp.where(turned, index[0, 0, odd_slot : odd_slot + 1, :], index[0, 0, even_slot : even_slot + 1, :])
+        ht_out[:, at * halo : (at + 1) * halo] = one_hot_t(row, own)
+    build_t(wt, hot_blocks(cols[0, 0], ct_high.shape[0], (turned, own, halo)), ct_high, ct_low)
 
 
 def conv_kernel(odd, wt, cols, ht, c_high, c_low, h_out, *, halo):
@@ -224,21 +232,50 @@
     send_rows(own_out[...], h, place(pieces, groups, halo), own, halo)
 
 
-def last_kernel(valid, own_in, *refs, groups, own, halo, off, width, chained):
-    n = len(groups)
-    arrived, (m_high, m_low, *rest) = refs[:n], refs[n:]
-    out, s_high, s_low, result, sems = rest[1:] if chained else rest
+def last_kernel(valid, own_in, *refs, groups, own, halo, off, width):
+    n = len(groups)
+    arrived, (m_high, m_low, out, s_high, s_low, result, sems) = refs[:n], refs[n:]
     copies = []
 
     def store(rows, block):
-        ids = lax.broadcasted_iota(jnp.int32, block.shape, 0) + rows.start
-        result[rows, :] = jnp.where(ids < valid[0, 0], block, 0.0)
-        copy = pltpu.make_async_copy(
-            result.at[rows, :], out.at[0, 0, rows, pl.ds(off, width)], sems.at[rows.start // TILE])
-        copy.start()
-        copies.append(copy)
+        copies.append(write_rows(valid, block, rows, result, out, off, width, sems))
 
     forward(own_in, arrived, groups, m_high, m_low, s_high, s_low, store, own, halo)
+    for copy in copies:
+        copy.wait()
+
+
+def write_rows(valid, block, rows, result, out, off, width, sems):
+    ids = lax.broadcasted_iota(jnp.int32, block.shape, 0) + rows.start
+    result[rows, :] = jnp.where(ids < valid[0, 0], block, 0.0)
+    copy = pltpu.make_async_copy(result.at[rows, :], out.at[0, 0, rows, pl.ds(off, width)], sems.at[rows.start // TILE])
+    copy.start()
+    return copy
+
+
+def part_kernel(own_in, *refs, groups, own, halo):
+    n = len(groups) - 1
+    arrived, (m_high, m_low, out, s_high, s_low) = refs[:n], refs[n:]
+    count = len(groups[0]) * halo
+    for ref in (s_high, s_low):
+        ref[own : own + count, :] = jnp.zeros((count, ref.shape[1]), BF16)
+
+    def store(rows, block):
+        out[rows, :] = block
+
+    forward(own_in, arrived, groups[1:], m_high, m_low, s_high, s_low, store, own, halo)
+
+
+def tail_kernel(valid, part, late, m_high, m_low, so_far, out, result, sems, *, own, off, width):
+    del so_far
+    high, low = split(late[...])
+    cols = slice(own, own + late.shape[0])
+    copies = []
+    for start in range(0, m_high.shape[0], TILE):
+        rows = slice(start, start + TILE)
+        block = (mul(m_high[rows, cols], high) + mul(m_high[rows, cols], low)
+                 + mul(m_low[rows, cols], high) + part[rows, :])
+        copies.append(write_rows(valid, block, rows, result, out, off, width, sems))
     for copy in copies:
         copy.wait()
 
@@ -253,10 +290,6 @@
     far_ctrl, far_wt, far_cols = (
         pltpu.with_memory_space_constraint(array, pltpu.HBM) for array in (ctrl, interp_wt, interp_cols))
     odd = lax.axis_index("ty") % 2
-    index = halo_index[0, 0]
-    up, down = index[0:3], index[5:8]
-    halo_row = jnp.concatenate(
-        [index[3:5], jnp.where(odd == 1, up, down), jnp.where(odd == 1, down, up)]).reshape(1, -1)
     odd = odd.astype(jnp.int32).reshape(1, 1)
     groups = slot_groups(lax.axis_size("tx"))
     known = dict(groups=groups, own=own, halo=halo)
@@ -284,22 +317,29 @@
     def leaving(width):
         return [shape(own, width)] + [shape(len(group) * halo, width) for group in groups]
 
-    state = []
-    for number, (off, width) in enumerate(chunks):
-        more = dict(off=off, width=width, **known)
-        field = pltpu.VMEM((grid_rows, width), F32)
-        if number == 0:
-            *got, it_high, it_low = call(
-                first_kernel, leaving(width) + [shape(ext, grid_rows, BF16)] * 2,
-                (valid, odd, far_ctrl, far_wt, far_cols), [SMEM, SMEM, HBM, HBM, HBM],
-                [field, pltpu.VMEM(interp_wt.shape, F32), pltpu.VMEM(interp_cols.shape, jnp.int32), dma((3,))], **more)
-        else:
-            got = call(again_kernel, leaving(width), (valid, far_ctrl, it_high, it_low), [SMEM, HBM],
-                       [field, dma(())], **more)
-        state.append(got)
+    crossing = [group for group in groups if group[0] < CROSSING]
+    straight = groups[len(crossing) :]
+
+    def first(kind, count):
+        shapes = []
+        for _, width in chunks:
+            shapes += [] if kind else [shape(own, width)]
+            shapes += [shape(len(group) * halo, width) for group in (crossing if kind else straight)]
+        outs = call(
+            first_kernel, shapes, (valid, odd, far_ctrl, far_wt, far_cols), [SMEM, SMEM, HBM, HBM, HBM],
+            [pltpu.VMEM((count, grid_rows), BF16)] * 2
+            + [pltpu.VMEM(ctrl.shape, F32), pltpu.VMEM(interp_wt.shape, F32), pltpu.VMEM(interp_cols.shape, jnp.int32),
+               dma((3,))],
+            chunks=chunks, groups=crossing if kind else straight, own=own, halo=halo, crossing=kind)
+        each = len(outs) // len(chunks)
+        return [list(outs[k * each : (k + 1) * each]) for k in range(len(chunks))]
+
+    over = first(True, CROSSING * halo)
+    rest = first(False, ext - CROSSING * halo)
+    state = [[mine[0]] + sent + mine[1:] for sent, mine in zip(over, rest)]
     ct_high, ct_low, ht = call(
         early_kernel, [shape(ext, own, BF16)] * 2 + [shape(own, slots, BF16)],
-        (odd, conv_wt, conv_cols, halo_row), [SMEM], halo=halo)
+        (odd, conv_wt, conv_cols, halo_index), [SMEM], halo=halo)
     c_high, c_low, h = call(
         conv_kernel, [shape(own, ext, BF16)] * 2 + [shape(slots, own, BF16)],
         (odd, conv_wt, conv_cols, ht), [SMEM], halo=halo)
@@ -322,16 +362,20 @@
     advance(-1, second_kernel, (ht, ct_high, ct_low), slots)
     advance(-1, third_kernel, (ht, h), slots)
     advance(1, fourth_kernel, (c_high, c_low, h), ext)
+    whole = jax.ShapeDtypeStruct(ctrl.shape, F32)
     result = None
     for number, (off, width) in enumerate(chunks):
-        args = (valid, *arrive(number, 1), i_high, i_low)
-        specs = [SMEM] + [VMEM] * (len(args) - 1)
-        if number:
-            args, specs = (*args, result), specs + [HBM]
-        result = call(last_kernel, jax.ShapeDtypeStruct(ctrl.shape, F32), args, specs,
-                      scratch(ext, width) + [pltpu.VMEM((grid_rows, width), F32), dma((grid_rows // TILE,))],
-                      {len(args) - 1: 0} if number else None, HBM,
-                      off=off, width=width, chained=number > 0, **known)
+        mine, *arrived = arrive(number, 1)
+        final = [pltpu.VMEM((grid_rows, width), F32), dma((grid_rows // TILE,))]
+        if number == 0:
+            result = call(last_kernel, whole, (valid, mine, *arrived, i_high, i_low), [SMEM],
+                          scratch(ext, width) + final, None, HBM, off=off, width=width, **known)
+        else:
+            part = call(part_kernel, shape(grid_rows, width), (mine, *arrived[1:], i_high, i_low), (),
+                        scratch(ext, width), **known)
+            args = (valid, part, arrived[0], i_high, i_low, result)
+            result = call(tail_kernel, whole, args, [SMEM] + [VMEM] * 4 + [HBM], final, {5: 0}, HBM,
+                          own=own, off=off, width=width)
     return result
 
 

time: 113 us -> 113 us (level)
  the two profiles are of different devices: /device:TPU:0 before, /device:TPU:17 now
where the time goes in v2:
time: 113 us
  starting transfers between devices  69.6 us (62%)
  Pallas kernels  27.4 us (24%)
  waiting for transfers between devices  14.5 us (13%)
  between operations  1.28 us (1%)
    ppermute x40, starting transfers between devices, exchange(): arrived.append(lax.ppermute(piece, ('ty', 'tx'), pairs))  69.6 us
    pallas_call x14, Pallas kernels, call(): pl.pallas_call(functools.partial(kernel, **more), out_shape=outs, in_spec...  27.4 us
    ppermute x40, waiting for transfers between devices, exchange(): arrived.append(lax.ppermute(piece, ('ty', 'tx'), pairs))  14.5 us
  transfers between devices with their start and end apart: 40, of which 6 were waited for; matrix products, arithmetic and copies ran while one was open for 0% of the time, Pallas kernels for 20%

profile of v2, /device:TPU:17, one launch (start us, length us, event | category | flops | bytes accessed | tf_op | source)
XLA Modules:
  0.0 112.8 jit_solution(10141130969686662616)
XLA Ops:
  0.7 3.1 %shard_map.74 = (f32[128,384]{1,0:T(8,128)S(1)}, f32[128,384]{1,0:T(8,128)S(1)}, f32[128,384]{1,0:T(8,128)S(1)}, f32[128,256]{1,0:T(8,128)S(1)}, f32[128,256]{1,0:T(8,128)S(1)}, /*index=5*/f32[128,256]{1,0:T(8,128)S(1)}) custom-call(s32[1,1]{1,0:T(1,128)S(6)} %copy.10.valid, s32[1,1]{1,0:T(1,128)} %bitcast.odd, f32[1,1,512,640]{3,2,1,0:T(8,128)} %ctrl.3, ...), custom_call_target="tpu_custom_call" | custom-call | flops 1073741824 | bytes 4194304 | tf_op jit(solution)/shard_map/pallas_call | solution.py:301
  3.8 0.0 copy-start
  3.8 0.0 copy-start.2
  3.8 0.0 copy-start.4
  3.8 1.3 %collective-permute-start = (f32[128,256]{1,0:T(8,128)S(1)}, f32[128,256]{1,0:T(8,128)S(1)}, u32[]{:S(2)}, u32[]{:S(2)}) collective-permute-start(f32[128,256]{1,0:T(8,128)S(1)} %get-tuple-element.62), channel_id=1, source_target_pairs={{0,1},{1,0},{2,3},{3,2},{4,5},{5,4},{6,7},{7,6},{8,9},{9,8},{10,11... | collective-permute-start | bytes 393224 | tf_op jit(solution)/shard_map/ppermute | solution.py:65
  5.1 4.0 %shard_map.73 = (f32[512,384]{1,0:T(8,128)S(1)}, f32[64,384]{1,0:T(8,128)S(1)}, f32[64,384]{1,0:T(8,128)S(1)}, f32[512,256]{1,0:T(8,128)S(1)}, f32[64,256]{1,0:T(8,128)S(1)}, /*index=5*/f32[64,256]{1,0:T(8,128)S(1)}) custom-call(s32[1,1]{1,0:T(1,128)S(6)} %copy.10.valid, s32[1,1]{1,0:T(1,128)} %bitcast.odd, f32[1,1,512,640]{3,2,1,0:T(8,128)} %ctrl.3, ...), custom_call_target="tpu_custom_call" | custom-call | flops 1073741824 | bytes 4194304 | tf_op jit(solution)/shard_map/pallas_call | solution.py:301
  9.1 1.0 collective-permute-start.3
  10.2 3.0 %collective-permute-start.4 = (f32[64,256]{1,0:T(8,128)S(1)}, f32[64,256]{1,0:T(8,128)S(1)}, u32[]{:S(2)}, u32[]{:S(2)}) collective-permute-start(f32[64,256]{1,0:T(8,128)S(1)} %get-tuple-element.66), channel_id=1, source_target_pairs={{2,4},{3,5},{4,2},{5,3},{6,8},{7,9},{8,6},{9,7},{10,12},{11,13},{1... | collective-permute-start | bytes 196616 | tf_op jit(solution)/shard_map/ppermute | solution.py:65
  13.2 0.6 collective-permute-start.1
  13.8 4.1 %collective-permute-start.2 = (f32[128,256]{1,0:T(8,128)S(1)}, f32[128,256]{1,0:T(8,128)S(1)}, u32[]{:S(2)}, u32[]{:S(2)}) collective-permute-start(f32[128,256]{1,0:T(8,128)S(1)} %get-tuple-element.64), channel_id=1, source_target_pairs={{2,5},{3,4},{4,3},{5,2},{6,9},{7,8},{8,7},{9,6},{10,13},{11,12},{1... | collective-permute-start | bytes 393224 | tf_op jit(solution)/shard_map/ppermute | solution.py:65
  17.9 0.3 collective-permute-start.20
  18.2 0.7 collective-permute-start.21
  19.0 0.0 collective-permute-done.refs_0_
  19.0 3.9 %collective-permute-start.22 = (f32[128,384]{1,0:T(8,128)S(1)}, f32[128,384]{1,0:T(8,128)S(1)}, u32[]{:S(2)}, u32[]{:S(2)}) collective-permute-start(f32[128,384]{1,0:T(8,128)S(1)} %get-tuple-element.96), channel_id=1, source_target_pairs={{2,5},{3,4},{4,3},{5,2},{6,9},{7,8},{8,7},{9,6},{10,13},{11,12},{1... | collective-permute-start | bytes 589832 | tf_op jit(solution)/shard_map/ppermute | solution.py:65
  22.9 1.7 %shard_map.75 = (bf16[1024,512]{1,0:T(8,128)(2,1)S(1)}, bf16[1024,512]{1,0:T(8,128)(2,1)S(1)}, bf16[512,512]{1,0:T(8,128)(2,1)S(1)}) custom-call(s32[1,1]{1,0:T(1,128)} %bitcast.odd, f32[1,1,4,128,512]{4,3,2,1,0:T(8,128)S(1)} %copy-done, s32[1,1,4,512]{3,2,1,0:T(4,128)S(1)} %copy-done.2, s32[1,1,8,64]{3,2,1,0:T(8,128)S(1)} %copy-done.4), custom_call_target="tpu_custom_call" | custom-call | flops 1073741824 | bytes 4194304 | tf_op jit(solution)/shard_map/pallas_call | solution.py:301
  24.6 0.1 collective-permute-start.23
  24.7 2.5 %collective-permute-start.24 = (f32[64,384]{1,0:T(8,128)S(1)}, f32[64,384]{1,0:T(8,128)S(1)}, u32[]{:S(2)}, u32[]{:S(2)}) collective-permute-start(f32[64,384]{1,0:T(8,128)S(1)} %get-tuple-element.98), channel_id=1, source_target_pairs={{2,4},{3,5},{4,2},{5,3},{6,8},{7,9},{8,6},{9,7},{10,12},{11,13},{1... | collective-permute-start | bytes 294920 | tf_op jit(solution)/shard_map/ppermute | solution.py:65
  27.2 1.8 %shard_map.76 = (f32[512,256]{1,0:T(8,128)S(1)}, f32[128,256]{1,0:T(8,128)S(1)}, f32[128,256]{1,0:T(8,128)S(1)}, f32[128,256]{1,0:T(8,128)S(1)}, f32[64,256]{1,0:T(8,128)S(1)}, /*index=5*/f32[64,256]{1,0:T(8,128)S(1)}) custom-call(f32[512,256]{1,0:T(8,128)S(1)} %get-tuple-element.61.own_in, f32[128,256]{1,0:T(8,128)S(1)} %collective-permute-done.refs_0_, ...), custom_call_target="tpu_custom_call" | custom-call | flops 1073741824 | bytes 4194304 | tf_op jit(solution)/shard_map/pallas_call | solution.py:301
  29.0 0.7 collective-permute-start.5
  29.8 2.2 %collective-permute-done.24.refs_4_ = f32[64,384]{1,0:T(8,128)S(1)} collective-permute-done((f32[64,384]{1,0:T(8,128)S(1)}, f32[64,384]{1,0:T(8,128)S(1)}, u32[]{:S(2)}, u32[]{:S(2)}) %collective-permute-start.24) | collective-permute-done | bytes 98336 | tf_op jit(solution)/shard_map/ppermute | solution.py:65
  31.9 0.1 collective-permute-start.8
  32.1 2.0 %collective-permute-start.9 = (f32[64,256]{1,0:T(8,128)S(1)}, f32[64,256]{1,0:T(8,128)S(1)}, u32[]{:S(2)}, u32[]{:S(2)}) collective-permute-start(f32[64,256]{1,0:T(8,128)S(1)} %get-tuple-element.75), channel_id=1, source_target_pairs={{2,4},{3,5},{4,2},{5,3},{6,8},{7,9},{8,6},{9,7},{10,12},{11,13},{1... | collective-permute-start | bytes 196616 | tf_op jit(solution)/shard_map/ppermute | solution.py:65
  34.1 2.0 %collective-permute-start.6 = (f32[128,256]{1,0:T(8,128)S(1)}, f32[128,256]{1,0:T(8,128)S(1)}, u32[]{:S(2)}, u32[]{:S(2)}) collective-permute-start(f32[128,256]{1,0:T(8,128)S(1)} %get-tuple-element.72), channel_id=1, source_target_pairs={{0,3},{1,2},{2,1},{3,0},{4,7},{5,6},{6,5},{7,4},{8,11},{9,10},{10,... | collective-permute-start | bytes 393224 | tf_op jit(solution)/shard_map/ppermute | solution.py:65
  36.1 0.3 collective-permute-done.22.refs_2_
  36.4 4.2 %collective-permute-start.7 = (f32[128,256]{1,0:T(8,128)S(1)}, f32[128,256]{1,0:T(8,128)S(1)}, u32[]{:S(2)}, u32[]{:S(2)}) collective-permute-start(f32[128,256]{1,0:T(8,128)S(1)} %get-tuple-element.73), channel_id=1, source_target_pairs={{2,5},{3,4},{4,3},{5,2},{6,9},{7,8},{8,7},{9,6},{10,13},{11,12},{1... | collective-permute-start | bytes 393224 | tf_op jit(solution)/shard_map/ppermute | solution.py:65
  40.6 2.5 %shard_map.82 = (f32[512,384]{1,0:T(8,128)S(1)}, f32[128,384]{1,0:T(8,128)S(1)}, f32[128,384]{1,0:T(8,128)S(1)}, f32[128,384]{1,0:T(8,128)S(1)}, f32[64,384]{1,0:T(8,128)S(1)}, /*index=5*/f32[64,384]{1,0:T(8,128)S(1)}) custom-call(f32[512,384]{1,0:T(8,128)S(1)} %get-tuple-element.93.own_in, f32[128,384]{1,0:T(8,128)S(1)} %collective-permute-done.20.refs_0_, ...), custom_call_target="tpu_custom_call" | custom-call | flops 1073741824 | bytes 4194304 | tf_op jit(solution)/shard_map/pallas_call | solution.py:301
  43.1 0.3 collective-permute-start.25
  43.4 0.7 collective-permute-start.26
  44.2 3.3 %collective-permute-start.27 = (f32[128,384]{1,0:T(8,128)S(1)}, f32[128,384]{1,0:T(8,128)S(1)}, u32[]{:S(2)}, u32[]{:S(2)}) collective-permute-start(f32[128,384]{1,0:T(8,128)S(1)} %get-tuple-element.102), channel_id=1, source_target_pairs={{2,5},{3,4},{4,3},{5,2},{6,9},{7,8},{8,7},{9,6},{10,13},{11,12},{1... | collective-permute-start | bytes 589832 | tf_op jit(solution)/shard_map/ppermute | solution.py:65
  47.5 1.5 %shard_map.77 = (bf16[512,1024]{1,0:T(8,128)(2,1)S(1)}, bf16[512,1024]{1,0:T(8,128)(2,1)S(1)}, bf16[512,512]{1,0:T(8,128)(2,1)S(1)}) custom-call(s32[1,1]{1,0:T(1,128)} %bitcast.odd, f32[1,1,4,128,512]{4,3,2,1,0:T(8,128)S(1)} %copy-done, s32[1,1,4,512]{3,2,1,0:T(4,128)S(1)} %copy-done.2, bf16[512,512]{1,0:T(8,128)(2,1)S(1)} %get-tuple-element.67.refs_5_.ht), custom_call_target="tpu_custom_call" | custom-call | flops 1073741824 | bytes 4194304 | tf_op jit(solution)/shard_map/pallas_call | solution.py:301
  48.9 0.3 collective-permute-start.28
  49.2 2.5 %collective-permute-start.29 = (f32[64,384]{1,0:T(8,128)S(1)}, f32[64,384]{1,0:T(8,128)S(1)}, u32[]{:S(2)}, u32[]{:S(2)}) collective-permute-start(f32[64,384]{1,0:T(8,128)S(1)} %get-tuple-element.104), channel_id=1, source_target_pairs={{2,4},{3,5},{4,2},{5,3},{6,8},{7,9},{8,6},{9,7},{10,12},{11,13},{1... | collective-permute-start | bytes 294920 | tf_op jit(solution)/shard_map/ppermute | solution.py:65
  51.7 1.3 %shard_map.78 = (f32[512,256]{1,0:T(8,128)S(1)}, f32[128,256]{1,0:T(8,128)S(1)}, f32[128,256]{1,0:T(8,128)S(1)}, f32[128,256]{1,0:T(8,128)S(1)}, f32[64,256]{1,0:T(8,128)S(1)}, /*index=5*/f32[64,256]{1,0:T(8,128)S(1)}) custom-call(f32[512,256]{1,0:T(8,128)S(1)} %get-tuple-element.70.own_in, f32[128,256]{1,0:T(8,128)S(1)} %collective-permute-done.5.refs_0_, ...), custom_call_target="tpu_custom_call" | custom-call | flops 1073741824 | bytes 4194304 | tf_op jit(solution)/shard_map/pallas_call | solution.py:301
  53.0 1.1 collective-permute-start.10
  54.1 3.4 %collective-permute-done.29.refs_4_ = f32[64,384]{1,0:T(8,128)S(1)} collective-permute-done((f32[64,384]{1,0:T(8,128)S(1)}, f32[64,384]{1,0:T(8,128)S(1)}, u32[]{:S(2)}, u32[]{:S(2)}) %collective-permute-start.29) | collective-permute-done | bytes 98336 | tf_op jit(solution)/shard_map/ppermute | solution.py:65
  57.5 1.9 %collective-permute-start.14 = (f32[64,256]{1,0:T(8,128)S(1)}, f32[64,256]{1,0:T(8,128)S(1)}, u32[]{:S(2)}, u32[]{:S(2)}) collective-permute-start(f32[64,256]{1,0:T(8,128)S(1)} %get-tuple-element.82), channel_id=1, source_target_pairs={{2,4},{3,5},{4,2},{5,3},{6,8},{7,9},{8,6},{9,7},{10,12},{11,13},{1... | collective-permute-start | bytes 196616 | tf_op jit(solution)/shard_map/ppermute | solution.py:65
  59.4 4.6 %collective-permute-start.11 = (f32[128,256]{1,0:T(8,128)S(1)}, f32[128,256]{1,0:T(8,128)S(1)}, u32[]{:S(2)}, u32[]{:S(2)}) collective-permute-start(f32[128,256]{1,0:T(8,128)S(1)} %get-tuple-element.79), channel_id=1, source_target_pairs={{0,3},{1,2},{2,1},{3,0},{4,7},{5,6},{6,5},{7,4},{8,11},{9,10},{10,... | collective-permute-start | bytes 393224 | tf_op jit(solution)/shard_map/ppermute | solution.py:65
  64.0 2.8 %collective-permute-start.12 = (f32[128,256]{1,0:T(8,128)S(1)}, f32[128,256]{1,0:T(8,128)S(1)}, u32[]{:S(2)}, u32[]{:S(2)}) collective-permute-start(f32[128,256]{1,0:T(8,128)S(1)} %get-tuple-element.80), channel_id=1, source_target_pairs={{2,5},{3,4},{4,3},{5,2},{6,9},{7,8},{8,7},{9,6},{10,13},{11,12},{1... | collective-permute-start | bytes 393224 | tf_op jit(solution)/shard_map/ppermute | solution.py:65
  66.8 1.4 %shard_map.83 = (f32[512,384]{1,0:T(8,128)S(1)}, f32[128,384]{1,0:T(8,128)S(1)}, f32[128,384]{1,0:T(8,128)S(1)}, f32[128,384]{1,0:T(8,128)S(1)}, f32[64,384]{1,0:T(8,128)S(1)}, /*index=5*/f32[64,384]{1,0:T(8,128)S(1)}) custom-call(f32[512,384]{1,0:T(8,128)S(1)} %get-tuple-element.99.own_in, f32[128,384]{1,0:T(8,128)S(1)} %collective-permute-done.25.refs_0_, ...), custom_call_target="tpu_custom_call" | custom-call | flops 1073741824 | bytes 4194304 | tf_op jit(solution)/shard_map/pallas_call | solution.py:301
  68.2 1.0 collective-permute-start.30
  69.2 0.5 collective-permute-start.31
  69.7 2.5 %collective-permute-start.32 = (f32[128,384]{1,0:T(8,128)S(1)}, f32[128,384]{1,0:T(8,128)S(1)}, u32[]{:S(2)}, u32[]{:S(2)}) collective-permute-start(f32[128,384]{1,0:T(8,128)S(1)} %get-tuple-element.108), channel_id=1, source_target_pairs={{2,5},{3,4},{4,3},{5,2},{6,9},{7,8},{8,7},{9,6},{10,13},{11,12},{1... | collective-permute-start | bytes 589832 | tf_op jit(solution)/shard_map/ppermute | solution.py:65
  72.2 1.7 %collective-permute-start.33 = (f32[64,384]{1,0:T(8,128)S(1)}, f32[64,384]{1,0:T(8,128)S(1)}, u32[]{:S(2)}, u32[]{:S(2)}) collective-permute-start(f32[64,384]{1,0:T(8,128)S(1)} %get-tuple-element.109), channel_id=1, source_target_pairs={{0,2},{1,3},{2,0},{3,1},{4,6},{5,7},{6,4},{7,5},{8,10},{9,11},{10,... | collective-permute-start | bytes 294920 | tf_op jit(solution)/shard_map/ppermute | solution.py:65
  74.0 2.0 %collective-permute-start.34 = (f32[64,384]{1,0:T(8,128)S(1)}, f32[64,384]{1,0:T(8,128)S(1)}, u32[]{:S(2)}, u32[]{:S(2)}) collective-permute-start(f32[64,384]{1,0:T(8,128)S(1)} %get-tuple-element.110), channel_id=1, source_target_pairs={{2,4},{3,5},{4,2},{5,3},{6,8},{7,9},{8,6},{9,7},{10,12},{11,13},{1... | collective-permute-start | bytes 294920 | tf_op jit(solution)/shard_map/ppermute | solution.py:65
  75.9 1.4 %shard_map.79 = (f32[512,256]{1,0:T(8,128)S(1)}, f32[128,256]{1,0:T(8,128)S(1)}, f32[128,256]{1,0:T(8,128)S(1)}, f32[128,256]{1,0:T(8,128)S(1)}, f32[64,256]{1,0:T(8,128)S(1)}, /*index=5*/f32[64,256]{1,0:T(8,128)S(1)}) custom-call(f32[512,256]{1,0:T(8,128)S(1)} %get-tuple-element.77.own_in, f32[128,256]{1,0:T(8,128)S(1)} %collective-permute-done.10.refs_0_, ...), custom_call_target="tpu_custom_call" | custom-call | flops 1073741824 | bytes 4194304 | tf_op jit(solution)/shard_map/pallas_call | solution.py:301
  77.4 1.9 %collective-permute-start.15 = (f32[128,256]{1,0:T(8,128)S(1)}, f32[128,256]{1,0:T(8,128)S(1)}, u32[]{:S(2)}, u32[]{:S(2)}) collective-permute-start(f32[128,256]{1,0:T(8,128)S(1)} %get-tuple-element.86), channel_id=1, source_target_pairs={{0,3},{1,2},{2,1},{3,0},{4,7},{5,6},{6,5},{7,4},{8,11},{9,10},{10,... | collective-permute-start | bytes 393224 | tf_op jit(solution)/shard_map/ppermute | solution.py:65
  79.2 2.0 %collective-permute-done.34.refs_4_ = f32[64,384]{1,0:T(8,128)S(1)} collective-permute-done((f32[64,384]{1,0:T(8,128)S(1)}, f32[64,384]{1,0:T(8,128)S(1)}, u32[]{:S(2)}, u32[]{:S(2)}) %collective-permute-start.34) | collective-permute-done | bytes 98336 | tf_op jit(solution)/shard_map/ppermute | solution.py:65
  81.2 2.6 %collective-permute-start.18 = (f32[64,256]{1,0:T(8,128)S(1)}, f32[64,256]{1,0:T(8,128)S(1)}, u32[]{:S(2)}, u32[]{:S(2)}) collective-permute-start(f32[64,256]{1,0:T(8,128)S(1)} %get-tuple-element.89), channel_id=1, source_target_pairs={{2,4},{3,5},{4,2},{5,3},{6,8},{7,9},{8,6},{9,7},{10,12},{11,13},{1... | collective-permute-start | bytes 196616 | tf_op jit(solution)/shard_map/ppermute | solution.py:65
  83.9 3.3 %collective-permute-start.16 = (f32[128,256]{1,0:T(8,128)S(1)}, f32[128,256]{1,0:T(8,128)S(1)}, u32[]{:S(2)}, u32[]{:S(2)}) collective-permute-start(f32[128,256]{1,0:T(8,128)S(1)} %get-tuple-element.87), channel_id=1, source_target_pairs={{2,5},{3,4},{4,3},{5,2},{6,9},{7,8},{8,7},{9,6},{10,13},{11,12},{1... | collective-permute-start | bytes 393224 | tf_op jit(solution)/shard_map/ppermute | solution.py:65
  87.2 0.0 copy-start.1
  87.2 0.0 copy-start.3
  87.2 2.5 %shard_map.84 = (f32[512,384]{1,0:T(8,128)S(1)}, f32[128,384]{1,0:T(8,128)S(1)}, f32[128,384]{1,0:T(8,128)S(1)}, f32[128,384]{1,0:T(8,128)S(1)}, f32[64,384]{1,0:T(8,128)S(1)}, /*index=5*/f32[64,384]{1,0:T(8,128)S(1)}) custom-call(f32[512,384]{1,0:T(8,128)S(1)} %get-tuple-element.105.own_in, f32[128,384]{1,0:T(8,128)S(1)} %collective-permute-done.30.refs_0_, ...), custom_call_target="tpu_custom_call" | custom-call | flops 1073741824 | bytes 4194304 | tf_op jit(solution)/shard_map/pallas_call | solution.py:301
  89.7 1.3 %collective-permute-start.38 = (f32[64,384]{1,0:T(8,128)S(1)}, f32[64,384]{1,0:T(8,128)S(1)}, u32[]{:S(2)}, u32[]{:S(2)}) collective-permute-start(f32[64,384]{1,0:T(8,128)S(1)} %get-tuple-element.115), channel_id=1, source_target_pairs={{0,2},{1,3},{2,0},{3,1},{4,6},{5,7},{6,4},{7,5},{8,10},{9,11},{10,... | collective-permute-start | bytes 294920 | tf_op jit(solution)/shard_map/ppermute | solution.py:65
  91.0 1.0 collective-permute-start.35
  92.0 0.7 collective-permute-start.36
  92.7 3.6 %collective-permute-start.37 = (f32[128,384]{1,0:T(8,128)S(1)}, f32[128,384]{1,0:T(8,128)S(1)}, u32[]{:S(2)}, u32[]{:S(2)}) collective-permute-start(f32[128,384]{1,0:T(8,128)S(1)} %get-tuple-element.114), channel_id=1, source_target_pairs={{2,5},{3,4},{4,3},{5,2},{6,9},{7,8},{8,7},{9,6},{10,13},{11,12},{1... | collective-permute-start | bytes 589832 | tf_op jit(solution)/shard_map/ppermute | solution.py:65
  96.3 1.4 %shard_map.80 = (bf16[512,1024]{1,0:T(8,128)(2,1)S(1)}, bf16[512,1024]{1,0:T(8,128)(2,1)S(1)}) custom-call(s32[1,1]{1,0:T(1,128)} %bitcast.odd, f32[1,1,4,128,384]{4,3,2,1,0:T(8,128)S(1)} %copy-done.1, s32[1,1,4,384]{3,2,1,0:T(4,128)S(1)} %copy-done.3), custom_call_target="tpu_custom_call" | custom-call | flops 1073741824 | bytes 4194304 | tf_op jit(solution)/shard_map/pallas_call | solution.py:301
  97.7 1.2 %collective-permute-start.19 = (f32[128,256]{1,0:T(8,128)S(1)}, f32[128,256]{1,0:T(8,128)S(1)}, u32[]{:S(2)}, u32[]{:S(2)}) collective-permute-start(f32[128,256]{1,0:T(8,128)S(1)} %get-tuple-element.92), channel_id=1, source_target_pairs={{0,1},{1,0},{2,3},{3,2},{4,5},{5,4},{6,7},{7,6},{8,9},{9,8},{10,11... | collective-permute-start | bytes 393224 | tf_op jit(solution)/shard_map/ppermute | solution.py:65
  98.9 2.3 %collective-permute-start.39 = (f32[64,384]{1,0:T(8,128)S(1)}, f32[64,384]{1,0:T(8,128)S(1)}, u32[]{:S(2)}, u32[]{:S(2)}) collective-permute-start(f32[64,384]{1,0:T(8,128)S(1)} %get-tuple-element.116), channel_id=1, source_target_pairs={{2,4},{3,5},{4,2},{5,3},{6,8},{7,9},{8,6},{9,7},{10,12},{11,13},{1... | collective-permute-start | bytes 294920 | tf_op jit(solution)/shard_map/ppermute | solution.py:65
  101.2 1.0 shard_map.81.part
  102.2 3.0 %collective-permute-done.39.refs_4_ = f32[64,384]{1,0:T(8,128)S(1)} collective-permute-done((f32[64,384]{1,0:T(8,128)S(1)}, f32[64,384]{1,0:T(8,128)S(1)}, u32[]{:S(2)}, u32[]{:S(2)}) %collective-permute-start.39) | collective-permute-done | bytes 98336 | tf_op jit(solution)/shard_map/ppermute | solution.py:65
  105.2 3.6 %collective-permute-done.37.refs_2_ = f32[128,384]{1,0:T(8,128)S(1)} collective-permute-done((f32[128,384]{1,0:T(8,128)S(1)}, f32[128,384]{1,0:T(8,128)S(1)}, u32[]{:S(2)}, u32[]{:S(2)}) %collective-permute-start.37) | collective-permute-done | bytes 196640 | tf_op jit(solution)/shard_map/ppermute | solution.py:65
  108.8 2.6 %shard_map.85.so_far = f32[1,1,512,640]{3,2,1,0:T(8,128)} custom-call(s32[1,1]{1,0:T(1,128)S(6)} %copy.10.valid, f32[512,384]{1,0:T(8,128)S(1)} %get-tuple-element.111.own_in, f32[128,384]{1,0:T(8,128)S(1)} %collective-permute-done.35.refs_0_, f32[128,384]{1,0:T(8,128)S(1)} %collective-permute-done.36.refs_1_, ...), custom_call_target="tpu_custom_call" | custom-call | flops 1073741824 | bytes 4194304 | tf_op jit(solution)/shard_map/pallas_call | solution.py:301
  111.4 1.2 %shard_map.86 = f32[1,1,512,640]{3,2,1,0:T(8,128)} custom-call(s32[1,1]{1,0:T(1,128)S(6)} %copy.10.valid, f32[512,256]{1,0:T(8,128)S(1)} %shard_map.81.part, f32[128,256]{1,0:T(8,128)S(1)} %collective-permute-done.19.late, bf16[512,1024]{1,0:T(8,128)(2,1)S(1)} %get-tuple-element.90.refs_4_.refs_5_.m_high, ...), custom_call_target="tpu_custom_call", output_to_operand_aliasing={{}: (5, {})} | custom-call | flops 1073741824 | bytes 4194304 | tf_op jit(solution)/shard_map/pallas_call | solution.py:301
  (40 shorter events, 0.1 us)
Async XLA Ops:
  3.8 19.0 %copy-start = (f32[1,1,4,128,512]{4,3,2,1,0:T(8,128)S(1)}, f32[1,1,4,128,512]{4,3,2,1,0:T(8,128)}, u32[]{:S(2)}) copy-start(f32[1,1,4,128,512]{4,3,2,1,0:T(8,128)} %wt.8) | copy-start | bytes 3145732
  3.8 19.0 %copy-start.2 = (s32[1,1,4,512]{3,2,1,0:T(4,128)S(1)}, s32[1,1,4,512]{3,2,1,0:T(4,128)}, u32[]{:S(2)}) copy-start(s32[1,1,4,512]{3,2,1,0:T(4,128)} %cols.8) | copy-start | bytes 24580
  3.8 19.0 %copy-start.4 = (s32[1,1,8,64]{3,2,1,0:T(8,128)S(1)}, s32[1,1,8,64]{3,2,1,0:T(8,128)}, u32[]{:S(2)}) copy-start(s32[1,1,8,64]{3,2,1,0:T(8,128)} %index.1) | copy-start | bytes 6148
  3.8 15.1 %collective-permute-start = (f32[128,256]{1,0:T(8,128)S(1)}, f32[128,256]{1,0:T(8,128)S(1)}, u32[]{:S(2)}, u32[]{:S(2)}) collective-permute-start(f32[128,256]{1,0:T(8,128)S(1)} %get-tuple-element.62), channel_id=1, source_target_pairs={{0,1},{1,0},{2,3},{3,2},{4,5},{5,4},{6,7},{7,6},{8,9},{9,8},{10,11... | collective-permute-start | bytes 393224 | tf_op jit(solution)/shard_map/ppermute | solution.py:65
  9.1 8.7 %collective-permute-start.3 = (f32[64,256]{1,0:T(8,128)S(1)}, f32[64,256]{1,0:T(8,128)S(1)}, u32[]{:S(2)}, u32[]{:S(2)}) collective-permute-start(f32[64,256]{1,0:T(8,128)S(1)} %get-tuple-element.65), channel_id=1, source_target_pairs={{0,2},{1,3},{2,0},{3,1},{4,6},{5,7},{6,4},{7,5},{8,10},{9,11},{10,... | collective-permute-start | bytes 196616 | tf_op jit(solution)/shard_map/ppermute | solution.py:65
  10.2 8.1 %collective-permute-start.4 = (f32[64,256]{1,0:T(8,128)S(1)}, f32[64,256]{1,0:T(8,128)S(1)}, u32[]{:S(2)}, u32[]{:S(2)}) collective-permute-start(f32[64,256]{1,0:T(8,128)S(1)} %get-tuple-element.66), channel_id=1, source_target_pairs={{2,4},{3,5},{4,2},{5,3},{6,8},{7,9},{8,6},{9,7},{10,12},{11,13},{1... | collective-permute-start | bytes 196616 | tf_op jit(solution)/shard_map/ppermute | solution.py:65
  13.2 11.3 %collective-permute-start.1 = (f32[128,256]{1,0:T(8,128)S(1)}, f32[128,256]{1,0:T(8,128)S(1)}, u32[]{:S(2)}, u32[]{:S(2)}) collective-permute-start(f32[128,256]{1,0:T(8,128)S(1)} %get-tuple-element.63), channel_id=1, source_target_pairs={{0,3},{1,2},{2,1},{3,0},{4,7},{5,6},{6,5},{7,4},{8,11},{9,10},{10,... | collective-permute-start | bytes 393224 | tf_op jit(solution)/shard_map/ppermute | solution.py:65
  13.8 10.9 %collective-permute-start.2 = (f32[128,256]{1,0:T(8,128)S(1)}, f32[128,256]{1,0:T(8,128)S(1)}, u32[]{:S(2)}, u32[]{:S(2)}) collective-permute-start(f32[128,256]{1,0:T(8,128)S(1)} %get-tuple-element.64), channel_id=1, source_target_pairs={{2,5},{3,4},{4,3},{5,2},{6,9},{7,8},{8,7},{9,6},{10,13},{11,12},{1... | collective-permute-start | bytes 393224 | tf_op jit(solution)/shard_map/ppermute | solution.py:65
  17.9 14.2 %collective-permute-start.20 = (f32[128,384]{1,0:T(8,128)S(1)}, f32[128,384]{1,0:T(8,128)S(1)}, u32[]{:S(2)}, u32[]{:S(2)}) collective-permute-start(f32[128,384]{1,0:T(8,128)S(1)} %get-tuple-element.94), channel_id=1, source_target_pairs={{0,1},{1,0},{2,3},{3,2},{4,5},{5,4},{6,7},{7,6},{8,9},{9,8},{10,11... | collective-permute-start | bytes 589832 | tf_op jit(solution)/shard_map/ppermute | solution.py:65
  18.2 15.8 %collective-permute-start.21 = (f32[128,384]{1,0:T(8,128)S(1)}, f32[128,384]{1,0:T(8,128)S(1)}, u32[]{:S(2)}, u32[]{:S(2)}) collective-permute-start(f32[128,384]{1,0:T(8,128)S(1)} %get-tuple-element.95), channel_id=1, source_target_pairs={{0,3},{1,2},{2,1},{3,0},{4,7},{5,6},{6,5},{7,4},{8,11},{9,10},{10,... | collective-permute-start | bytes 589832 | tf_op jit(solution)/shard_map/ppermute | solution.py:65
  19.0 17.5 %collective-permute-start.22 = (f32[128,384]{1,0:T(8,128)S(1)}, f32[128,384]{1,0:T(8,128)S(1)}, u32[]{:S(2)}, u32[]{:S(2)}) collective-permute-start(f32[128,384]{1,0:T(8,128)S(1)} %get-tuple-element.96), channel_id=1, source_target_pairs={{2,5},{3,4},{4,3},{5,2},{6,9},{7,8},{8,7},{9,6},{10,13},{11,12},{1... | collective-permute-start | bytes 589832 | tf_op jit(solution)/shard_map/ppermute | solution.py:65
  24.6 4.5 %collective-permute-start.23 = (f32[64,384]{1,0:T(8,128)S(1)}, f32[64,384]{1,0:T(8,128)S(1)}, u32[]{:S(2)}, u32[]{:S(2)}) collective-permute-start(f32[64,384]{1,0:T(8,128)S(1)} %get-tuple-element.97), channel_id=1, source_target_pairs={{0,2},{1,3},{2,0},{3,1},{4,6},{5,7},{6,4},{7,5},{8,10},{9,11},{10,... | collective-permute-start | bytes 294920 | tf_op jit(solution)/shard_map/ppermute | solution.py:65
  24.7 7.3 %collective-permute-start.24 = (f32[64,384]{1,0:T(8,128)S(1)}, f32[64,384]{1,0:T(8,128)S(1)}, u32[]{:S(2)}, u32[]{:S(2)}) collective-permute-start(f32[64,384]{1,0:T(8,128)S(1)} %get-tuple-element.98), channel_id=1, source_target_pairs={{2,4},{3,5},{4,2},{5,3},{6,8},{7,9},{8,6},{9,7},{10,12},{11,13},{1... | collective-permute-start | bytes 294920 | tf_op jit(solution)/shard_map/ppermute | solution.py:65
  29.0 15.1 %collective-permute-start.5 = (f32[128,256]{1,0:T(8,128)S(1)}, f32[128,256]{1,0:T(8,128)S(1)}, u32[]{:S(2)}, u32[]{:S(2)}) collective-permute-start(f32[128,256]{1,0:T(8,128)S(1)} %get-tuple-element.71), channel_id=1, source_target_pairs={{0,1},{1,0},{2,3},{3,2},{4,5},{5,4},{6,7},{7,6},{8,9},{9,8},{10,11... | collective-permute-start | bytes 393224 | tf_op jit(solution)/shard_map/ppermute | solution.py:65
  31.9 11.2 %collective-permute-start.8 = (f32[64,256]{1,0:T(8,128)S(1)}, f32[64,256]{1,0:T(8,128)S(1)}, u32[]{:S(2)}, u32[]{:S(2)}) collective-permute-start(f32[64,256]{1,0:T(8,128)S(1)} %get-tuple-element.74), channel_id=1, source_target_pairs={{0,2},{1,3},{2,0},{3,1},{4,6},{5,7},{6,4},{7,5},{8,10},{9,11},{10,... | collective-permute-start | bytes 196616 | tf_op jit(solution)/shard_map/ppermute | solution.py:65
  32.1 11.4 %collective-permute-start.9 = (f32[64,256]{1,0:T(8,128)S(1)}, f32[64,256]{1,0:T(8,128)S(1)}, u32[]{:S(2)}, u32[]{:S(2)}) collective-permute-start(f32[64,256]{1,0:T(8,128)S(1)} %get-tuple-element.75), channel_id=1, source_target_pairs={{2,4},{3,5},{4,2},{5,3},{6,8},{7,9},{8,6},{9,7},{10,12},{11,13},{1... | collective-permute-start | bytes 196616 | tf_op jit(solution)/shard_map/ppermute | solution.py:65
  34.1 14.9 %collective-permute-start.6 = (f32[128,256]{1,0:T(8,128)S(1)}, f32[128,256]{1,0:T(8,128)S(1)}, u32[]{:S(2)}, u32[]{:S(2)}) collective-permute-start(f32[128,256]{1,0:T(8,128)S(1)} %get-tuple-element.72), channel_id=1, source_target_pairs={{0,3},{1,2},{2,1},{3,0},{4,7},{5,6},{6,5},{7,4},{8,11},{9,10},{10,... | collective-permute-start | bytes 393224 | tf_op jit(solution)/shard_map/ppermute | solution.py:65
  36.4 12.8 %collective-permute-start.7 = (f32[128,256]{1,0:T(8,128)S(1)}, f32[128,256]{1,0:T(8,128)S(1)}, u32[]{:S(2)}, u32[]{:S(2)}) collective-permute-start(f32[128,256]{1,0:T(8,128)S(1)} %get-tuple-element.73), channel_id=1, source_target_pairs={{2,5},{3,4},{4,3},{5,2},{6,9},{7,8},{8,7},{9,6},{10,13},{11,12},{1... | collective-permute-start | bytes 393224 | tf_op jit(solution)/shard_map/ppermute | solution.py:65
  43.1 14.4 %collective-permute-start.25 = (f32[128,384]{1,0:T(8,128)S(1)}, f32[128,384]{1,0:T(8,128)S(1)}, u32[]{:S(2)}, u32[]{:S(2)}) collective-permute-start(f32[128,384]{1,0:T(8,128)S(1)} %get-tuple-element.100), channel_id=1, source_target_pairs={{0,1},{1,0},{2,3},{3,2},{4,5},{5,4},{6,7},{7,6},{8,9},{9,8},{10,11... | collective-permute-start | bytes 589832 | tf_op jit(solution)/shard_map/ppermute | solution.py:65
  43.4 16.0 %collective-permute-start.26 = (f32[128,384]{1,0:T(8,128)S(1)}, f32[128,384]{1,0:T(8,128)S(1)}, u32[]{:S(2)}, u32[]{:S(2)}) collective-permute-start(f32[128,384]{1,0:T(8,128)S(1)} %get-tuple-element.101), channel_id=1, source_target_pairs={{0,3},{1,2},{2,1},{3,0},{4,7},{5,6},{6,5},{7,4},{8,11},{9,10},{10,... | collective-permute-start | bytes 589832 | tf_op jit(solution)/shard_map/ppermute | solution.py:65
  44.2 19.8 %collective-permute-start.27 = (f32[128,384]{1,0:T(8,128)S(1)}, f32[128,384]{1,0:T(8,128)S(1)}, u32[]{:S(2)}, u32[]{:S(2)}) collective-permute-start(f32[128,384]{1,0:T(8,128)S(1)} %get-tuple-element.102), channel_id=1, source_target_pairs={{2,5},{3,4},{4,3},{5,2},{6,9},{7,8},{8,7},{9,6},{10,13},{11,12},{1... | collective-permute-start | bytes 589832 | tf_op jit(solution)/shard_map/ppermute | solution.py:65
  48.9 4.1 %collective-permute-start.28 = (f32[64,384]{1,0:T(8,128)S(1)}, f32[64,384]{1,0:T(8,128)S(1)}, u32[]{:S(2)}, u32[]{:S(2)}) collective-permute-start(f32[64,384]{1,0:T(8,128)S(1)} %get-tuple-element.103), channel_id=1, source_target_pairs={{0,2},{1,3},{2,0},{3,1},{4,6},{5,7},{6,4},{7,5},{8,10},{9,11},{10,... | collective-permute-start | bytes 294920 | tf_op jit(solution)/shard_map/ppermute | solution.py:65
  49.2 8.3 %collective-permute-start.29 = (f32[64,384]{1,0:T(8,128)S(1)}, f32[64,384]{1,0:T(8,128)S(1)}, u32[]{:S(2)}, u32[]{:S(2)}) collective-permute-start(f32[64,384]{1,0:T(8,128)S(1)} %get-tuple-element.104), channel_id=1, source_target_pairs={{2,4},{3,5},{4,2},{5,3},{6,8},{7,9},{8,6},{9,7},{10,12},{11,13},{1... | collective-permute-start | bytes 294920 | tf_op jit(solution)/shard_map/ppermute | solution.py:65
  53.0 16.7 %collective-permute-start.10 = (f32[128,256]{1,0:T(8,128)S(1)}, f32[128,256]{1,0:T(8,128)S(1)}, u32[]{:S(2)}, u32[]{:S(2)}) collective-permute-start(f32[128,256]{1,0:T(8,128)S(1)} %get-tuple-element.78), channel_id=1, source_target_pairs={{0,1},{1,0},{2,3},{3,2},{4,5},{5,4},{6,7},{7,6},{8,9},{9,8},{10,11... | collective-permute-start | bytes 393224 | tf_op jit(solution)/shard_map/ppermute | solution.py:65
  57.5 10.7 %collective-permute-start.13 = (f32[64,256]{1,0:T(8,128)S(1)}, f32[64,256]{1,0:T(8,128)S(1)}, u32[]{:S(2)}, u32[]{:S(2)}) collective-permute-start(f32[64,256]{1,0:T(8,128)S(1)} %get-tuple-element.81), channel_id=1, source_target_pairs={{0,2},{1,3},{2,0},{3,1},{4,6},{5,7},{6,4},{7,5},{8,10},{9,11},{10,... | collective-permute-start | bytes 196616 | tf_op jit(solution)/shard_map/ppermute | solution.py:65
  57.5 11.7 %collective-permute-start.14 = (f32[64,256]{1,0:T(8,128)S(1)}, f32[64,256]{1,0:T(8,128)S(1)}, u32[]{:S(2)}, u32[]{:S(2)}) collective-permute-start(f32[64,256]{1,0:T(8,128)S(1)} %get-tuple-element.82), channel_id=1, source_target_pairs={{2,4},{3,5},{4,2},{5,3},{6,8},{7,9},{8,6},{9,7},{10,12},{11,13},{1... | collective-permute-start | bytes 196616 | tf_op jit(solution)/shard_map/ppermute | solution.py:65
  59.4 12.8 %collective-permute-start.11 = (f32[128,256]{1,0:T(8,128)S(1)}, f32[128,256]{1,0:T(8,128)S(1)}, u32[]{:S(2)}, u32[]{:S(2)}) collective-permute-start(f32[128,256]{1,0:T(8,128)S(1)} %get-tuple-element.79), channel_id=1, source_target_pairs={{0,3},{1,2},{2,1},{3,0},{4,7},{5,6},{6,5},{7,4},{8,11},{9,10},{10,... | collective-permute-start | bytes 393224 | tf_op jit(solution)/shard_map/ppermute | solution.py:65
  64.0 10.0 %collective-permute-start.12 = (f32[128,256]{1,0:T(8,128)S(1)}, f32[128,256]{1,0:T(8,128)S(1)}, u32[]{:S(2)}, u32[]{:S(2)}) collective-permute-start(f32[128,256]{1,0:T(8,128)S(1)} %get-tuple-element.80), channel_id=1, source_target_pairs={{2,5},{3,4},{4,3},{5,2},{6,9},{7,8},{8,7},{9,6},{10,13},{11,12},{1... | collective-permute-start | bytes 393224 | tf_op jit(solution)/shard_map/ppermute | solution.py:65
  68.2 13.1 %collective-permute-start.30 = (f32[128,384]{1,0:T(8,128)S(1)}, f32[128,384]{1,0:T(8,128)S(1)}, u32[]{:S(2)}, u32[]{:S(2)}) collective-permute-start(f32[128,384]{1,0:T(8,128)S(1)} %get-tuple-element.106), channel_id=1, source_target_pairs={{0,1},{1,0},{2,3},{3,2},{4,5},{5,4},{6,7},{7,6},{8,9},{9,8},{10,11... | collective-permute-start | bytes 589832 | tf_op jit(solution)/shard_map/ppermute | solution.py:65
  69.2 14.6 %collective-permute-start.31 = (f32[128,384]{1,0:T(8,128)S(1)}, f32[128,384]{1,0:T(8,128)S(1)}, u32[]{:S(2)}, u32[]{:S(2)}) collective-permute-start(f32[128,384]{1,0:T(8,128)S(1)} %get-tuple-element.107), channel_id=1, source_target_pairs={{0,3},{1,2},{2,1},{3,0},{4,7},{5,6},{6,5},{7,4},{8,11},{9,10},{10,... | collective-permute-start | bytes 589832 | tf_op jit(solution)/shard_map/ppermute | solution.py:65
  69.7 17.5 %collective-permute-start.32 = (f32[128,384]{1,0:T(8,128)S(1)}, f32[128,384]{1,0:T(8,128)S(1)}, u32[]{:S(2)}, u32[]{:S(2)}) collective-permute-start(f32[128,384]{1,0:T(8,128)S(1)} %get-tuple-element.108), channel_id=1, source_target_pairs={{2,5},{3,4},{4,3},{5,2},{6,9},{7,8},{8,7},{9,6},{10,13},{11,12},{1... | collective-permute-start | bytes 589832 | tf_op jit(solution)/shard_map/ppermute | solution.py:65
  72.2 5.1 %collective-permute-start.33 = (f32[64,384]{1,0:T(8,128)S(1)}, f32[64,384]{1,0:T(8,128)S(1)}, u32[]{:S(2)}, u32[]{:S(2)}) collective-permute-start(f32[64,384]{1,0:T(8,128)S(1)} %get-tuple-element.109), channel_id=1, source_target_pairs={{0,2},{1,3},{2,0},{3,1},{4,6},{5,7},{6,4},{7,5},{8,10},{9,11},{10,... | collective-permute-start | bytes 294920 | tf_op jit(solution)/shard_map/ppermute | solution.py:65
  74.0 7.3 %collective-permute-start.34 = (f32[64,384]{1,0:T(8,128)S(1)}, f32[64,384]{1,0:T(8,128)S(1)}, u32[]{:S(2)}, u32[]{:S(2)}) collective-permute-start(f32[64,384]{1,0:T(8,128)S(1)} %get-tuple-element.110), channel_id=1, source_target_pairs={{2,4},{3,5},{4,2},{5,3},{6,8},{7,9},{8,6},{9,7},{10,12},{11,13},{1... | collective-permute-start | bytes 294920 | tf_op jit(solution)/shard_map/ppermute | solution.py:65
  77.4 15.3 %collective-permute-start.15 = (f32[128,256]{1,0:T(8,128)S(1)}, f32[128,256]{1,0:T(8,128)S(1)}, u32[]{:S(2)}, u32[]{:S(2)}) collective-permute-start(f32[128,256]{1,0:T(8,128)S(1)} %get-tuple-element.86), channel_id=1, source_target_pairs={{0,3},{1,2},{2,1},{3,0},{4,7},{5,6},{6,5},{7,4},{8,11},{9,10},{10,... | collective-permute-start | bytes 393224 | tf_op jit(solution)/shard_map/ppermute | solution.py:65
  81.2 9.7 %collective-permute-start.17 = (f32[64,256]{1,0:T(8,128)S(1)}, f32[64,256]{1,0:T(8,128)S(1)}, u32[]{:S(2)}, u32[]{:S(2)}) collective-permute-start(f32[64,256]{1,0:T(8,128)S(1)} %get-tuple-element.88), channel_id=1, source_target_pairs={{0,2},{1,3},{2,0},{3,1},{4,6},{5,7},{6,4},{7,5},{8,10},{9,11},{10,... | collective-permute-start | bytes 196616 | tf_op jit(solution)/shard_map/ppermute | solution.py:65
  81.2 10.8 %collective-permute-start.18 = (f32[64,256]{1,0:T(8,128)S(1)}, f32[64,256]{1,0:T(8,128)S(1)}, u32[]{:S(2)}, u32[]{:S(2)}) collective-permute-start(f32[64,256]{1,0:T(8,128)S(1)} %get-tuple-element.89), channel_id=1, source_target_pairs={{2,4},{3,5},{4,2},{5,3},{6,8},{7,9},{8,6},{9,7},{10,12},{11,13},{1... | collective-permute-start | bytes 196616 | tf_op jit(solution)/shard_map/ppermute | solution.py:65
  83.9 13.8 %collective-permute-start.16 = (f32[128,256]{1,0:T(8,128)S(1)}, f32[128,256]{1,0:T(8,128)S(1)}, u32[]{:S(2)}, u32[]{:S(2)}) collective-permute-start(f32[128,256]{1,0:T(8,128)S(1)} %get-tuple-element.87), channel_id=1, source_target_pairs={{2,5},{3,4},{4,3},{5,2},{6,9},{7,8},{8,7},{9,6},{10,13},{11,12},{1... | collective-permute-start | bytes 393224 | tf_op jit(solution)/shard_map/ppermute | solution.py:65
  87.2 9.1 %copy-start.1 = (f32[1,1,4,128,384]{4,3,2,1,0:T(8,128)S(1)}, f32[1,1,4,128,384]{4,3,2,1,0:T(8,128)}, u32[]{:S(2)}) copy-start(f32[1,1,4,128,384]{4,3,2,1,0:T(8,128)} %wt.9) | copy-start | bytes 2359300
  87.2 9.1 %copy-start.3 = (s32[1,1,4,384]{3,2,1,0:T(4,128)S(1)}, s32[1,1,4,384]{3,2,1,0:T(4,128)}, u32[]{:S(2)}) copy-start(s32[1,1,4,384]{3,2,1,0:T(4,128)} %cols.9) | copy-start | bytes 18436
  89.7 9.2 %collective-permute-start.38 = (f32[64,384]{1,0:T(8,128)S(1)}, f32[64,384]{1,0:T(8,128)S(1)}, u32[]{:S(2)}, u32[]{:S(2)}) collective-permute-start(f32[64,384]{1,0:T(8,128)S(1)} %get-tuple-element.115), channel_id=1, source_target_pairs={{0,2},{1,3},{2,0},{3,1},{4,6},{5,7},{6,4},{7,5},{8,10},{9,11},{10,... | collective-permute-start | bytes 294920 | tf_op jit(solution)/shard_map/ppermute | solution.py:65
  91.0 14.2 %collective-permute-start.35 = (f32[128,384]{1,0:T(8,128)S(1)}, f32[128,384]{1,0:T(8,128)S(1)}, u32[]{:S(2)}, u32[]{:S(2)}) collective-permute-start(f32[128,384]{1,0:T(8,128)S(1)} %get-tuple-element.112), channel_id=1, source_target_pairs={{0,1},{1,0},{2,3},{3,2},{4,5},{5,4},{6,7},{7,6},{8,9},{9,8},{10,11... | collective-permute-start | bytes 589832 | tf_op jit(solution)/shard_map/ppermute | solution.py:65
  92.0 13.2 %collective-permute-start.36 = (f32[128,384]{1,0:T(8,128)S(1)}, f32[128,384]{1,0:T(8,128)S(1)}, u32[]{:S(2)}, u32[]{:S(2)}) collective-permute-start(f32[128,384]{1,0:T(8,128)S(1)} %get-tuple-element.113), channel_id=1, source_target_pairs={{0,3},{1,2},{2,1},{3,0},{4,7},{5,6},{6,5},{7,4},{8,11},{9,10},{10,... | collective-permute-start | bytes 589832 | tf_op jit(solution)/shard_map/ppermute | solution.py:65
  92.7 16.1 %collective-permute-start.37 = (f32[128,384]{1,0:T(8,128)S(1)}, f32[128,384]{1,0:T(8,128)S(1)}, u32[]{:S(2)}, u32[]{:S(2)}) collective-permute-start(f32[128,384]{1,0:T(8,128)S(1)} %get-tuple-element.114), channel_id=1, source_target_pairs={{2,5},{3,4},{4,3},{5,2},{6,9},{7,8},{8,7},{9,6},{10,13},{11,12},{1... | collective-permute-start | bytes 589832 | tf_op jit(solution)/shard_map/ppermute | solution.py:65
  97.7 13.7 %collective-permute-start.19 = (f32[128,256]{1,0:T(8,128)S(1)}, f32[128,256]{1,0:T(8,128)S(1)}, u32[]{:S(2)}, u32[]{:S(2)}) collective-permute-start(f32[128,256]{1,0:T(8,128)S(1)} %get-tuple-element.92), channel_id=1, source_target_pairs={{0,1},{1,0},{2,3},{3,2},{4,5},{5,4},{6,7},{7,6},{8,9},{9,8},{10,11... | collective-permute-start | bytes 393224 | tf_op jit(solution)/shard_map/ppermute | solution.py:65
  98.9 6.2 %collective-permute-start.39 = (f32[64,384]{1,0:T(8,128)S(1)}, f32[64,384]{1,0:T(8,128)S(1)}, u32[]{:S(2)}, u32[]{:S(2)}) collective-permute-start(f32[64,384]{1,0:T(8,128)S(1)} %get-tuple-element.116), channel_id=1, source_target_pairs={{2,4},{3,5},{4,2},{5,3},{6,8},{7,9},{8,6},{9,7},{10,12},{11,13},{1... | collective-permute-start | bytes 294920 | tf_op jit(solution)/shard_map/ppermute | solution.py:65

commit v3 on v2

--- a/solution.py
+++ b/solution.py
@@ -23,6 +23,12 @@
 
 def mul(left, right):
     return jnp.dot(left, right, preferred_element_type=F32)
+
+
+def mul_split(m_high, m_low, high, low):
+    width = high.shape[1]
+    both = mul(m_high, jnp.concatenate([high, low], axis=1))
+    return both[:, :width] + both[:, width:] + mul(m_low, high)
 
 
 def mul_nt(left, right):
@@ -126,14 +132,13 @@
     last = mt_high.shape[0] if last is None else last
     for start in range(first, last, TILE):
         rows = slice(start, min(start + TILE, last))
-        block = mul(mt_high[rows, :], high) + mul(mt_high[rows, :], low) + mul(mt_low[rows, :], high)
+        block = mul_split(mt_high[rows, :], mt_low[rows, :], high, low)
         emit(block, start - first + base, own_ref, spots, own, halo)
 
 
-def first_kernel(valid, odd, ctrl, wt, cols, *refs, chunks, groups, own, halo, crossing):
+def first_kernel(valid, odd, ctrl, wt, cols, high, low, blocks, cols_in, *refs, chunks, groups, own, halo):
     n = len(groups)
-    each = n if crossing else n + 1
-    outs, (mt_high, mt_low, field, blocks, cols_in, sems) = refs[: each * len(chunks)], refs[each * len(chunks) :]
+    outs, (mt_high, mt_low, field, sems) = refs[: n * len(chunks)], refs[n * len(chunks) :]
     copies = [
         pltpu.make_async_copy(cols, cols_in, sems.at[0]),
         pltpu.make_async_copy(wt, blocks, sems.at[1]),
@@ -142,40 +147,43 @@
     for copy in copies:
         copy.start()
     copies[0].wait()
-    side = CROSSING * halo
-    rows = dict(low=own) if crossing else dict(high=own, gap=side)
-    hots = hot_blocks(cols_in[0, 0], mt_high.shape[0], (odd[0, 0] == 1, own, halo), **rows)
+    hots = hot_blocks(cols_in[0, 0], mt_high.shape[0], (odd[0, 0] == 1, own, halo), low=own)
     copies[1].wait()
     build_t(blocks, hots, mt_high, mt_low)
     copies[2].wait()
+    ids = lax.broadcasted_iota(jnp.int32, high.shape, 0)
+    high[...], low[...] = split(jnp.where(ids < valid[0, 0], field[0, 0], 0.0))
+    for number, (off, width) in enumerate(chunks):
+        spots = place(outs[number * n : (number + 1) * n], groups, halo)
+        cols_of = slice(off, off + width)
+        apply_t(high[:, cols_of], low[:, cols_of], mt_high, mt_low, None, spots, own, halo, base=own)
+
+
+def rest_kernel(odd, high, low, wt, cols, *refs, chunks, groups, own, halo):
+    each = len(groups) + 1
+    outs, (mt_high, mt_low) = refs[: each * len(chunks)], refs[each * len(chunks) :]
+    side = CROSSING * halo
+    build_t(wt, hot_blocks(cols[0, 0], mt_high.shape[0], (odd[0, 0] == 1, own, halo), high=own, gap=side), mt_high, mt_low)
     for number, (off, width) in enumerate(chunks):
         mine = outs[number * each : (number + 1) * each]
-        part = field[0, 0, :, off : off + width]
-        ids = lax.broadcasted_iota(jnp.int32, part.shape, 0)
-        high, low = split(jnp.where(ids < valid[0, 0], part, 0.0))
-        if crossing:
-            apply_t(high, low, mt_high, mt_low, None, place(mine, groups, halo), own, halo, base=own)
-        else:
-            spots = place(mine[1:], groups, halo)
-            apply_t(high, low, mt_high, mt_low, mine[0], spots, own, halo, last=own)
-            apply_t(high, low, mt_high, mt_low, mine[0], spots, own, halo, base=own + side, first=own)
-
-
-def early_kernel(odd, wt, cols, index, ct_high, ct_low, ht_out, *, halo):
+        part = high[:, off : off + width], low[:, off : off + width]
+        spots = place(mine[1:], groups, halo)
+        apply_t(*part, mt_high, mt_low, mine[0], spots, own, halo, last=own)
+        apply_t(*part, mt_high, mt_low, mine[0], spots, own, halo, base=own + side, first=own)
+
+
+def early_kernel(odd, wt, cols, index, ct_high, ct_low, ht_out, h_out, *, halo):
     own = ht_out.shape[0]
     turned = odd[0, 0] == 1
     for at, (even_slot, odd_slot) in enumerate(zip(TAKEN[0], TAKEN[1])):
         row = jnp.where(turned, index[0, 0, odd_slot : odd_slot + 1, :], index[0, 0, even_slot : even_slot + 1, :])
-        ht_out[:, at * halo : (at + 1) * halo] = one_hot_t(row, own)
+        hot = one_hot_t(row, own)
+        ht_out[:, at * halo : (at + 1) * halo] = hot
+        h_out[at * halo : (at + 1) * halo, :] = hot.astype(F32).T.astype(BF16)
     build_t(wt, hot_blocks(cols[0, 0], ct_high.shape[0], (turned, own, halo)), ct_high, ct_low)
 
 
-def conv_kernel(odd, wt, cols, ht, c_high, c_low, h_out, *, halo):
-    h_out[...] = ht[...].astype(F32).T.astype(BF16)
-    build(wt, hot_blocks(cols[0, 0], c_high.shape[1], (odd[0, 0] == 1, ht.shape[0], halo)), c_high, c_low)
-
-
-def interp_kernel(odd, wt, cols, high, low, *, own, halo):
+def late_kernel(odd, wt, cols, high, low, *, own, halo):
     build(wt, hot_blocks(cols[0, 0], high.shape[1], (odd[0, 0] == 1, own, halo)), high, low)
 
 
@@ -216,8 +224,7 @@
     collect(place(arrived, groups, halo), s_high, s_low, own, halo)
     for start in range(0, m_high.shape[0], TILE):
         rows = slice(start, start + TILE)
-        out(rows, mul(m_high[rows, :], s_high[...]) + mul(m_high[rows, :], s_low[...])
-            + mul(m_low[rows, :], s_high[...]))
+        out(rows, mul_split(m_high[rows, :], m_low[rows, :], s_high[...], s_low[...]))
 
 
 def fourth_kernel(own_in, *refs, groups, own, halo):
@@ -320,32 +327,34 @@
     crossing = [group for group in groups if group[0] < CROSSING]
     straight = groups[len(crossing) :]
 
-    def first(kind, count):
-        shapes = []
-        for _, width in chunks:
-            shapes += [] if kind else [shape(own, width)]
-            shapes += [shape(len(group) * halo, width) for group in (crossing if kind else straight)]
-        outs = call(
-            first_kernel, shapes, (valid, odd, far_ctrl, far_wt, far_cols), [SMEM, SMEM, HBM, HBM, HBM],
-            [pltpu.VMEM((count, grid_rows), BF16)] * 2
-            + [pltpu.VMEM(ctrl.shape, F32), pltpu.VMEM(interp_wt.shape, F32), pltpu.VMEM(interp_cols.shape, jnp.int32),
-               dma((3,))],
-            chunks=chunks, groups=crossing if kind else straight, own=own, halo=halo, crossing=kind)
-        each = len(outs) // len(chunks)
-        return [list(outs[k * each : (k + 1) * each]) for k in range(len(chunks))]
-
-    over = first(True, CROSSING * halo)
-    rest = first(False, ext - CROSSING * halo)
+    def operator(rows):
+        return [pltpu.VMEM((rows, grid_rows), BF16)] * 2
+
+    def apart(arrays):
+        each = len(arrays) // len(chunks)
+        return [list(arrays[k * each : (k + 1) * each]) for k in range(len(chunks))]
+
+    over = [shape(len(group) * halo, width) for _, width in chunks for group in crossing]
+    keep = [shape(grid_rows, width_all, BF16)] * 2 + [
+        jax.ShapeDtypeStruct(array.shape, array.dtype) for array in (interp_wt, interp_cols)]
+    high, low, near_wt, near_cols, *over = call(
+        first_kernel, keep + over, (valid, odd, far_ctrl, far_wt, far_cols), [SMEM, SMEM, HBM, HBM, HBM],
+        operator(CROSSING * halo) + [pltpu.VMEM(ctrl.shape, F32), dma((3,))],
+        chunks=chunks, groups=crossing, own=own, halo=halo)
+    rest = []
+    for _, width in chunks:
+        rest += [shape(own, width)] + [shape(len(group) * halo, width) for group in straight]
+    rest = call(rest_kernel, rest, (odd, high, low, near_wt, near_cols), [SMEM],
+                operator(ext - CROSSING * halo), chunks=chunks, groups=straight, own=own, halo=halo)
+    over, rest = apart(over), apart(rest)
     state = [[mine[0]] + sent + mine[1:] for sent, mine in zip(over, rest)]
-    ct_high, ct_low, ht = call(
-        early_kernel, [shape(ext, own, BF16)] * 2 + [shape(own, slots, BF16)],
+    ct_high, ct_low, ht, h = call(
+        early_kernel, [shape(ext, own, BF16)] * 2 + [shape(own, slots, BF16), shape(slots, own, BF16)],
         (odd, conv_wt, conv_cols, halo_index), [SMEM], halo=halo)
-    c_high, c_low, h = call(
-        conv_kernel, [shape(own, ext, BF16)] * 2 + [shape(slots, own, BF16)],
-        (odd, conv_wt, conv_cols, ht), [SMEM], halo=halo)
+    c_high, c_low = call(
+        late_kernel, [shape(own, ext, BF16)] * 2, (odd, conv_wt, conv_cols), [SMEM], own=own, halo=halo)
     i_high, i_low = call(
-        interp_kernel, [shape(grid_rows, ext, BF16)] * 2, (odd, interp_wt, interp_cols), [SMEM],
-        own=own, halo=halo)
+        late_kernel, [shape(grid_rows, ext, BF16)] * 2, (odd, interp_wt, interp_cols), [SMEM], own=own, halo=halo)
 
     def scratch(rows, width):
         return [pltpu.VMEM((rows, width), BF16)] * 2

time: 113 us -> 114 us (level)
  the two profiles are of different devices: /device:TPU:17 before, /device:TPU:9 now
where the time goes in v3:
time: 114 us
  starting transfers between devices  73 us (64%)
  Pallas kernels  25 us (22%)
  waiting for transfers between devices  14.5 us (13%)
  between operations  1.31 us (1%)
    ppermute x40, starting transfers between devices, exchange(): arrived.append(lax.ppermute(piece, ('ty', 'tx'), pairs))  73 us
    pallas_call x14, Pallas kernels, call(): pl.pallas_call(functools.partial(kernel, **more), out_shape=outs, in_spec...  25 us
    ppermute x40, waiting for transfers between devices, exchange(): arrived.append(lax.ppermute(piece, ('ty', 'tx'), pairs))  14.5 us
  transfers between devices with their start and end apart: 40, of which 6 were waited for; matrix products, arithmetic and copies ran while one was open for 0% of the time, Pallas kernels for 18%

profile of v3, /device:TPU:9, one launch (start us, length us, event | category | flops | bytes accessed | tf_op | source)
XLA Modules:
  0.0 113.9 jit_solution(15423133504455157831)
XLA Ops:
  0.7 3.2 %shard_map.73 = (bf16[512,640]{1,0:T(8,128)(2,1)S(1)}, bf16[512,640]{1,0:T(8,128)(2,1)S(1)}, f32[1,1,4,128,384]{4,3,2,1,0:T(8,128)S(1)}, s32[1,1,4,384]{3,2,1,0:...) custom-call(s32[1,1]{1,0:T(1,128)S(6)} %copy.10.valid, ...), custom_call_target="tpu_custom_call" | custom-call | flops 1073741824 | bytes 4194304 | tf_op jit(solution)/shard_map/pallas_call | solution.py:308
  3.9 1.3 %collective-permute-start = (f32[128,256]{1,0:T(8,128)S(1)}, f32[128,256]{1,0:T(8,128)S(1)}, u32[]{:S(2)}, u32[]{:S(2)}) collective-permute-start(f32[128,256]{1,0:T(8,128)S(1)} %get-tuple-element.70), channel_id=1, source_target_pairs={{0,1},{1,0},{2,3},{3,2},{4,5},{5,4},{6,7},{7,6},{8,9},{9,8},{10,11... | collective-permute-start | bytes 393224 | tf_op jit(solution)/shard_map/ppermute | solution.py:71
  5.1 2.5 %shard_map.74 = (f32[512,384]{1,0:T(8,128)S(1)}, f32[64,384]{1,0:T(8,128)S(1)}, f32[64,384]{1,0:T(8,128)S(1)}, f32[512,256]{1,0:T(8,128)S(1)}, f32[64,256]{1,0:T(8,128)S(1)}, /*index=5*/f32[64,256]{1,0:T(8,128)S(1)}) custom-call(s32[1,1]{1,0:T(1,128)} %bitcast.odd, bf16[512,640]{1,0:T(8,128)(2,1)S(1)} %get-tuple-element.65.high, ...), custom_call_target="tpu_custom_call" | custom-call | flops 1073741824 | bytes 4194304 | tf_op jit(solution)/shard_map/pallas_call | solution.py:308
  7.6 1.0 collective-permute-start.3
  8.6 3.0 %collective-permute-start.4 = (f32[64,256]{1,0:T(8,128)S(1)}, f32[64,256]{1,0:T(8,128)S(1)}, u32[]{:S(2)}, u32[]{:S(2)}) collective-permute-start(f32[64,256]{1,0:T(8,128)S(1)} %get-tuple-element.74), channel_id=1, source_target_pairs={{2,4},{3,5},{4,2},{5,3},{6,8},{7,9},{8,6},{9,7},{10,12},{11,13},{1... | collective-permute-start | bytes 196616 | tf_op jit(solution)/shard_map/ppermute | solution.py:71
  11.7 0.6 collective-permute-start.1
  12.3 4.1 %collective-permute-start.2 = (f32[128,256]{1,0:T(8,128)S(1)}, f32[128,256]{1,0:T(8,128)S(1)}, u32[]{:S(2)}, u32[]{:S(2)}) collective-permute-start(f32[128,256]{1,0:T(8,128)S(1)} %get-tuple-element.72), channel_id=1, source_target_pairs={{2,5},{3,4},{4,3},{5,2},{6,9},{7,8},{8,7},{9,6},{10,13},{11,12},{1... | collective-permute-start | bytes 393224 | tf_op jit(solution)/shard_map/ppermute | solution.py:71
  16.4 0.0 collective-permute-done.3.refs_3_
  16.4 0.3 collective-permute-start.20
  16.7 0.7 collective-permute-start.21
  17.4 0.0 collective-permute-done.refs_0_
  17.4 3.9 %collective-permute-start.22 = (f32[128,384]{1,0:T(8,128)S(1)}, f32[128,384]{1,0:T(8,128)S(1)}, u32[]{:S(2)}, u32[]{:S(2)}) collective-permute-start(f32[128,384]{1,0:T(8,128)S(1)} %get-tuple-element.104), channel_id=1, source_target_pairs={{2,5},{3,4},{4,3},{5,2},{6,9},{7,8},{8,7},{9,6},{10,13},{11,12},{1... | collective-permute-start | bytes 589832 | tf_op jit(solution)/shard_map/ppermute | solution.py:71
  21.3 1.7 %shard_map.75 = (bf16[1024,512]{1,0:T(8,128)(2,1)S(1)}, bf16[1024,512]{1,0:T(8,128)(2,1)S(1)}, bf16[512,512]{1,0:T(8,128)(2,1)S(1)}, bf16[512,512]{1,0:T(8,128)(2,1)S(1)}) custom-call(s32[1,1]{1,0:T(1,128)} %bitcast.odd, f32[1,1,4,128,512]{4,3,2,1,0:T(8,128)S(1)} %copy-done, s32[1,1,4,512]{3,2,1,0:T(4,128)S(1)} %copy-done.2, s32[1,1,8,64]{3,2,1,0:T(8,128)S(1)} %copy-done.4), custom_call_target="tpu_custom_call" | custom-call | flops 1073741824 | bytes 4194304 | tf_op jit(solution)/shard_map/pallas_call | solution.py:308
  23.0 0.0 collective-permute-done.1.refs_1_
  23.0 0.1 collective-permute-start.23
  23.1 3.5 %collective-permute-start.24 = (f32[64,384]{1,0:T(8,128)S(1)}, f32[64,384]{1,0:T(8,128)S(1)}, u32[]{:S(2)}, u32[]{:S(2)}) collective-permute-start(f32[64,384]{1,0:T(8,128)S(1)} %get-tuple-element.106), channel_id=1, source_target_pairs={{2,4},{3,5},{4,2},{5,3},{6,8},{7,9},{8,6},{9,7},{10,12},{11,13},{1... | collective-permute-start | bytes 294920 | tf_op jit(solution)/shard_map/ppermute | solution.py:71
  26.6 1.8 %shard_map.76 = (f32[512,256]{1,0:T(8,128)S(1)}, f32[128,256]{1,0:T(8,128)S(1)}, f32[128,256]{1,0:T(8,128)S(1)}, f32[128,256]{1,0:T(8,128)S(1)}, f32[64,256]{1,0:T(8,128)S(1)}, /*index=5*/f32[64,256]{1,0:T(8,128)S(1)}) custom-call(f32[512,256]{1,0:T(8,128)S(1)} %get-tuple-element.69.own_in, f32[128,256]{1,0:T(8,128)S(1)} %collective-permute-done.refs_0_, ...), custom_call_target="tpu_custom_call" | custom-call | flops 1073741824 | bytes 4194304 | tf_op jit(solution)/shard_map/pallas_call | solution.py:308
  28.5 1.3 %collective-permute-start.5 = (f32[128,256]{1,0:T(8,128)S(1)}, f32[128,256]{1,0:T(8,128)S(1)}, u32[]{:S(2)}, u32[]{:S(2)}) collective-permute-start(f32[128,256]{1,0:T(8,128)S(1)} %get-tuple-element.79), channel_id=1, source_target_pairs={{0,1},{1,0},{2,3},{3,2},{4,5},{5,4},{6,7},{7,6},{8,9},{9,8},{10,11... | collective-permute-start | bytes 393224 | tf_op jit(solution)/shard_map/ppermute | solution.py:71
  29.8 0.6 collective-permute-done.24.refs_4_
  30.4 1.2 %collective-permute-start.6 = (f32[128,256]{1,0:T(8,128)S(1)}, f32[128,256]{1,0:T(8,128)S(1)}, u32[]{:S(2)}, u32[]{:S(2)}) collective-permute-start(f32[128,256]{1,0:T(8,128)S(1)} %get-tuple-element.80), channel_id=1, source_target_pairs={{0,3},{1,2},{2,1},{3,0},{4,7},{5,6},{6,5},{7,4},{8,11},{9,10},{10,... | collective-permute-start | bytes 393224 | tf_op jit(solution)/shard_map/ppermute | solution.py:71
  31.7 2.9 %collective-permute-start.7 = (f32[128,256]{1,0:T(8,128)S(1)}, f32[128,256]{1,0:T(8,128)S(1)}, u32[]{:S(2)}, u32[]{:S(2)}) collective-permute-start(f32[128,256]{1,0:T(8,128)S(1)} %get-tuple-element.81), channel_id=1, source_target_pairs={{2,5},{3,4},{4,3},{5,2},{6,9},{7,8},{8,7},{9,6},{10,13},{11,12},{1... | collective-permute-start | bytes 393224 | tf_op jit(solution)/shard_map/ppermute | solution.py:71
  34.6 0.1 collective-permute-start.8
  34.7 0.3 collective-permute-done.22.refs_2_
  35.0 3.6 %collective-permute-start.9 = (f32[64,256]{1,0:T(8,128)S(1)}, f32[64,256]{1,0:T(8,128)S(1)}, u32[]{:S(2)}, u32[]{:S(2)}) collective-permute-start(f32[64,256]{1,0:T(8,128)S(1)} %get-tuple-element.83), channel_id=1, source_target_pairs={{2,4},{3,5},{4,2},{5,3},{6,8},{7,9},{8,6},{9,7},{10,12},{11,13},{1... | collective-permute-start | bytes 196616 | tf_op jit(solution)/shard_map/ppermute | solution.py:71
  38.6 2.2 %shard_map.82 = (f32[512,384]{1,0:T(8,128)S(1)}, f32[128,384]{1,0:T(8,128)S(1)}, f32[128,384]{1,0:T(8,128)S(1)}, f32[128,384]{1,0:T(8,128)S(1)}, f32[64,384]{1,0:T(8,128)S(1)}, /*index=5*/f32[64,384]{1,0:T(8,128)S(1)}) custom-call(f32[512,384]{1,0:T(8,128)S(1)} %get-tuple-element.101.own_in, f32[128,384]{1,0:T(8,128)S(1)} %collective-permute-done.20.refs_0_, ...), custom_call_target="tpu_custom_call" | custom-call | flops 1073741824 | bytes 4194304 | tf_op jit(solution)/shard_map/pallas_call | solution.py:308
  40.9 1.3 %collective-permute-start.25 = (f32[128,384]{1,0:T(8,128)S(1)}, f32[128,384]{1,0:T(8,128)S(1)}, u32[]{:S(2)}, u32[]{:S(2)}) collective-permute-start(f32[128,384]{1,0:T(8,128)S(1)} %get-tuple-element.108), channel_id=1, source_target_pairs={{0,1},{1,0},{2,3},{3,2},{4,5},{5,4},{6,7},{7,6},{8,9},{9,8},{10,11... | collective-permute-start | bytes 589832 | tf_op jit(solution)/shard_map/ppermute | solution.py:71
  42.1 0.6 collective-permute-done.9.refs_4_
  42.7 0.5 collective-permute-start.26
  43.3 4.0 %collective-permute-start.27 = (f32[128,384]{1,0:T(8,128)S(1)}, f32[128,384]{1,0:T(8,128)S(1)}, u32[]{:S(2)}, u32[]{:S(2)}) collective-permute-start(f32[128,384]{1,0:T(8,128)S(1)} %get-tuple-element.110), channel_id=1, source_target_pairs={{2,5},{3,4},{4,3},{5,2},{6,9},{7,8},{8,7},{9,6},{10,13},{11,12},{1... | collective-permute-start | bytes 589832 | tf_op jit(solution)/shard_map/ppermute | solution.py:71
  47.3 0.1 collective-permute-start.28
  47.4 3.5 %collective-permute-start.29 = (f32[64,384]{1,0:T(8,128)S(1)}, f32[64,384]{1,0:T(8,128)S(1)}, u32[]{:S(2)}, u32[]{:S(2)}) collective-permute-start(f32[64,384]{1,0:T(8,128)S(1)} %get-tuple-element.112), channel_id=1, source_target_pairs={{2,4},{3,5},{4,2},{5,3},{6,8},{7,9},{8,6},{9,7},{10,12},{11,13},{1... | collective-permute-start | bytes 294920 | tf_op jit(solution)/shard_map/ppermute | solution.py:71
  50.9 1.3 %shard_map.77 = (f32[512,256]{1,0:T(8,128)S(1)}, f32[128,256]{1,0:T(8,128)S(1)}, f32[128,256]{1,0:T(8,128)S(1)}, f32[128,256]{1,0:T(8,128)S(1)}, f32[64,256]{1,0:T(8,128)S(1)}, /*index=5*/f32[64,256]{1,0:T(8,128)S(1)}) custom-call(f32[512,256]{1,0:T(8,128)S(1)} %get-tuple-element.78.own_in, f32[128,256]{1,0:T(8,128)S(1)} %collective-permute-done.5.refs_0_, ...), custom_call_target="tpu_custom_call" | custom-call | flops 1073741824 | bytes 4194304 | tf_op jit(solution)/shard_map/pallas_call | solution.py:308
  52.1 1.3 %collective-permute-start.10 = (f32[128,256]{1,0:T(8,128)S(1)}, f32[128,256]{1,0:T(8,128)S(1)}, u32[]{:S(2)}, u32[]{:S(2)}) collective-permute-start(f32[128,256]{1,0:T(8,128)S(1)} %get-tuple-element.86), channel_id=1, source_target_pairs={{0,1},{1,0},{2,3},{3,2},{4,5},{5,4},{6,7},{7,6},{8,9},{9,8},{10,11... | collective-permute-start | bytes 393224 | tf_op jit(solution)/shard_map/ppermute | solution.py:71
  53.4 3.6 %collective-permute-done.29.refs_4_ = f32[64,384]{1,0:T(8,128)S(1)} collective-permute-done((f32[64,384]{1,0:T(8,128)S(1)}, f32[64,384]{1,0:T(8,128)S(1)}, u32[]{:S(2)}, u32[]{:S(2)}) %collective-permute-start.29) | collective-permute-done | bytes 98336 | tf_op jit(solution)/shard_map/ppermute | solution.py:71
  57.0 3.6 %collective-permute-start.12 = (f32[128,256]{1,0:T(8,128)S(1)}, f32[128,256]{1,0:T(8,128)S(1)}, u32[]{:S(2)}, u32[]{:S(2)}) collective-permute-start(f32[128,256]{1,0:T(8,128)S(1)} %get-tuple-element.88), channel_id=1, source_target_pairs={{2,5},{3,4},{4,3},{5,2},{6,9},{7,8},{8,7},{9,6},{10,13},{11,12},{1... | collective-permute-start | bytes 393224 | tf_op jit(solution)/shard_map/ppermute | solution.py:71
  60.6 0.8 collective-permute-start.13
  61.4 4.2 %collective-permute-start.14 = (f32[64,256]{1,0:T(8,128)S(1)}, f32[64,256]{1,0:T(8,128)S(1)}, u32[]{:S(2)}, u32[]{:S(2)}) collective-permute-start(f32[64,256]{1,0:T(8,128)S(1)} %get-tuple-element.90), channel_id=1, source_target_pairs={{2,4},{3,5},{4,2},{5,3},{6,8},{7,9},{8,6},{9,7},{10,12},{11,13},{1... | collective-permute-start | bytes 196616 | tf_op jit(solution)/shard_map/ppermute | solution.py:71
  65.7 1.4 %shard_map.83 = (f32[512,384]{1,0:T(8,128)S(1)}, f32[128,384]{1,0:T(8,128)S(1)}, f32[128,384]{1,0:T(8,128)S(1)}, f32[128,384]{1,0:T(8,128)S(1)}, f32[64,384]{1,0:T(8,128)S(1)}, /*index=5*/f32[64,384]{1,0:T(8,128)S(1)}) custom-call(f32[512,384]{1,0:T(8,128)S(1)} %get-tuple-element.107.own_in, f32[128,384]{1,0:T(8,128)S(1)} %collective-permute-done.25.refs_0_, ...), custom_call_target="tpu_custom_call" | custom-call | flops 1073741824 | bytes 4194304 | tf_op jit(solution)/shard_map/pallas_call | solution.py:308
  67.1 1.3 %collective-permute-start.30 = (f32[128,384]{1,0:T(8,128)S(1)}, f32[128,384]{1,0:T(8,128)S(1)}, u32[]{:S(2)}, u32[]{:S(2)}) collective-permute-start(f32[128,384]{1,0:T(8,128)S(1)} %get-tuple-element.114), channel_id=1, source_target_pairs={{0,1},{1,0},{2,3},{3,2},{4,5},{5,4},{6,7},{7,6},{8,9},{9,8},{10,11... | collective-permute-start | bytes 589832 | tf_op jit(solution)/shard_map/ppermute | solution.py:71
  68.4 1.1 collective-permute-start.31
  69.4 3.6 %collective-permute-start.32 = (f32[128,384]{1,0:T(8,128)S(1)}, f32[128,384]{1,0:T(8,128)S(1)}, u32[]{:S(2)}, u32[]{:S(2)}) collective-permute-start(f32[128,384]{1,0:T(8,128)S(1)} %get-tuple-element.116), channel_id=1, source_target_pairs={{2,5},{3,4},{4,3},{5,2},{6,9},{7,8},{8,7},{9,6},{10,13},{11,12},{1... | collective-permute-start | bytes 589832 | tf_op jit(solution)/shard_map/ppermute | solution.py:71
  73.1 1.4 %shard_map.78 = (bf16[512,1024]{1,0:T(8,128)(2,1)S(1)}, bf16[512,1024]{1,0:T(8,128)(2,1)S(1)}) custom-call(s32[1,1]{1,0:T(1,128)} %bitcast.odd, f32[1,1,4,128,512]{4,3,2,1,0:T(8,128)S(1)} %copy-done, s32[1,1,4,512]{3,2,1,0:T(4,128)S(1)} %copy-done.2), custom_call_target="tpu_custom_call" | custom-call | flops 1073741824 | bytes 4194304 | tf_op jit(solution)/shard_map/pallas_call | solution.py:308
  74.5 0.1 collective-permute-start.33
  74.6 4.1 %collective-permute-start.34 = (f32[64,384]{1,0:T(8,128)S(1)}, f32[64,384]{1,0:T(8,128)S(1)}, u32[]{:S(2)}, u32[]{:S(2)}) collective-permute-start(f32[64,384]{1,0:T(8,128)S(1)} %get-tuple-element.118), channel_id=1, source_target_pairs={{2,4},{3,5},{4,2},{5,3},{6,8},{7,9},{8,6},{9,7},{10,12},{11,13},{1... | collective-permute-start | bytes 294920 | tf_op jit(solution)/shard_map/ppermute | solution.py:71
  78.7 1.4 %shard_map.79 = (f32[512,256]{1,0:T(8,128)S(1)}, f32[128,256]{1,0:T(8,128)S(1)}, f32[128,256]{1,0:T(8,128)S(1)}, f32[128,256]{1,0:T(8,128)S(1)}, f32[64,256]{1,0:T(8,128)S(1)}, /*index=5*/f32[64,256]{1,0:T(8,128)S(1)}) custom-call(f32[512,256]{1,0:T(8,128)S(1)} %get-tuple-element.85.own_in, f32[128,256]{1,0:T(8,128)S(1)} %collective-permute-done.10.refs_0_, ...), custom_call_target="tpu_custom_call" | custom-call | flops 1073741824 | bytes 4194304 | tf_op jit(solution)/shard_map/pallas_call | solution.py:308
  80.1 0.2 collective-permute-start.15
  80.3 3.9 %collective-permute-done.34.refs_4_ = f32[64,384]{1,0:T(8,128)S(1)} collective-permute-done((f32[64,384]{1,0:T(8,128)S(1)}, f32[64,384]{1,0:T(8,128)S(1)}, u32[]{:S(2)}, u32[]{:S(2)}) %collective-permute-start.34) | collective-permute-done | bytes 98336 | tf_op jit(solution)/shard_map/ppermute | solution.py:71
  84.2 2.2 %collective-permute-start.16 = (f32[128,256]{1,0:T(8,128)S(1)}, f32[128,256]{1,0:T(8,128)S(1)}, u32[]{:S(2)}, u32[]{:S(2)}) collective-permute-start(f32[128,256]{1,0:T(8,128)S(1)} %get-tuple-element.95), channel_id=1, source_target_pairs={{2,5},{3,4},{4,3},{5,2},{6,9},{7,8},{8,7},{9,6},{10,13},{11,12},{1... | collective-permute-start | bytes 393224 | tf_op jit(solution)/shard_map/ppermute | solution.py:71
  86.4 0.1 collective-permute-start.17
  86.5 4.1 %collective-permute-start.18 = (f32[64,256]{1,0:T(8,128)S(1)}, f32[64,256]{1,0:T(8,128)S(1)}, u32[]{:S(2)}, u32[]{:S(2)}) collective-permute-start(f32[64,256]{1,0:T(8,128)S(1)} %get-tuple-element.97), channel_id=1, source_target_pairs={{2,4},{3,5},{4,2},{5,3},{6,8},{7,9},{8,6},{9,7},{10,12},{11,13},{1... | collective-permute-start | bytes 196616 | tf_op jit(solution)/shard_map/ppermute | solution.py:71
  90.6 0.0 copy-start.1
  90.6 0.0 copy-start.3
  90.6 2.2 %shard_map.84 = (f32[512,384]{1,0:T(8,128)S(1)}, f32[128,384]{1,0:T(8,128)S(1)}, f32[128,384]{1,0:T(8,128)S(1)}, f32[128,384]{1,0:T(8,128)S(1)}, f32[64,384]{1,0:T(8,128)S(1)}, /*index=5*/f32[64,384]{1,0:T(8,128)S(1)}) custom-call(f32[512,384]{1,0:T(8,128)S(1)} %get-tuple-element.113.own_in, f32[128,384]{1,0:T(8,128)S(1)} %collective-permute-done.30.refs_0_, ...), custom_call_target="tpu_custom_call" | custom-call | flops 1073741824 | bytes 4194304 | tf_op jit(solution)/shard_map/pallas_call | solution.py:308
  92.8 0.5 collective-permute-start.35
  93.3 1.2 %collective-permute-start.36 = (f32[128,384]{1,0:T(8,128)S(1)}, f32[128,384]{1,0:T(8,128)S(1)}, u32[]{:S(2)}, u32[]{:S(2)}) collective-permute-start(f32[128,384]{1,0:T(8,128)S(1)} %get-tuple-element.121), channel_id=1, source_target_pairs={{0,3},{1,2},{2,1},{3,0},{4,7},{5,6},{6,5},{7,4},{8,11},{9,10},{10,... | collective-permute-start | bytes 589832 | tf_op jit(solution)/shard_map/ppermute | solution.py:71
  94.5 3.9 %collective-permute-start.37 = (f32[128,384]{1,0:T(8,128)S(1)}, f32[128,384]{1,0:T(8,128)S(1)}, u32[]{:S(2)}, u32[]{:S(2)}) collective-permute-start(f32[128,384]{1,0:T(8,128)S(1)} %get-tuple-element.122), channel_id=1, source_target_pairs={{2,5},{3,4},{4,3},{5,2},{6,9},{7,8},{8,7},{9,6},{10,13},{11,12},{1... | collective-permute-start | bytes 589832 | tf_op jit(solution)/shard_map/ppermute | solution.py:71
  98.4 0.1 collective-permute-start.38
  98.5 1.4 %shard_map.80 = (bf16[512,1024]{1,0:T(8,128)(2,1)S(1)}, bf16[512,1024]{1,0:T(8,128)(2,1)S(1)}) custom-call(s32[1,1]{1,0:T(1,128)} %bitcast.odd, f32[1,1,4,128,384]{4,3,2,1,0:T(8,128)S(1)} %copy-done.1, s32[1,1,4,384]{3,2,1,0:T(4,128)S(1)} %copy-done.3), custom_call_target="tpu_custom_call" | custom-call | flops 1073741824 | bytes 4194304 | tf_op jit(solution)/shard_map/pallas_call | solution.py:308
  99.9 1.2 %collective-permute-start.19 = (f32[128,256]{1,0:T(8,128)S(1)}, f32[128,256]{1,0:T(8,128)S(1)}, u32[]{:S(2)}, u32[]{:S(2)}) collective-permute-start(f32[128,256]{1,0:T(8,128)S(1)} %get-tuple-element.100), channel_id=1, source_target_pairs={{0,1},{1,0},{2,3},{3,2},{4,5},{5,4},{6,7},{7,6},{8,9},{9,8},{10,11... | collective-permute-start | bytes 393224 | tf_op jit(solution)/shard_map/ppermute | solution.py:71
  101.1 2.7 %collective-permute-start.39 = (f32[64,384]{1,0:T(8,128)S(1)}, f32[64,384]{1,0:T(8,128)S(1)}, u32[]{:S(2)}, u32[]{:S(2)}) collective-permute-start(f32[64,384]{1,0:T(8,128)S(1)} %get-tuple-element.124), channel_id=1, source_target_pairs={{2,4},{3,5},{4,2},{5,3},{6,8},{7,9},{8,6},{9,7},{10,12},{11,13},{1... | collective-permute-start | bytes 294920 | tf_op jit(solution)/shard_map/ppermute | solution.py:71
  103.8 1.0 shard_map.81.part
  104.8 5.4 %collective-permute-done.39.refs_4_ = f32[64,384]{1,0:T(8,128)S(1)} collective-permute-done((f32[64,384]{1,0:T(8,128)S(1)}, f32[64,384]{1,0:T(8,128)S(1)}, u32[]{:S(2)}, u32[]{:S(2)}) %collective-permute-start.39) | collective-permute-done | bytes 98336 | tf_op jit(solution)/shard_map/ppermute | solution.py:71
  110.2 2.3 %shard_map.85.so_far = f32[1,1,512,640]{3,2,1,0:T(8,128)} custom-call(s32[1,1]{1,0:T(1,128)S(6)} %copy.10.valid, f32[512,384]{1,0:T(8,128)S(1)} %get-tuple-element.119.own_in, f32[128,384]{1,0:T(8,128)S(1)} %collective-permute-done.35.refs_0_, f32[128,384]{1,0:T(8,128)S(1)} %collective-permute-done.36.refs_1_, ...), custom_call_target="tpu_custom_call" | custom-call | flops 1073741824 | bytes 4194304 | tf_op jit(solution)/shard_map/pallas_call | solution.py:308
  112.5 1.2 %shard_map.86 = f32[1,1,512,640]{3,2,1,0:T(8,128)} custom-call(s32[1,1]{1,0:T(1,128)S(6)} %copy.10.valid, f32[512,256]{1,0:T(8,128)S(1)} %shard_map.81.part, f32[128,256]{1,0:T(8,128)S(1)} %collective-permute-done.19.late, bf16[512,1024]{1,0:T(8,128)(2,1)S(1)} %get-tuple-element.98.refs_4_.refs_5_.m_high, ...), custom_call_target="tpu_custom_call", output_to_operand_aliasing={{}: (5, {})} | custom-call | flops 1073741824 | bytes 4194304 | tf_op jit(solution)/shard_map/pallas_call | solution.py:308
  (40 shorter events, 0.1 us)
Async XLA Ops:
  3.9 13.6 %collective-permute-start = (f32[128,256]{1,0:T(8,128)S(1)}, f32[128,256]{1,0:T(8,128)S(1)}, u32[]{:S(2)}, u32[]{:S(2)}) collective-permute-start(f32[128,256]{1,0:T(8,128)S(1)} %get-tuple-element.70), channel_id=1, source_target_pairs={{0,1},{1,0},{2,3},{3,2},{4,5},{5,4},{6,7},{7,6},{8,9},{9,8},{10,11... | collective-permute-start | bytes 393224 | tf_op jit(solution)/shard_map/ppermute | solution.py:71
  5.1 16.2 %copy-start = (f32[1,1,4,128,512]{4,3,2,1,0:T(8,128)S(1)}, f32[1,1,4,128,512]{4,3,2,1,0:T(8,128)}, u32[]{:S(2)}) copy-start(f32[1,1,4,128,512]{4,3,2,1,0:T(8,128)} %wt.6) | copy-start | bytes 3145732
  5.1 16.2 %copy-start.2 = (s32[1,1,4,512]{3,2,1,0:T(4,128)S(1)}, s32[1,1,4,512]{3,2,1,0:T(4,128)}, u32[]{:S(2)}) copy-start(s32[1,1,4,512]{3,2,1,0:T(4,128)} %cols.6) | copy-start | bytes 24580
  5.1 16.2 %copy-start.4 = (s32[1,1,8,64]{3,2,1,0:T(8,128)S(1)}, s32[1,1,8,64]{3,2,1,0:T(8,128)}, u32[]{:S(2)}) copy-start(s32[1,1,8,64]{3,2,1,0:T(8,128)} %index.1) | copy-start | bytes 6148
  7.6 8.8 %collective-permute-start.3 = (f32[64,256]{1,0:T(8,128)S(1)}, f32[64,256]{1,0:T(8,128)S(1)}, u32[]{:S(2)}, u32[]{:S(2)}) collective-permute-start(f32[64,256]{1,0:T(8,128)S(1)} %get-tuple-element.73), channel_id=1, source_target_pairs={{0,2},{1,3},{2,0},{3,1},{4,6},{5,7},{6,4},{7,5},{8,10},{9,11},{10,... | collective-permute-start | bytes 196616 | tf_op jit(solution)/shard_map/ppermute | solution.py:71
  8.6 8.1 %collective-permute-start.4 = (f32[64,256]{1,0:T(8,128)S(1)}, f32[64,256]{1,0:T(8,128)S(1)}, u32[]{:S(2)}, u32[]{:S(2)}) collective-permute-start(f32[64,256]{1,0:T(8,128)S(1)} %get-tuple-element.74), channel_id=1, source_target_pairs={{2,4},{3,5},{4,2},{5,3},{6,8},{7,9},{8,6},{9,7},{10,12},{11,13},{1... | collective-permute-start | bytes 196616 | tf_op jit(solution)/shard_map/ppermute | solution.py:71
  11.7 11.3 %collective-permute-start.1 = (f32[128,256]{1,0:T(8,128)S(1)}, f32[128,256]{1,0:T(8,128)S(1)}, u32[]{:S(2)}, u32[]{:S(2)}) collective-permute-start(f32[128,256]{1,0:T(8,128)S(1)} %get-tuple-element.71), channel_id=1, source_target_pairs={{0,3},{1,2},{2,1},{3,0},{4,7},{5,6},{6,5},{7,4},{8,11},{9,10},{10,... | collective-permute-start | bytes 393224 | tf_op jit(solution)/shard_map/ppermute | solution.py:71
  12.3 10.8 %collective-permute-start.2 = (f32[128,256]{1,0:T(8,128)S(1)}, f32[128,256]{1,0:T(8,128)S(1)}, u32[]{:S(2)}, u32[]{:S(2)}) collective-permute-start(f32[128,256]{1,0:T(8,128)S(1)} %get-tuple-element.72), channel_id=1, source_target_pairs={{2,5},{3,4},{4,3},{5,2},{6,9},{7,8},{8,7},{9,6},{10,13},{11,12},{1... | collective-permute-start | bytes 393224 | tf_op jit(solution)/shard_map/ppermute | solution.py:71
  16.4 15.3 %collective-permute-start.20 = (f32[128,384]{1,0:T(8,128)S(1)}, f32[128,384]{1,0:T(8,128)S(1)}, u32[]{:S(2)}, u32[]{:S(2)}) collective-permute-start(f32[128,384]{1,0:T(8,128)S(1)} %get-tuple-element.102), channel_id=1, source_target_pairs={{0,1},{1,0},{2,3},{3,2},{4,5},{5,4},{6,7},{7,6},{8,9},{9,8},{10,11... | collective-permute-start | bytes 589832 | tf_op jit(solution)/shard_map/ppermute | solution.py:71
  16.7 17.9 %collective-permute-start.21 = (f32[128,384]{1,0:T(8,128)S(1)}, f32[128,384]{1,0:T(8,128)S(1)}, u32[]{:S(2)}, u32[]{:S(2)}) collective-permute-start(f32[128,384]{1,0:T(8,128)S(1)} %get-tuple-element.103), channel_id=1, source_target_pairs={{0,3},{1,2},{2,1},{3,0},{4,7},{5,6},{6,5},{7,4},{8,11},{9,10},{10,... | collective-permute-start | bytes 589832 | tf_op jit(solution)/shard_map/ppermute | solution.py:71
  17.4 17.6 %collective-permute-start.22 = (f32[128,384]{1,0:T(8,128)S(1)}, f32[128,384]{1,0:T(8,128)S(1)}, u32[]{:S(2)}, u32[]{:S(2)}) collective-permute-start(f32[128,384]{1,0:T(8,128)S(1)} %get-tuple-element.104), channel_id=1, source_target_pairs={{2,5},{3,4},{4,3},{5,2},{6,9},{7,8},{8,7},{9,6},{10,13},{11,12},{1... | collective-permute-start | bytes 589832 | tf_op jit(solution)/shard_map/ppermute | solution.py:71
  23.0 5.5 %collective-permute-start.23 = (f32[64,384]{1,0:T(8,128)S(1)}, f32[64,384]{1,0:T(8,128)S(1)}, u32[]{:S(2)}, u32[]{:S(2)}) collective-permute-start(f32[64,384]{1,0:T(8,128)S(1)} %get-tuple-element.105), channel_id=1, source_target_pairs={{0,2},{1,3},{2,0},{3,1},{4,6},{5,7},{6,4},{7,5},{8,10},{9,11},{10,... | collective-permute-start | bytes 294920 | tf_op jit(solution)/shard_map/ppermute | solution.py:71
  23.1 7.3 %collective-permute-start.24 = (f32[64,384]{1,0:T(8,128)S(1)}, f32[64,384]{1,0:T(8,128)S(1)}, u32[]{:S(2)}, u32[]{:S(2)}) collective-permute-start(f32[64,384]{1,0:T(8,128)S(1)} %get-tuple-element.106), channel_id=1, source_target_pairs={{2,4},{3,5},{4,2},{5,3},{6,8},{7,9},{8,6},{9,7},{10,12},{11,13},{1... | collective-permute-start | bytes 294920 | tf_op jit(solution)/shard_map/ppermute | solution.py:71
  28.5 14.8 %collective-permute-start.5 = (f32[128,256]{1,0:T(8,128)S(1)}, f32[128,256]{1,0:T(8,128)S(1)}, u32[]{:S(2)}, u32[]{:S(2)}) collective-permute-start(f32[128,256]{1,0:T(8,128)S(1)} %get-tuple-element.79), channel_id=1, source_target_pairs={{0,1},{1,0},{2,3},{3,2},{4,5},{5,4},{6,7},{7,6},{8,9},{9,8},{10,11... | collective-permute-start | bytes 393224 | tf_op jit(solution)/shard_map/ppermute | solution.py:71
  30.4 16.8 %collective-permute-start.6 = (f32[128,256]{1,0:T(8,128)S(1)}, f32[128,256]{1,0:T(8,128)S(1)}, u32[]{:S(2)}, u32[]{:S(2)}) collective-permute-start(f32[128,256]{1,0:T(8,128)S(1)} %get-tuple-element.80), channel_id=1, source_target_pairs={{0,3},{1,2},{2,1},{3,0},{4,7},{5,6},{6,5},{7,4},{8,11},{9,10},{10,... | collective-permute-start | bytes 393224 | tf_op jit(solution)/shard_map/ppermute | solution.py:71
  31.7 15.7 %collective-permute-start.7 = (f32[128,256]{1,0:T(8,128)S(1)}, f32[128,256]{1,0:T(8,128)S(1)}, u32[]{:S(2)}, u32[]{:S(2)}) collective-permute-start(f32[128,256]{1,0:T(8,128)S(1)} %get-tuple-element.81), channel_id=1, source_target_pairs={{2,5},{3,4},{4,3},{5,2},{6,9},{7,8},{8,7},{9,6},{10,13},{11,12},{1... | collective-permute-start | bytes 393224 | tf_op jit(solution)/shard_map/ppermute | solution.py:71
  34.6 6.3 %collective-permute-start.8 = (f32[64,256]{1,0:T(8,128)S(1)}, f32[64,256]{1,0:T(8,128)S(1)}, u32[]{:S(2)}, u32[]{:S(2)}) collective-permute-start(f32[64,256]{1,0:T(8,128)S(1)} %get-tuple-element.82), channel_id=1, source_target_pairs={{0,2},{1,3},{2,0},{3,1},{4,6},{5,7},{6,4},{7,5},{8,10},{9,11},{10,... | collective-permute-start | bytes 196616 | tf_op jit(solution)/shard_map/ppermute | solution.py:71
  35.0 7.7 %collective-permute-start.9 = (f32[64,256]{1,0:T(8,128)S(1)}, f32[64,256]{1,0:T(8,128)S(1)}, u32[]{:S(2)}, u32[]{:S(2)}) collective-permute-start(f32[64,256]{1,0:T(8,128)S(1)} %get-tuple-element.83), channel_id=1, source_target_pairs={{2,4},{3,5},{4,2},{5,3},{6,8},{7,9},{8,6},{9,7},{10,12},{11,13},{1... | collective-permute-start | bytes 196616 | tf_op jit(solution)/shard_map/ppermute | solution.py:71
  40.9 16.2 %collective-permute-start.25 = (f32[128,384]{1,0:T(8,128)S(1)}, f32[128,384]{1,0:T(8,128)S(1)}, u32[]{:S(2)}, u32[]{:S(2)}) collective-permute-start(f32[128,384]{1,0:T(8,128)S(1)} %get-tuple-element.108), channel_id=1, source_target_pairs={{0,1},{1,0},{2,3},{3,2},{4,5},{5,4},{6,7},{7,6},{8,9},{9,8},{10,11... | collective-permute-start | bytes 589832 | tf_op jit(solution)/shard_map/ppermute | solution.py:71
  42.7 17.9 %collective-permute-start.26 = (f32[128,384]{1,0:T(8,128)S(1)}, f32[128,384]{1,0:T(8,128)S(1)}, u32[]{:S(2)}, u32[]{:S(2)}) collective-permute-start(f32[128,384]{1,0:T(8,128)S(1)} %get-tuple-element.109), channel_id=1, source_target_pairs={{0,3},{1,2},{2,1},{3,0},{4,7},{5,6},{6,5},{7,4},{8,11},{9,10},{10,... | collective-permute-start | bytes 589832 | tf_op jit(solution)/shard_map/ppermute | solution.py:71
  43.3 18.2 %collective-permute-start.27 = (f32[128,384]{1,0:T(8,128)S(1)}, f32[128,384]{1,0:T(8,128)S(1)}, u32[]{:S(2)}, u32[]{:S(2)}) collective-permute-start(f32[128,384]{1,0:T(8,128)S(1)} %get-tuple-element.110), channel_id=1, source_target_pairs={{2,5},{3,4},{4,3},{5,2},{6,9},{7,8},{8,7},{9,6},{10,13},{11,12},{1... | collective-permute-start | bytes 589832 | tf_op jit(solution)/shard_map/ppermute | solution.py:71
  47.3 4.9 %collective-permute-start.28 = (f32[64,384]{1,0:T(8,128)S(1)}, f32[64,384]{1,0:T(8,128)S(1)}, u32[]{:S(2)}, u32[]{:S(2)}) collective-permute-start(f32[64,384]{1,0:T(8,128)S(1)} %get-tuple-element.111), channel_id=1, source_target_pairs={{0,2},{1,3},{2,0},{3,1},{4,6},{5,7},{6,4},{7,5},{8,10},{9,11},{10,... | collective-permute-start | bytes 294920 | tf_op jit(solution)/shard_map/ppermute | solution.py:71
  47.4 9.7 %collective-permute-start.29 = (f32[64,384]{1,0:T(8,128)S(1)}, f32[64,384]{1,0:T(8,128)S(1)}, u32[]{:S(2)}, u32[]{:S(2)}) collective-permute-start(f32[64,384]{1,0:T(8,128)S(1)} %get-tuple-element.112), channel_id=1, source_target_pairs={{2,4},{3,5},{4,2},{5,3},{6,8},{7,9},{8,6},{9,7},{10,12},{11,13},{1... | collective-permute-start | bytes 294920 | tf_op jit(solution)/shard_map/ppermute | solution.py:71
  52.1 17.3 %collective-permute-start.10 = (f32[128,256]{1,0:T(8,128)S(1)}, f32[128,256]{1,0:T(8,128)S(1)}, u32[]{:S(2)}, u32[]{:S(2)}) collective-permute-start(f32[128,256]{1,0:T(8,128)S(1)} %get-tuple-element.86), channel_id=1, source_target_pairs={{0,1},{1,0},{2,3},{3,2},{4,5},{5,4},{6,7},{7,6},{8,9},{9,8},{10,11... | collective-permute-start | bytes 393224 | tf_op jit(solution)/shard_map/ppermute | solution.py:71
  57.0 17.5 %collective-permute-start.11 = (f32[128,256]{1,0:T(8,128)S(1)}, f32[128,256]{1,0:T(8,128)S(1)}, u32[]{:S(2)}, u32[]{:S(2)}) collective-permute-start(f32[128,256]{1,0:T(8,128)S(1)} %get-tuple-element.87), channel_id=1, source_target_pairs={{0,3},{1,2},{2,1},{3,0},{4,7},{5,6},{6,5},{7,4},{8,11},{9,10},{10,... | collective-permute-start | bytes 393224 | tf_op jit(solution)/shard_map/ppermute | solution.py:71
  57.0 17.6 %collective-permute-start.12 = (f32[128,256]{1,0:T(8,128)S(1)}, f32[128,256]{1,0:T(8,128)S(1)}, u32[]{:S(2)}, u32[]{:S(2)}) collective-permute-start(f32[128,256]{1,0:T(8,128)S(1)} %get-tuple-element.88), channel_id=1, source_target_pairs={{2,5},{3,4},{4,3},{5,2},{6,9},{7,8},{8,7},{9,6},{10,13},{11,12},{1... | collective-permute-start | bytes 393224 | tf_op jit(solution)/shard_map/ppermute | solution.py:71
  60.6 6.4 %collective-permute-start.13 = (f32[64,256]{1,0:T(8,128)S(1)}, f32[64,256]{1,0:T(8,128)S(1)}, u32[]{:S(2)}, u32[]{:S(2)}) collective-permute-start(f32[64,256]{1,0:T(8,128)S(1)} %get-tuple-element.89), channel_id=1, source_target_pairs={{0,2},{1,3},{2,0},{3,1},{4,6},{5,7},{6,4},{7,5},{8,10},{9,11},{10,... | collective-permute-start | bytes 196616 | tf_op jit(solution)/shard_map/ppermute | solution.py:71
  61.4 6.9 %collective-permute-start.14 = (f32[64,256]{1,0:T(8,128)S(1)}, f32[64,256]{1,0:T(8,128)S(1)}, u32[]{:S(2)}, u32[]{:S(2)}) collective-permute-start(f32[64,256]{1,0:T(8,128)S(1)} %get-tuple-element.90), channel_id=1, source_target_pairs={{2,4},{3,5},{4,2},{5,3},{6,8},{7,9},{8,6},{9,7},{10,12},{11,13},{1... | collective-permute-start | bytes 196616 | tf_op jit(solution)/shard_map/ppermute | solution.py:71
  67.1 19.3 %collective-permute-start.30 = (f32[128,384]{1,0:T(8,128)S(1)}, f32[128,384]{1,0:T(8,128)S(1)}, u32[]{:S(2)}, u32[]{:S(2)}) collective-permute-start(f32[128,384]{1,0:T(8,128)S(1)} %get-tuple-element.114), channel_id=1, source_target_pairs={{0,1},{1,0},{2,3},{3,2},{4,5},{5,4},{6,7},{7,6},{8,9},{9,8},{10,11... | collective-permute-start | bytes 589832 | tf_op jit(solution)/shard_map/ppermute | solution.py:71
  68.4 18.1 %collective-permute-start.31 = (f32[128,384]{1,0:T(8,128)S(1)}, f32[128,384]{1,0:T(8,128)S(1)}, u32[]{:S(2)}, u32[]{:S(2)}) collective-permute-start(f32[128,384]{1,0:T(8,128)S(1)} %get-tuple-element.115), channel_id=1, source_target_pairs={{0,3},{1,2},{2,1},{3,0},{4,7},{5,6},{6,5},{7,4},{8,11},{9,10},{10,... | collective-permute-start | bytes 589832 | tf_op jit(solution)/shard_map/ppermute | solution.py:71
  69.4 21.2 %collective-permute-start.32 = (f32[128,384]{1,0:T(8,128)S(1)}, f32[128,384]{1,0:T(8,128)S(1)}, u32[]{:S(2)}, u32[]{:S(2)}) collective-permute-start(f32[128,384]{1,0:T(8,128)S(1)} %get-tuple-element.116), channel_id=1, source_target_pairs={{2,5},{3,4},{4,3},{5,2},{6,9},{7,8},{8,7},{9,6},{10,13},{11,12},{1... | collective-permute-start | bytes 589832 | tf_op jit(solution)/shard_map/ppermute | solution.py:71
  74.5 5.6 %collective-permute-start.33 = (f32[64,384]{1,0:T(8,128)S(1)}, f32[64,384]{1,0:T(8,128)S(1)}, u32[]{:S(2)}, u32[]{:S(2)}) collective-permute-start(f32[64,384]{1,0:T(8,128)S(1)} %get-tuple-element.117), channel_id=1, source_target_pairs={{0,2},{1,3},{2,0},{3,1},{4,6},{5,7},{6,4},{7,5},{8,10},{9,11},{10,... | collective-permute-start | bytes 294920 | tf_op jit(solution)/shard_map/ppermute | solution.py:71
  74.6 9.6 %collective-permute-start.34 = (f32[64,384]{1,0:T(8,128)S(1)}, f32[64,384]{1,0:T(8,128)S(1)}, u32[]{:S(2)}, u32[]{:S(2)}) collective-permute-start(f32[64,384]{1,0:T(8,128)S(1)} %get-tuple-element.118), channel_id=1, source_target_pairs={{2,4},{3,5},{4,2},{5,3},{6,8},{7,9},{8,6},{9,7},{10,12},{11,13},{1... | collective-permute-start | bytes 294920 | tf_op jit(solution)/shard_map/ppermute | solution.py:71
  80.1 18.2 %collective-permute-start.15 = (f32[128,256]{1,0:T(8,128)S(1)}, f32[128,256]{1,0:T(8,128)S(1)}, u32[]{:S(2)}, u32[]{:S(2)}) collective-permute-start(f32[128,256]{1,0:T(8,128)S(1)} %get-tuple-element.94), channel_id=1, source_target_pairs={{0,3},{1,2},{2,1},{3,0},{4,7},{5,6},{6,5},{7,4},{8,11},{9,10},{10,... | collective-permute-start | bytes 393224 | tf_op jit(solution)/shard_map/ppermute | solution.py:71
  84.2 15.7 %collective-permute-start.16 = (f32[128,256]{1,0:T(8,128)S(1)}, f32[128,256]{1,0:T(8,128)S(1)}, u32[]{:S(2)}, u32[]{:S(2)}) collective-permute-start(f32[128,256]{1,0:T(8,128)S(1)} %get-tuple-element.95), channel_id=1, source_target_pairs={{2,5},{3,4},{4,3},{5,2},{6,9},{7,8},{8,7},{9,6},{10,13},{11,12},{1... | collective-permute-start | bytes 393224 | tf_op jit(solution)/shard_map/ppermute | solution.py:71
  86.4 6.9 %collective-permute-start.17 = (f32[64,256]{1,0:T(8,128)S(1)}, f32[64,256]{1,0:T(8,128)S(1)}, u32[]{:S(2)}, u32[]{:S(2)}) collective-permute-start(f32[64,256]{1,0:T(8,128)S(1)} %get-tuple-element.96), channel_id=1, source_target_pairs={{0,2},{1,3},{2,0},{3,1},{4,6},{5,7},{6,4},{7,5},{8,10},{9,11},{10,... | collective-permute-start | bytes 196616 | tf_op jit(solution)/shard_map/ppermute | solution.py:71
  86.5 8.0 %collective-permute-start.18 = (f32[64,256]{1,0:T(8,128)S(1)}, f32[64,256]{1,0:T(8,128)S(1)}, u32[]{:S(2)}, u32[]{:S(2)}) collective-permute-start(f32[64,256]{1,0:T(8,128)S(1)} %get-tuple-element.97), channel_id=1, source_target_pairs={{2,4},{3,5},{4,2},{5,3},{6,8},{7,9},{8,6},{9,7},{10,12},{11,13},{1... | collective-permute-start | bytes 196616 | tf_op jit(solution)/shard_map/ppermute | solution.py:71
  90.6 7.8 %copy-start.1 = (f32[1,1,4,128,384]{4,3,2,1,0:T(8,128)S(1)}, f32[1,1,4,128,384]{4,3,2,1,0:T(8,128)}, u32[]{:S(2)}) copy-start(f32[1,1,4,128,384]{4,3,2,1,0:T(8,128)} %wt.7) | copy-start | bytes 2359300
  90.6 7.8 %copy-start.3 = (s32[1,1,4,384]{3,2,1,0:T(4,128)S(1)}, s32[1,1,4,384]{3,2,1,0:T(4,128)}, u32[]{:S(2)}) copy-start(s32[1,1,4,384]{3,2,1,0:T(4,128)} %cols.7) | copy-start | bytes 18436
  92.8 17.3 %collective-permute-start.35 = (f32[128,384]{1,0:T(8,128)S(1)}, f32[128,384]{1,0:T(8,128)S(1)}, u32[]{:S(2)}, u32[]{:S(2)}) collective-permute-start(f32[128,384]{1,0:T(8,128)S(1)} %get-tuple-element.120), channel_id=1, source_target_pairs={{0,1},{1,0},{2,3},{3,2},{4,5},{5,4},{6,7},{7,6},{8,9},{9,8},{10,11... | collective-permute-start | bytes 589832 | tf_op jit(solution)/shard_map/ppermute | solution.py:71
  93.3 16.8 %collective-permute-start.36 = (f32[128,384]{1,0:T(8,128)S(1)}, f32[128,384]{1,0:T(8,128)S(1)}, u32[]{:S(2)}, u32[]{:S(2)}) collective-permute-start(f32[128,384]{1,0:T(8,128)S(1)} %get-tuple-element.121), channel_id=1, source_target_pairs={{0,3},{1,2},{2,1},{3,0},{4,7},{5,6},{6,5},{7,4},{8,11},{9,10},{10,... | collective-permute-start | bytes 589832 | tf_op jit(solution)/shard_map/ppermute | solution.py:71
  94.5 15.7 %collective-permute-start.37 = (f32[128,384]{1,0:T(8,128)S(1)}, f32[128,384]{1,0:T(8,128)S(1)}, u32[]{:S(2)}, u32[]{:S(2)}) collective-permute-start(f32[128,384]{1,0:T(8,128)S(1)} %get-tuple-element.122), channel_id=1, source_target_pairs={{2,5},{3,4},{4,3},{5,2},{6,9},{7,8},{8,7},{9,6},{10,13},{11,12},{1... | collective-permute-start | bytes 589832 | tf_op jit(solution)/shard_map/ppermute | solution.py:71
  98.4 2.7 %collective-permute-start.38 = (f32[64,384]{1,0:T(8,128)S(1)}, f32[64,384]{1,0:T(8,128)S(1)}, u32[]{:S(2)}, u32[]{:S(2)}) collective-permute-start(f32[64,384]{1,0:T(8,128)S(1)} %get-tuple-element.123), channel_id=1, source_target_pairs={{0,2},{1,3},{2,0},{3,1},{4,6},{5,7},{6,4},{7,5},{8,10},{9,11},{10,... | collective-permute-start | bytes 294920 | tf_op jit(solution)/shard_map/ppermute | solution.py:71
  99.9 12.7 %collective-permute-start.19 = (f32[128,256]{1,0:T(8,128)S(1)}, f32[128,256]{1,0:T(8,128)S(1)}, u32[]{:S(2)}, u32[]{:S(2)}) collective-permute-start(f32[128,256]{1,0:T(8,128)S(1)} %get-tuple-element.100), channel_id=1, source_target_pairs={{0,1},{1,0},{2,3},{3,2},{4,5},{5,4},{6,7},{7,6},{8,9},{9,8},{10,11... | collective-permute-start | bytes 393224 | tf_op jit(solution)/shard_map/ppermute | solution.py:71
  101.1 9.1 %collective-permute-start.39 = (f32[64,384]{1,0:T(8,128)S(1)}, f32[64,384]{1,0:T(8,128)S(1)}, u32[]{:S(2)}, u32[]{:S(2)}) collective-permute-start(f32[64,384]{1,0:T(8,128)S(1)} %get-tuple-element.124), channel_id=1, source_target_pairs={{2,4},{3,5},{4,2},{5,3},{6,8},{7,9},{8,6},{9,7},{10,12},{11,13},{1... | collective-permute-start | bytes 294920 | tf_op jit(solution)/shard_map/ppermute | solution.py:71
